TPU v7x, 32 devices: a whole 2x2x4 slice. The times are simulated.
32 devices in a mesh: gx: 4 (over x, core), gy: 4 (over z), gz: 2 (over y).
Axes of the slice: x: 2, y: 2, z: 4, core: 2. Of those that a mesh axis runs over, the one named last changes fastest.
Arguments:
- traces: bfloat16 [2, 4, 4, 2, 512, 768], P(None, 'gx', 'gy', 'gz'), may hold values from -6 to 6
- sources: bfloat16 [2, 4, 4, 2, 512, 768], P(None, 'gx', 'gy', 'gz'), may hold values from -4 to 4
- local_ops: bfloat16 [2, 4, 4, 2, 768, 768], P(None, 'gx', 'gy', 'gz'), may hold values from -0.15625 to 0.15625
- plane_coupling: bfloat16 [4, 8, 8], P('gx'), may hold values from -1 to 1
- face_owner: int32 [4, 8], P('gx'), may hold values from 0 to 7, each once within a row
Outputs:
- new_traces: bfloat16 [2, 4, 4, 2, 512, 768], P(None, 'gx', 'gy', 'gz')
Inputs may be any that keep to these rules, and one draw needn't show every extreme that they name: `face_owner`: each row is a permutation of the 8 plane positions.
All inputs are finite; a program needn't handle non-finite values.
Results may differ from a plain program's by a relative error of at most 0.0062.
Values may be sent and summed in bfloat16 or wider, within the bound.
No kernel may reach another device: no remote copies, remote signals or barrier semaphores. Data moves between devices by JAX's collectives and lax.ppermute only.
A program may use at most 64 MiB of HBM per device.

v0:
```python
import jax
import jax.numpy as jnp
from jax import lax
from jax.sharding import PartitionSpec as P

SWEEPS = 2


def with_halo(block, sides, width):
    for axis, dim in sides:
        count = lax.axis_size(axis)
        forward = [(i, i + 1) for i in range(count - 1)]
        forward.append((count - 1, 0))
        backward = [(target, source) for source, target in forward]
        low = lax.ppermute(
            lax.slice_in_dim(block, block.shape[dim] - width, None, axis=dim), axis, forward
        )
        high = lax.ppermute(lax.slice_in_dim(block, 0, width, axis=dim), axis, backward)
        block = jnp.concatenate([low, block, high], axis=dim)
    return block


def on_device(traces, sources, local_ops, plane_coupling, face_owner):
    columns_all = local_ops.shape[-1]
    slab_width = columns_all // 6
    slab_rows = traces.shape[4]
    count_y = lax.axis_size("gy")
    count_z = lax.axis_size("gz")
    plane_size = count_y * count_z
    block_rows_count = slab_rows // plane_size
    operators = local_ops.reshape(2, columns_all, columns_all)
    source_rows = sources.reshape(2, slab_rows, columns_all).astype(jnp.float32)
    incoming = traces.reshape(2, slab_rows, columns_all)
    owners = face_owner.reshape(plane_size)
    select = (owners[:, None] == jnp.arange(plane_size, dtype=jnp.int32)[None, :]).astype(
        jnp.float32
    )
    mixing = jnp.dot(
        plane_coupling.reshape(plane_size, plane_size).astype(jnp.float32),
        select,
        precision=lax.Precision.HIGHEST,
    ).astype(jnp.bfloat16)
    for sweep_step in range(SWEEPS):
        real_part = (
            jnp.dot(incoming[0], operators[0], preferred_element_type=jnp.float32)
            - jnp.dot(incoming[1], operators[1], preferred_element_type=jnp.float32)
            + source_rows[0]
        )
        imag_part = (
            jnp.dot(incoming[0], operators[1], preferred_element_type=jnp.float32)
            + jnp.dot(incoming[1], operators[0], preferred_element_type=jnp.float32)
            + source_rows[1]
        )
        outgoing = (
            jnp.stack([real_part, imag_part])
            .astype(jnp.bfloat16)
            .reshape(2, slab_rows, 6, slab_width)
        )
        along_x = with_halo(outgoing[:, :, 0:2, :], (("gx", 2),), 1)
        partial_faces = jnp.concatenate(
            [along_x[:, :, 0:1], along_x[:, :, 3:4], outgoing[:, :, 2:6]], axis=2
        )
        blocks = partial_faces.reshape(2, plane_size, block_rows_count, 6, slab_width)
        update_block_rows = lax.all_to_all(
            blocks, ("gy", "gz"), split_axis=1, concat_axis=1, tiled=True
        )
        row_count = update_block_rows.shape[2]
        grid_view = update_block_rows.reshape(2, count_y, count_z, row_count, 6, slab_width)
        moved = jnp.stack(
            [
                grid_view[:, :, :, :, 0],
                grid_view[:, :, :, :, 1],
                jnp.roll(grid_view[:, :, :, :, 3], 1, axis=1),
                jnp.roll(grid_view[:, :, :, :, 2], -1, axis=1),
                jnp.roll(grid_view[:, :, :, :, 5], 1, axis=2),
                jnp.roll(grid_view[:, :, :, :, 4], -1, axis=2),
            ],
            axis=4,
        )
        block_rows = moved.reshape(2, plane_size, row_count * columns_all)
        coupled = jnp.einsum("pq,rqc->rpc", mixing, block_rows, preferred_element_type=jnp.float32)
        updated = (block_rows.astype(jnp.float32) - coupled).astype(jnp.bfloat16)
        updated = updated.reshape(2, plane_size, row_count, 6, slab_width)
        returned = lax.all_to_all(updated, ("gy", "gz"), split_axis=1, concat_axis=1, tiled=True)
        incoming = returned.reshape(2, slab_rows, columns_all)
    return incoming.reshape(traces.shape)


def solution(mesh):
    placed = (
        P(None, "gx", "gy", "gz", None, None),
        P(None, "gx", "gy", "gz", None, None),
        P(None, "gx", "gy", "gz", None, None),
        P("gx", None, None),
        P("gx", None),
    )
    return jax.shard_map(
        on_device,
        mesh=mesh,
        in_specs=placed,
        out_specs=P(None, "gx", "gy", "gz", None, None),
        check_vma=False,
    )
```

profile of v0, /device:TPU:0, one launch (start us, length us, event | category | flops | bytes accessed | tf_op | source)
XLA Modules:
  0.0 244.9 jit_solution(13589258390737344345)
XLA Ops:
  0.0 0.0 copy-start
  0.0 2.4 fusion.15
  2.4 0.0 copy-done.2
  2.5 0.0 copy-start.8
  2.5 2.0 fusion.22
  4.5 0.0 copy-done.8
  4.5 0.0 copy-start.9
  4.5 0.2 convert_element_type.26
  4.8 1.2 copy-done.9
  5.9 1.7 add_convert_fusion.2
  7.6 1.7 add_convert_fusion.3
  9.4 2.3 copy.84
  11.6 2.3 copy.85
  14.0 1.3 pad_maximum_fusion.3
  15.2 0.5 collective-permute-start
  15.8 2.0 collective-permute-start.1
  17.8 4.2 %collective-permute-done = bf16[2,512,1,128]{1,3,2,0:T(8,128)(2,1)S(1)} collective-permute-done((bf16[2,512,1,128]{1,3,2,0:T(8,128)(2,1)S(1)}, bf16[2,512,1,128]{1,3,2,0:T(8,128)(2,1)S(1)}, u32[]{:S(2)}, u32[]{:S(2)}) %collective-permute-start) | collective-permute-done | bytes 262176 | tf_op jit(solution)/shard_map/ppermute | solution.py:15
  22.0 2.4 collective-permute-done.1
  24.4 0.0 copy-done.5
  24.4 0.0 copy-done.6
  24.4 1.3 fusion.9
  25.7 2.6 %copy.86 = bf16[2,512,6,128]{3,1,2,0:T(8,128)(2,1)} copy(bf16[2,512,6,128]{1,3,2,0:T(8,128)(2,1)} %fusion.9) | data formatting | bytes 3145728 | tf_op jit(solution)/shard_map/concatenate | solution.py:60
  28.3 2.7 %copy.87 = bf16[2,8,64,6,128]{4,2,3,0,1:T(8,128)(2,1)} copy(bf16[2,8,64,6,128]{4,2,1,3,0:T(8,128)(2,1)} %bitcast.150) | data formatting | bytes 3145728 | tf_op jit(solution)/shard_map/reshape | solution.py:63
  31.0 6.0 %all-to-all-start = ((bf16[2,8,64,6,128]{4,2,3,0,1:T(8,128)(2,1)}), bf16[2,8,64,6,128]{4,2,3,0,1:T(8,128)(2,1)}, u32[]{:S(2)}, u32[]{:S(2)}) async-start(bf16[2,8,64,6,128]{4,2,3,0,1:T(8,128)(2,1)} %copy.87), calls=%async_computation | async-start | bytes 3145728 | tf_op jit(solution)/shard_map/all_to_all | solution.py:64
  37.0 0.0 copy-done
  37.0 0.0 copy-done.10
  37.0 0.3 fusion.24
  37.3 37.8 %all-to-all-done = bf16[2,8,64,6,128]{4,2,3,0,1:T(8,128)(2,1)} async-done(((bf16[2,8,64,6,128]{4,2,3,0,1:T(8,128)(2,1)}), bf16[2,8,64,6,128]{4,2,3,0,1:T(8,128)(2,1)}, u32[]{:S(2)}, u32[]{:S(2)}) %all-to-all-start) | async-done | bytes 1572896 | tf_op jit(solution)/shard_map/all_to_all | solution.py:64
  75.1 1.6 copy.88
  76.7 0.1 slice_bitcast_fusion.6
  77.1 2.7 %copy.89 = bf16[2,4,2,64,6,128]{5,4,3,2,1,0:T(8,128)(2,1)} copy(bf16[2,4,2,64,6,128]{5,3,2,1,0,4:T(8,128)(2,1)S(1)} %fusion.52) | data formatting | bytes 3145728 | tf_op jit(solution)/shard_map/stack | solution.py:69
  79.8 3.8 %reshape.65 = bf16[2,8,49152]{2,1,0:T(8,128)(2,1)} reshape(bf16[2,4,2,64,6,128]{5,4,3,2,1,0:T(8,128)(2,1)} %copy.89) | data formatting | bytes 3145728 | tf_op jit(solution)/shard_map/reshape | solution.py:80
  83.6 2.5 %fusion.3 = bf16[2,8,49152]{2,1,0:T(8,128)(2,1)S(1)} fusion(bf16[2,8,49152]{2,1,0:T(8,128)(2,1)} %reshape.65, bf16[8,8,1]{1,0,2:T(8,128)(2,1)S(1)} %fusion.24), kind=kOutput, calls=%fused_computation.5 | convolution fusion | flops 14942208 | bytes 3145856 | tf_op jit(solution)/shard_map/pq,rqc->rpc/dot_general | solution.py:81
  86.1 0.4 copy.91
  86.5 40.6 %all_to_all.20 = bf16[2,8,64,6,128]{4,2,3,0,1:T(8,128)(2,1)S(1)} all-to-all(bf16[2,8,64,6,128]{4,2,3,0,1:T(8,128)(2,1)S(1)} %copy.91), channel_id=1, replica_groups=mesh['gx'=4,'gy'=4,'gz'=2] {'gy','gz'}, dimensions={1} | all-to-all | bytes 3145728 | tf_op jit(solution)/shard_map/all_to_all | solution.py:84
  127.2 0.2 fusion.61
  127.3 0.6 copy.92
  127.9 0.9 copy-done.3
  128.8 0.8 fusion.12
  129.6 1.9 fusion.19
  131.6 0.6 copy.93
  132.1 0.0 copy-start.7
  132.1 1.0 copy-done.7
  133.1 1.7 add_convert_fusion
  134.8 2.3 copy.95
  137.2 3.8 %add_convert_fusion.1 = bf16[512,768]{1,0:T(8,128)(2,1)} fusion(f32[512,768]{1,0:T(8,128)} %fusion.19, f32[2,1,1,1,512,768]{5,4,3,2,1,0:T(8,128)S(1)} %convert_element_type.26, bf16[2,1,1,1,768,768]{5,4,3,2,1,0:T(8,128)(2,1)} %param.7, bf16[64,8,6,128]{3,2,1,0:T(8,128)(2,1)} %bitcast.145), kind=kOutput, calls=%fused_computation.18 | convolution fusion | flops 605159424 | bytes 6160384 | tf_op jit(solution)/shard_map/dot_general | solution.py:46
  141.0 1.5 copy.94
  142.5 0.1 collective-permute-start.2
  142.6 1.7 collective-permute-start.3
  144.3 5.1 %collective-permute-done.2 = bf16[2,512,1,128]{1,3,2,0:T(8,128)(2,1)S(1)} collective-permute-done((bf16[2,512,1,128]{1,3,2,0:T(8,128)(2,1)S(1)}, bf16[2,512,1,128]{1,3,2,0:T(8,128)(2,1)S(1)}, u32[]{:S(2)}, u32[]{:S(2)}) %collective-permute-start.2) | collective-permute-done | bytes 262176 | tf_op jit(solution)/shard_map/ppermute | solution.py:15
  149.4 0.8 collective-permute-done.3
  150.2 0.1 fusion.11
  150.3 0.9 copy.96
  151.2 0.2 copy.97
  151.4 41.4 %all_to_all.21 = bf16[2,8,64,6,128]{4,2,3,0,1:T(8,128)(2,1)S(1)} all-to-all(bf16[2,8,64,6,128]{4,2,3,0,1:T(8,128)(2,1)S(1)} %copy.97), channel_id=1, replica_groups=mesh['gx'=4,'gy'=4,'gz'=2] {'gy','gz'}, dimensions={1} | all-to-all | bytes 3145728 | tf_op jit(solution)/shard_map/all_to_all | solution.py:64
  192.7 0.2 copy.98
  192.9 0.1 slice_bitcast_fusion.2
  193.4 1.3 copy.99
  194.7 2.6 %reshape.70 = bf16[2,8,49152]{2,1,0:T(8,128)(2,1)} reshape(bf16[2,4,2,64,6,128]{5,4,3,2,1,0:T(8,128)(2,1)S(1)} %copy.99) | data formatting | bytes 3145728 | tf_op jit(solution)/shard_map/reshape | solution.py:80
  197.3 2.5 %fusion.2 = bf16[2,8,49152]{2,1,0:T(8,128)(2,1)S(1)} fusion(bf16[2,8,49152]{2,1,0:T(8,128)(2,1)} %reshape.70, bf16[8,8,1]{1,0,2:T(8,128)(2,1)S(1)} %fusion.24), kind=kOutput, calls=%fused_computation.4 | convolution fusion | flops 14942208 | bytes 3145856 | tf_op jit(solution)/shard_map/pq,rqc->rpc/dot_general | solution.py:81
  199.8 0.4 copy.101
  200.2 40.7 %all_to_all.22 = bf16[2,8,64,6,128]{4,2,3,0,1:T(8,128)(2,1)S(1)} all-to-all(bf16[2,8,64,6,128]{4,2,3,0,1:T(8,128)(2,1)S(1)} %copy.101), channel_id=1, replica_groups=mesh['gx'=4,'gy'=4,'gz'=2] {'gy','gz'}, dimensions={1} | all-to-all | bytes 3145728 | tf_op jit(solution)/shard_map/all_to_all | solution.py:84
  240.9 1.3 copy.102
  242.2 2.7 %reshape_reshape.3 = bf16[2,1,1,1,512,768]{5,4,0,3,2,1:T(8,128)(2,1)} reshape(bf16[2,8,64,6,128]{4,3,2,1,0:T(8,128)(2,1)S(1)} %copy.102) | data formatting | bytes 3145728 | tf_op jit(solution)/shard_map/reshape;reshape | solution.py:86
  (31 shorter events, 0.6 us)
Async XLA Ops:
  0.0 37.0 %copy-start = (bf16[1,8,8]{2,1,0:T(8,128)(2,1)S(1)}, bf16[1,8,8]{2,1,0:T(8,128)(2,1)}, u32[]{:S(2)}) copy-start(bf16[1,8,8]{2,1,0:T(8,128)(2,1)} %param.8) | copy-start | bytes 388
  0.0 2.4 copy-start.2
  2.5 2.0 copy-start.8
  4.5 1.4 copy-start.9
  14.0 10.4 %copy-start.5 = (bf16[512,768]{0,1:T(8,128)(2,1)S(1)}, bf16[512,768]{0,1:T(8,128)(2,1)}, u32[]{:S(2)}) copy-start(bf16[512,768]{0,1:T(8,128)(2,1)} %copy.84) | copy-start | bytes 2359300
  14.0 10.4 %copy-start.6 = (bf16[512,768]{0,1:T(8,128)(2,1)S(1)}, bf16[512,768]{0,1:T(8,128)(2,1)}, u32[]{:S(2)}) copy-start(bf16[512,768]{0,1:T(8,128)(2,1)} %copy.85) | copy-start | bytes 2359300
  15.2 6.7 %collective-permute-start = (bf16[2,512,1,128]{1,3,2,0:T(8,128)(2,1)S(1)}, bf16[2,512,1,128]{1,3,2,0:T(8,128)(2,1)S(1)}, u32[]{:S(2)}, u32[]{:S(2)}) collective-permute-start(bf16[2,512,1,128]{1,3,2,0:T(8,128)(2,1)S(1)} %get-tuple-element.17), channel_id=1, source_target_pairs={{0,8},{8,16},{16,24},{24,0},{1,9},{9,17},{17,25},{25,1},{2,10},{10... | collective-permute-start | bytes 786440 | tf_op jit(solution)/shard_map/ppermute | solution.py:15
  15.8 8.6 %collective-permute-start.1 = (bf16[2,512,1,128]{1,3,2,0:T(8,128)(2,1)S(1)}, bf16[2,512,1,128]{1,3,2,0:T(8,128)(2,1)S(1)}, u32[]{:S(2)}, u32[]{:S(2)}) collective-permute-start(bf16[2,512,1,128]{1,3,2,0:T(8,128)(2,1)S(1)} %get-tuple-element.18), channel_id=1, source_target_pairs={{8,0},{16,8},{24,16},{0,24},{9,1},{17,9},{25,17},{1,25},{10,2},{18... | collective-permute-start | bytes 786440 | tf_op jit(solution)/shard_map/ppermute | solution.py:18
  31.0 6.0 %copy-start.10 = (s32[1,8]{1,0:T(1,128)S(1)}, s32[1,8]{1,0:T(1,128)}, u32[]{:S(2)}) copy-start(s32[1,8]{1,0:T(1,128)} %param.9) | copy-start | bytes 100
  31.0 44.1 %all-to-all-start = ((bf16[2,8,64,6,128]{4,2,3,0,1:T(8,128)(2,1)}), bf16[2,8,64,6,128]{4,2,3,0,1:T(8,128)(2,1)}, u32[]{:S(2)}, u32[]{:S(2)}) async-start(bf16[2,8,64,6,128]{4,2,3,0,1:T(8,128)(2,1)} %copy.87), calls=%async_computation | async-start | bytes 3145728 | tf_op jit(solution)/shard_map/all_to_all | solution.py:64
  127.2 1.7 copy-start.3
  132.1 1.0 copy-start.7
  141.0 1.5 copy-start.4
  142.5 6.9 %collective-permute-start.2 = (bf16[2,512,1,128]{1,3,2,0:T(8,128)(2,1)S(1)}, bf16[2,512,1,128]{1,3,2,0:T(8,128)(2,1)S(1)}, u32[]{:S(2)}, u32[]{:S(2)}) collective-permute-start(bf16[2,512,1,128]{1,3,2,0:T(8,128)(2,1)S(1)} %get-tuple-element.9), channel_id=1, source_target_pairs={{0,8},{8,16},{16,24},{24,0},{1,9},{9,17},{17,25},{25,1},{2,10},{10... | collective-permute-start | bytes 786440 | tf_op jit(solution)/shard_map/ppermute | solution.py:15
  142.6 7.6 %collective-permute-start.3 = (bf16[2,512,1,128]{1,3,2,0:T(8,128)(2,1)S(1)}, bf16[2,512,1,128]{1,3,2,0:T(8,128)(2,1)S(1)}, u32[]{:S(2)}, u32[]{:S(2)}) collective-permute-start(bf16[2,512,1,128]{1,3,2,0:T(8,128)(2,1)S(1)} %get-tuple-element.10), channel_id=1, source_target_pairs={{8,0},{16,8},{24,16},{0,24},{9,1},{17,9},{25,17},{1,25},{10,2},{18... | collective-permute-start | bytes 786440 | tf_op jit(solution)/shard_map/ppermute | solution.py:18
  240.9 4.0 %copy-start.1 = (bf16[1,8,8]{2,1,0:T(8,128)(2,1)S(1)}, bf16[1,8,8]{2,1,0:T(8,128)(2,1)}, u32[]{:S(2)}) copy-start(bf16[1,8,8]{2,1,0:T(8,128)(2,1)} %param.8) | copy-start | bytes 388
where the time goes:
time: 246 us; the launch traced here: 245 us
  blocking collectives  123 us (50%)
  waiting for transfers between devices  50.3 us (20%)
  local copies, waits for them, and re-layouts  36.5 us (15%)
  matrix products  21.5 us (9%)
  starting transfers between devices  10.3 us (4%)
  other arithmetic  3.27 us (1%)
    all_to_all x2, blocking collectives, on_device(): lax.all_to_all(updated, ('gy', 'gz'), split_axis=1, concat_axis=1, tiled=...  81.3 us
    all_to_all x1, blocking collectives, on_device(): lax.all_to_all(blocks, ('gy', 'gz'), split_axis=1, concat_axis=1, tiled=T...  41.4 us
    all_to_all x1, waiting for transfers between devices, on_device(): lax.all_to_all(blocks, ('gy', 'gz'), split_axis=1, concat_axis=1, tiled=T...  37.8 us
    ppermute x2, waiting for transfers between devices, with_halo(): lax.ppermute(lax.slice_in_dim(block, block.shape[dim] - width, None, axis...  9.29 us
    another operation x4, local copies, waits for them, and re-layouts  8.41 us
    reshape x2, local copies, waits for them, and re-layouts, on_device(): block_rows = moved.reshape(2, plane_size, row_count * columns_all)  6.42 us
    all_to_all x1, starting transfers between devices, on_device(): lax.all_to_all(blocks, ('gy', 'gz'), split_axis=1, concat_axis=1, tiled=T...  5.97 us
    dot_general x2, matrix products, on_device(): jnp.dot(incoming[1], operators[1], preferred_element_type=jnp.float32)  5.54 us
  transfers between devices with their start and end apart: 5, of which 5 were waited for; matrix products, arithmetic and copies ran while one was open for 0% of the time, Pallas kernels for 0%

commit v1 on v0

--- a/solution.py
+++ b/solution.py
@@ -1,6 +1,10 @@
+import functools
+
 import jax
 import jax.numpy as jnp
 from jax import lax
+from jax.experimental import pallas as pl
+from jax.experimental.pallas import tpu as pltpu
 from jax.sharding import PartitionSpec as P
 
 SWEEPS = 2
@@ -20,7 +24,7 @@
     return block
 
 
-def on_device(traces, sources, local_ops, plane_coupling, face_owner):
+def many_subdomains(traces, sources, local_ops, plane_coupling, face_owner):
     columns_all = local_ops.shape[-1]
     slab_width = columns_all // 6
     slab_rows = traces.shape[4]
@@ -40,7 +44,7 @@
         select,
         precision=lax.Precision.HIGHEST,
     ).astype(jnp.bfloat16)
-    for sweep_step in range(SWEEPS):
+    for _ in range(SWEEPS):
         real_part = (
             jnp.dot(incoming[0], operators[0], preferred_element_type=jnp.float32)
             - jnp.dot(incoming[1], operators[1], preferred_element_type=jnp.float32)
@@ -86,6 +90,235 @@
     return incoming.reshape(traces.shape)
 
 
+CHUNKS = 2
+VMEM = pl.BlockSpec(memory_space=pltpu.VMEM)
+SMEM = pl.BlockSpec(memory_space=pltpu.SMEM)
+
+
+def plane_position():
+    return lax.axis_index("gy") * lax.axis_size("gz") + lax.axis_index("gz")
+
+
+def call(kernel, in_specs, out_shape, flops, out_specs=None, aliases=None):
+    return pl.pallas_call(
+        kernel,
+        in_specs=in_specs,
+        out_shape=out_shape,
+        out_specs=out_specs if out_specs is not None else jax.tree.map(lambda _: VMEM, out_shape),
+        input_output_aliases=aliases or {},
+        cost_estimate=pl.CostEstimate(flops=flops, bytes_accessed=1 << 20, transcendentals=0),
+        compiler_params=pltpu.CompilerParams(vmem_limit_bytes=32 << 20),
+    )
+
+
+def solve_rows(real, imag, operators_ref, source_of, outputs):
+    real_part = jnp.dot(real, operators_ref[0], preferred_element_type=jnp.float32) - jnp.dot(
+        imag, operators_ref[1], preferred_element_type=jnp.float32
+    )
+    imag_part = jnp.dot(real, operators_ref[1], preferred_element_type=jnp.float32) + jnp.dot(
+        imag, operators_ref[0], preferred_element_type=jnp.float32
+    )
+    rows = outputs[0].shape[1]
+    for part, result in enumerate((real_part, imag_part)):
+        for k, output in enumerate(outputs):
+            block = result[k * rows : (k + 1) * rows] + source_of(part, k)
+            output[part] = block.astype(output.dtype)
+
+
+def row_start(chunk, k, plane_size, rows):
+    return pl.multiple_of((chunk * plane_size + (plane_position() ^ k)) * rows, rows)
+
+
+def first_solve(chunk, plane_size, rows, traces_ref, sources_ref, operators_ref, *outputs):
+    starts = [row_start(chunk, k, plane_size, rows) for k in range(plane_size)]
+    real, imag = (
+        jnp.concatenate([traces_ref[part, pl.ds(s, rows), :] for s in starts], axis=0)
+        for part in range(2)
+    )
+    solve_rows(
+        real,
+        imag,
+        operators_ref,
+        lambda part, k: sources_ref[part, pl.ds(starts[k], rows), :].astype(jnp.float32),
+        outputs,
+    )
+
+
+def next_solve(chunk, plane_size, rows, *refs):
+    blocks, (sources_ref, operators_ref) = refs[:plane_size], refs[plane_size : plane_size + 2]
+    starts = [row_start(chunk, k, plane_size, rows) for k in range(plane_size)]
+    real, imag = (jnp.concatenate([b[part] for b in blocks], axis=0) for part in range(2))
+    solve_rows(
+        real,
+        imag,
+        operators_ref,
+        lambda part, k: sources_ref[part, pl.ds(starts[k], rows), :].astype(jnp.float32),
+        refs[plane_size + 2 :],
+    )
+
+
+def gather_x_faces(plane_size, width, *refs):
+    blocks, (low_ref, high_ref) = refs[:plane_size], refs[plane_size:]
+    for k, block in enumerate(blocks):
+        low_ref[k] = block[:, :, 0:width]
+        high_ref[k] = block[:, :, width : 2 * width]
+
+
+def make_weights(count_y, count_z, coupling_ref, owner_ref, weights_ref, column_ref):
+    plane_size = count_y * count_z
+    me = plane_position()
+
+    def clear(q, carry):
+        for p in range(plane_size):
+            column_ref[p, q] = jnp.where(p == q, jnp.float32(1), jnp.float32(0))
+        return carry
+
+    def couple(q, carry):
+        owner = owner_ref[q]
+        for p in range(plane_size):
+            column_ref[p, owner] = column_ref[p, owner] - coupling_ref[p, q]
+        return carry
+
+    lax.fori_loop(0, plane_size, clear, 0)
+    lax.fori_loop(0, plane_size, couple, 0)
+
+    def fill(m, carry):
+        source = me ^ m
+        y, z = source // count_z, source % count_z
+        receivers = (
+            source,
+            ((y + 1) % count_y) * count_z + z,
+            ((y + count_y - 1) % count_y) * count_z + z,
+            y * count_z + (z + 1) % count_z,
+            y * count_z + (z + count_z - 1) % count_z,
+        )
+        for face, receiver in enumerate(receivers):
+            for k in range(plane_size):
+                weights_ref[face, k, m] = column_ref[me ^ k, receiver]
+        return carry
+
+    lax.fori_loop(0, plane_size, fill, 0)
+
+
+def mix_blocks(plane_size, width, *refs):
+    blocks = refs[:plane_size]
+    from_low_ref, from_high_ref, weights_ref = refs[plane_size : plane_size + 3]
+    outputs = refs[plane_size + 3 :]
+    plan = ((0, None), (0, None), (1, 3), (2, 2), (3, 5), (4, 4))
+    for face, (kind, source_face) in enumerate(plan):
+        for part in range(2):
+            if source_face is None:
+                arrived = (from_low_ref, from_high_ref)[face]
+                values = [arrived[m, part].astype(jnp.float32) for m in range(plane_size)]
+            else:
+                columns = slice(source_face * width, (source_face + 1) * width)
+                values = [b[part, :, columns].astype(jnp.float32) for b in blocks]
+            for k, output in enumerate(outputs):
+                total = values[0] * weights_ref[kind, k, 0]
+                for m in range(1, plane_size):
+                    total = total + values[m] * weights_ref[kind, k, m]
+                output[part, :, face * width : (face + 1) * width] = total.astype(output.dtype)
+
+
+def store_rows(chunks, plane_size, rows, *refs):
+    blocks, out_ref, sems = refs[: chunks * plane_size], refs[-2], refs[-1]
+    copies = []
+    for chunk in range(chunks):
+        for k in range(plane_size):
+            index = chunk * plane_size + k
+            copies.append(
+                pltpu.make_async_copy(
+                    blocks[index],
+                    out_ref.at[:, pl.ds(row_start(chunk, k, plane_size, rows), rows), :],
+                    sems.at[index],
+                )
+            )
+    for copy in copies:
+        copy.start()
+    for copy in copies:
+        copy.wait()
+
+
+def exchange(blocks, count_y, count_z):
+    plane_size = count_y * count_z
+    across = sorted(range(1, plane_size), key=lambda k: (-((k // count_z) // 2 > 0), k % count_z, k))
+    received = [blocks[0]] + [None] * (plane_size - 1)
+    for k in across:
+        received[k] = lax.ppermute(blocks[k], ("gy", "gz"), [(p, p ^ k) for p in range(plane_size)])
+    return received
+
+
+def few_subdomains(traces, sources, local_ops, plane_coupling, face_owner):
+    columns_all = local_ops.shape[-1]
+    width = columns_all // 6
+    slab_rows = traces.shape[4]
+    count_x, count_y, count_z = (lax.axis_size(a) for a in ("gx", "gy", "gz"))
+    plane_size = count_y * count_z
+    rows = slab_rows // (plane_size * CHUNKS)
+    operators = local_ops.reshape(2, columns_all, columns_all)
+    source_rows = sources.reshape(2, slab_rows, columns_all)
+    trace_rows = traces.reshape(2, slab_rows, columns_all)
+    block = jax.ShapeDtypeStruct((2, rows, columns_all), traces.dtype)
+    face = jax.ShapeDtypeStruct((plane_size, 2, rows, width), traces.dtype)
+    solve_flops = 8 * plane_size * rows * columns_all * columns_all
+    forward = [(i, (i + 1) % count_x) for i in range(count_x)]
+    backward = [(target, source) for source, target in forward]
+
+    weights = pl.pallas_call(
+        functools.partial(make_weights, count_y, count_z),
+        in_specs=[SMEM, SMEM],
+        out_specs=SMEM,
+        out_shape=jax.ShapeDtypeStruct((5, plane_size, plane_size), jnp.float32),
+        scratch_shapes=[pltpu.SMEM((plane_size, plane_size), jnp.float32)],
+    )(
+        plane_coupling.reshape(plane_size, plane_size).astype(jnp.float32),
+        face_owner.reshape(plane_size),
+    )
+    incoming = [None] * CHUNKS
+    for sweep in range(SWEEPS):
+        gathered = []
+        for chunk in range(CHUNKS):
+            if sweep == 0:
+                outgoing = call(
+                    functools.partial(first_solve, chunk, plane_size, rows),
+                    [VMEM] * 3,
+                    [block] * plane_size,
+                    solve_flops,
+                )(trace_rows, source_rows, operators)
+            else:
+                outgoing = call(
+                    functools.partial(next_solve, chunk, plane_size, rows),
+                    [VMEM] * (plane_size + 2),
+                    [block] * plane_size,
+                    solve_flops,
+                )(*incoming[chunk], source_rows, operators)
+            gathered.append(exchange(outgoing, count_y, count_z))
+        for chunk in range(CHUNKS):
+            low, high = call(
+                functools.partial(gather_x_faces, plane_size, width),
+                [VMEM] * plane_size,
+                [face] * 2,
+                solve_flops // 4,
+            )(*gathered[chunk])
+            from_low = lax.ppermute(high, "gx", forward)
+            from_high = lax.ppermute(low, "gx", backward)
+            updated = call(
+                functools.partial(mix_blocks, plane_size, width),
+                [VMEM] * (plane_size + 2) + [SMEM],
+                [block] * plane_size,
+                solve_flops,
+            )(*gathered[chunk], from_low, from_high, weights)
+            incoming[chunk] = exchange(updated, count_y, count_z)
+    result = pl.pallas_call(
+        functools.partial(store_rows, CHUNKS, plane_size, rows),
+        in_specs=[VMEM] * (CHUNKS * plane_size),
+        out_specs=pl.BlockSpec(memory_space=pl.ANY),
+        out_shape=jax.ShapeDtypeStruct((2, slab_rows, columns_all), traces.dtype),
+        scratch_shapes=[pltpu.SemaphoreType.DMA((CHUNKS * plane_size,))],
+    )(*(b for chunk in incoming for b in chunk))
+    return result.reshape(traces.shape)
+
+
 def solution(mesh):
     placed = (
         P(None, "gx", "gy", "gz", None, None),
@@ -94,8 +327,9 @@
         P("gx", None, None),
         P("gx", None),
     )
+    few = mesh.shape["gy"] * mesh.shape["gz"] <= 8
     return jax.shard_map(
-        on_device,
+        few_subdomains if few else many_subdomains,
         mesh=mesh,
         in_specs=placed,
         out_specs=P(None, "gx", "gy", "gz", None, None),

time: 246 us -> 172 us (0.70)
  blocking collectives: 123 us -> 0 us
  starting transfers between devices: 10.3 us -> 112 us
  local copies, waits for them, and re-layouts: 36.5 us -> 7.14 us
  matrix products: 21.5 us -> 0 us
  Pallas kernels: 0 us -> 18.6 us
  waiting for transfers between devices: 50.3 us -> 32.4 us
  other arithmetic: 3.27 us -> 0.58 us
    all_to_all x3 -> x0, blocking collectives: 123 us -> none  [the longest x2 81.3 us: on_device(): lax.all_to_all(updated, ('gy', 'gz'), split_axis=1, concat_axis=1, tiled=...]
    ppermute x4 -> x64, starting transfers between devices: 4.31 us -> 112 us  [the longest x56 108 us: exchange(): lax.ppermute(blocks[k], ('gy', 'gz'), [(p, p ^ k) for p in range(plane_si...]
    all_to_all x1 -> x0, waiting for transfers between devices: 37.8 us -> none  [on_device(): lax.all_to_all(blocks, ('gy', 'gz'), split_axis=1, concat_axis=1, tiled=T...]
    dot_general x11 -> x0, matrix products: 21.5 us -> none  [the longest x2 5.54 us: on_device(): jnp.dot(incoming[1], operators[1], preferred_element_type=jnp.float32)]
    ppermute x4 -> x64, waiting for transfers between devices: 12.5 us -> 32.4 us  [the longest x56 32.4 us: exchange(): lax.ppermute(blocks[k], ('gy', 'gz'), [(p, p ^ k) for p in range(plane_si...]
    pallas_call x0 -> x14, Pallas kernels: none -> 18.6 us  [the longest x4 7.34 us: few_subdomains(): call(functools.partial(mix_blocks, plane_size, width), [VMEM] * (plane_si...]
    another operation x7 -> x0, local copies, waits for them, and re-layouts: 15.1 us -> none
    reshape x6 -> x0, local copies, waits for them, and re-layouts: 10.1 us -> none  [the longest x2 6.42 us: on_device(): block_rows = moved.reshape(2, plane_size, row_count * columns_all)]
  transfers between devices with their start and end apart: 5 -> 64, of which waited for: 5 -> 13; matrix products, arithmetic and copies ran while one was open for 0% -> 0% of each run, Pallas kernels for 0% -> 8%
where the time goes in v1:
time: 172 us; the launch traced here: 171 us
  starting transfers between devices  112 us (65%)
  waiting for transfers between devices  32.4 us (19%)
  Pallas kernels  18.6 us (11%)
  local copies, waits for them, and re-layouts  7.14 us (4%)
    ppermute x56, starting transfers between devices, exchange(): lax.ppermute(blocks[k], ('gy', 'gz'), [(p, p ^ k) for p in range(plane_si...  108 us
    ppermute x56, waiting for transfers between devices, exchange(): lax.ppermute(blocks[k], ('gy', 'gz'), [(p, p ^ k) for p in range(plane_si...  32.4 us
    pallas_call x4, Pallas kernels, few_subdomains(): call(functools.partial(mix_blocks, plane_size, width), [VMEM] * (plane_si...  7.34 us
    unnamed x48, local copies, waits for them, and re-layouts  7.14 us
    ppermute x4, starting transfers between devices, few_subdomains(): from_high = lax.ppermute(low, 'gx', backward)  4 us
  transfers between devices with their start and end apart: 64, of which 13 were waited for; matrix products, arithmetic and copies ran while one was open for 0% of the time, Pallas kernels for 8%

profile of v1, /device:TPU:0, one launch (start us, length us, event | category | flops | bytes accessed | tf_op | source)
XLA Modules:
  0.0 171.2 jit_solution(14920637063713950058)
XLA Ops:
  0.0 1.7 copy-done
  1.7 1.4 copy-done.2
  3.1 1.4 copy-done.4
  4.5 1.4 shard_map.62
  5.9 3.1 %collective-permute-start.32 = (bf16[2,32,768]{2,1,0:T(8,128)(2,1)S(1)}, bf16[2,32,768]{2,1,0:T(8,128)(2,1)S(1)}, u32[]{:S(2)}, u32[]{:S(2)}) collective-permute-start(bf16[2,32,768]{2,1,0:T(8,128)(2,1)S(1)} %get-tuple-element.114), channel_id=1, source_target_pairs={{0,1},{1,0},{2,3},{3,2},{4,5},{5,4},{6,7},{7,6},{8,9},{9,8},{10,11... | collective-permute-start | bytes 294920 | tf_op jit(solution)/shard_map/ppermute | solution.py:247
  8.9 1.6 collective-permute-start.33
  10.5 3.0 %collective-permute-start.35 = (bf16[2,32,768]{2,1,0:T(8,128)(2,1)S(1)}, bf16[2,32,768]{2,1,0:T(8,128)(2,1)S(1)}, u32[]{:S(2)}, u32[]{:S(2)}) collective-permute-start(bf16[2,32,768]{2,1,0:T(8,128)(2,1)S(1)} %get-tuple-element.117), channel_id=1, source_target_pairs={{0,4},{1,5},{2,6},{3,7},{4,0},{5,1},{6,2},{7,3},{8,12},{9,13},{10,... | collective-permute-start | bytes 294920 | tf_op jit(solution)/shard_map/ppermute | solution.py:247
  13.5 1.3 collective-permute-start.36
  14.8 3.6 %collective-permute-start.37 = (bf16[2,32,768]{2,1,0:T(8,128)(2,1)S(1)}, bf16[2,32,768]{2,1,0:T(8,128)(2,1)S(1)}, u32[]{:S(2)}, u32[]{:S(2)}) collective-permute-start(bf16[2,32,768]{2,1,0:T(8,128)(2,1)S(1)} %get-tuple-element.119), channel_id=1, source_target_pairs={{0,6},{1,7},{2,4},{3,5},{4,2},{5,3},{6,0},{7,1},{8,14},{9,15},{10,... | collective-permute-start | bytes 294920 | tf_op jit(solution)/shard_map/ppermute | solution.py:247
  18.4 1.4 shard_map.55
  19.8 2.1 %collective-permute-start = (bf16[2,32,768]{2,1,0:T(8,128)(2,1)S(1)}, bf16[2,32,768]{2,1,0:T(8,128)(2,1)S(1)}, u32[]{:S(2)}, u32[]{:S(2)}) collective-permute-start(bf16[2,32,768]{2,1,0:T(8,128)(2,1)S(1)} %get-tuple-element.78), channel_id=1, source_target_pairs={{0,1},{1,0},{2,3},{3,2},{4,5},{5,4},{6,7},{7,6},{8,9},{9,8},{10,11... | collective-permute-start | bytes 294920 | tf_op jit(solution)/shard_map/ppermute | solution.py:247
  21.9 3.9 %collective-permute-start.1 = (bf16[2,32,768]{2,1,0:T(8,128)(2,1)S(1)}, bf16[2,32,768]{2,1,0:T(8,128)(2,1)S(1)}, u32[]{:S(2)}, u32[]{:S(2)}) collective-permute-start(bf16[2,32,768]{2,1,0:T(8,128)(2,1)S(1)} %get-tuple-element.79), channel_id=1, source_target_pairs={{0,2},{1,3},{2,0},{3,1},{4,6},{5,7},{6,4},{7,5},{8,10},{9,11},{10,... | collective-permute-start | bytes 294920 | tf_op jit(solution)/shard_map/ppermute | solution.py:247
  25.8 2.9 %collective-permute-done.36.refs_5_ = bf16[2,32,768]{2,1,0:T(8,128)(2,1)S(1)} collective-permute-done((bf16[2,32,768]{2,1,0:T(8,128)(2,1)S(1)}, bf16[2,32,768]{2,1,0:T(8,128)(2,1)S(1)}, u32[]{:S(2)}, u32[]{:S(2)}) %collective-permute-start.36) | collective-permute-done | bytes 98336 | tf_op jit(solution)/shard_map/ppermute | solution.py:247
  28.8 3.5 %collective-permute-start.3 = (bf16[2,32,768]{2,1,0:T(8,128)(2,1)S(1)}, bf16[2,32,768]{2,1,0:T(8,128)(2,1)S(1)}, u32[]{:S(2)}, u32[]{:S(2)}) collective-permute-start(bf16[2,32,768]{2,1,0:T(8,128)(2,1)S(1)} %get-tuple-element.81), channel_id=1, source_target_pairs={{0,4},{1,5},{2,6},{3,7},{4,0},{5,1},{6,2},{7,3},{8,12},{9,13},{10,... | collective-permute-start | bytes 294920 | tf_op jit(solution)/shard_map/ppermute | solution.py:247
  32.3 2.9 %collective-permute-start.4 = (bf16[2,32,768]{2,1,0:T(8,128)(2,1)S(1)}, bf16[2,32,768]{2,1,0:T(8,128)(2,1)S(1)}, u32[]{:S(2)}, u32[]{:S(2)}) collective-permute-start(bf16[2,32,768]{2,1,0:T(8,128)(2,1)S(1)} %get-tuple-element.82), channel_id=1, source_target_pairs={{0,5},{1,4},{2,7},{3,6},{4,1},{5,0},{6,3},{7,2},{8,13},{9,12},{10,... | collective-permute-start | bytes 294920 | tf_op jit(solution)/shard_map/ppermute | solution.py:247
  36.0 4.7 %collective-permute-start.6 = (bf16[2,32,768]{2,1,0:T(8,128)(2,1)S(1)}, bf16[2,32,768]{2,1,0:T(8,128)(2,1)S(1)}, u32[]{:S(2)}, u32[]{:S(2)}) collective-permute-start(bf16[2,32,768]{2,1,0:T(8,128)(2,1)S(1)} %get-tuple-element.84), channel_id=1, source_target_pairs={{0,7},{1,6},{2,5},{3,4},{4,3},{5,2},{6,1},{7,0},{8,15},{9,14},{10,... | collective-permute-start | bytes 294920 | tf_op jit(solution)/shard_map/ppermute | solution.py:247
  40.7 1.2 collective-permute-done.3.refs_4_
  43.0 2.7 %shard_map.57.refs_10_ = f32[5,8,8]{2,1,0:T(8,128)} custom-call(f32[8,8]{1,0:T(8,128)} %bitcast_convert_fusion.coupling_ref, s32[8]{0:T(128)} %bitcast.20), custom_call_target="tpu_custom_call" | custom-call | tf_op jit(solution)/shard_map/pallas_call | solution.py:267
  46.2 1.7 %collective-permute-start.8 = (bf16[8,2,32,128]{3,2,1,0:T(8,128)(2,1)S(1)}, bf16[8,2,32,128]{3,2,1,0:T(8,128)(2,1)S(1)}, u32[]{:S(2)}, u32[]{:S(2)}) collective-permute-start(bf16[8,2,32,128]{3,2,1,0:T(8,128)(2,1)S(1)} %get-tuple-element.86), channel_id=1, source_target_pairs={{8,0},{16,8},{24,16},{0,24},{9,1},{17,9},{25,17},{1,25},{10,2},{18... | collective-permute-start | bytes 393224 | tf_op jit(solution)/shard_map/ppermute | solution.py:304
  48.7 1.8 %shard_map.64 = (bf16[2,32,768]{2,1,0:T(8,128)(2,1)S(1)}, bf16[2,32,768]{2,1,0:T(8,128)(2,1)S(1)}, bf16[2,32,768]{2,1,0:T(8,128)(2,1)S(1)}, bf16[2,32,768]{2,1,0...) custom-call(bf16[2,32,768]{2,1,0:T(8,128)(2,1)S(1)} %get-tuple-eleme, ...), custom_call_target="tpu_custom_call" | custom-call | flops 1207959552 | bytes 1048576 | tf_op jit(solution)/shard_map/pallas_call | solution.py:305
  51.0 4.1 %collective-permute-start.42 = (bf16[2,32,768]{2,1,0:T(8,128)(2,1)S(1)}, bf16[2,32,768]{2,1,0:T(8,128)(2,1)S(1)}, u32[]{:S(2)}, u32[]{:S(2)}) collective-permute-start(bf16[2,32,768]{2,1,0:T(8,128)(2,1)S(1)} %get-tuple-element.125), channel_id=1, source_target_pairs={{0,2},{1,3},{2,0},{3,1},{4,6},{5,7},{6,4},{7,5},{8,10},{9,11},{10,... | collective-permute-start | bytes 294920 | tf_op jit(solution)/shard_map/ppermute | solution.py:247
  55.6 3.2 %collective-permute-start.44 = (bf16[2,32,768]{2,1,0:T(8,128)(2,1)S(1)}, bf16[2,32,768]{2,1,0:T(8,128)(2,1)S(1)}, u32[]{:S(2)}, u32[]{:S(2)}) collective-permute-start(bf16[2,32,768]{2,1,0:T(8,128)(2,1)S(1)} %get-tuple-element.127), channel_id=1, source_target_pairs={{0,4},{1,5},{2,6},{3,7},{4,0},{5,1},{6,2},{7,3},{8,12},{9,13},{10,... | collective-permute-start | bytes 294920 | tf_op jit(solution)/shard_map/ppermute | solution.py:247
  58.9 2.2 %collective-permute-start.46 = (bf16[2,32,768]{2,1,0:T(8,128)(2,1)S(1)}, bf16[2,32,768]{2,1,0:T(8,128)(2,1)S(1)}, u32[]{:S(2)}, u32[]{:S(2)}) collective-permute-start(bf16[2,32,768]{2,1,0:T(8,128)(2,1)S(1)} %get-tuple-element.129), channel_id=1, source_target_pairs={{0,6},{1,7},{2,4},{3,5},{4,2},{5,3},{6,0},{7,1},{8,14},{9,15},{10,... | collective-permute-start | bytes 294920 | tf_op jit(solution)/shard_map/ppermute | solution.py:247
  61.1 2.4 %collective-permute-start.47 = (bf16[2,32,768]{2,1,0:T(8,128)(2,1)S(1)}, bf16[2,32,768]{2,1,0:T(8,128)(2,1)S(1)}, u32[]{:S(2)}, u32[]{:S(2)}) collective-permute-start(bf16[2,32,768]{2,1,0:T(8,128)(2,1)S(1)} %get-tuple-element.130), channel_id=1, source_target_pairs={{0,7},{1,6},{2,5},{3,4},{4,3},{5,2},{6,1},{7,0},{8,15},{9,14},{10,... | collective-permute-start | bytes 294920 | tf_op jit(solution)/shard_map/ppermute | solution.py:247
  63.6 1.8 %shard_map.58 = (bf16[2,32,768]{2,1,0:T(8,128)(2,1)S(1)}, bf16[2,32,768]{2,1,0:T(8,128)(2,1)S(1)}, bf16[2,32,768]{2,1,0:T(8,128)(2,1)S(1)}, bf16[2,32,768]{2,1,0...) custom-call(bf16[2,32,768]{2,1,0:T(8,128)(2,1)S(1)} %get-tuple-eleme, ...), custom_call_target="tpu_custom_call" | custom-call | flops 1207959552 | bytes 1048576 | tf_op jit(solution)/shard_map/pallas_call | solution.py:305
  66.1 3.4 %collective-permute-done.44.refs_4_ = bf16[2,32,768]{2,1,0:T(8,128)(2,1)S(1)} collective-permute-done((bf16[2,32,768]{2,1,0:T(8,128)(2,1)S(1)}, bf16[2,32,768]{2,1,0:T(8,128)(2,1)S(1)}, u32[]{:S(2)}, u32[]{:S(2)}) %collective-permute-start.44) | collective-permute-done | bytes 98336 | tf_op jit(solution)/shard_map/ppermute | solution.py:247
  70.1 3.1 %collective-permute-done.45.refs_5_ = bf16[2,32,768]{2,1,0:T(8,128)(2,1)S(1)} collective-permute-done((bf16[2,32,768]{2,1,0:T(8,128)(2,1)S(1)}, bf16[2,32,768]{2,1,0:T(8,128)(2,1)S(1)}, u32[]{:S(2)}, u32[]{:S(2)}) %collective-permute-start.45) | collective-permute-done | bytes 98336 | tf_op jit(solution)/shard_map/ppermute | solution.py:247
  73.2 3.3 %collective-permute-start.12 = (bf16[2,32,768]{2,1,0:T(8,128)(2,1)S(1)}, bf16[2,32,768]{2,1,0:T(8,128)(2,1)S(1)}, u32[]{:S(2)}, u32[]{:S(2)}) collective-permute-start(bf16[2,32,768]{2,1,0:T(8,128)(2,1)S(1)} %get-tuple-element.91), channel_id=1, source_target_pairs={{0,4},{1,5},{2,6},{3,7},{4,0},{5,1},{6,2},{7,3},{8,12},{9,13},{10,... | collective-permute-start | bytes 294920 | tf_op jit(solution)/shard_map/ppermute | solution.py:247
  76.6 3.5 %collective-permute-start.13 = (bf16[2,32,768]{2,1,0:T(8,128)(2,1)S(1)}, bf16[2,32,768]{2,1,0:T(8,128)(2,1)S(1)}, u32[]{:S(2)}, u32[]{:S(2)}) collective-permute-start(bf16[2,32,768]{2,1,0:T(8,128)(2,1)S(1)} %get-tuple-element.92), channel_id=1, source_target_pairs={{0,5},{1,4},{2,7},{3,6},{4,1},{5,0},{6,3},{7,2},{8,13},{9,12},{10,... | collective-permute-start | bytes 294920 | tf_op jit(solution)/shard_map/ppermute | solution.py:247
  80.1 1.4 shard_map.65
  82.1 2.6 %collective-permute-start.15 = (bf16[2,32,768]{2,1,0:T(8,128)(2,1)S(1)}, bf16[2,32,768]{2,1,0:T(8,128)(2,1)S(1)}, u32[]{:S(2)}, u32[]{:S(2)}) collective-permute-start(bf16[2,32,768]{2,1,0:T(8,128)(2,1)S(1)} %get-tuple-element.94), channel_id=1, source_target_pairs={{0,7},{1,6},{2,5},{3,4},{4,3},{5,2},{6,1},{7,0},{8,15},{9,14},{10,... | collective-permute-start | bytes 294920 | tf_op jit(solution)/shard_map/ppermute | solution.py:247
  84.7 2.1 %collective-permute-start.48 = (bf16[2,32,768]{2,1,0:T(8,128)(2,1)S(1)}, bf16[2,32,768]{2,1,0:T(8,128)(2,1)S(1)}, u32[]{:S(2)}, u32[]{:S(2)}) collective-permute-start(bf16[2,32,768]{2,1,0:T(8,128)(2,1)S(1)} %get-tuple-element.132), channel_id=1, source_target_pairs={{0,1},{1,0},{2,3},{3,2},{4,5},{5,4},{6,7},{7,6},{8,9},{9,8},{10,11... | collective-permute-start | bytes 294920 | tf_op jit(solution)/shard_map/ppermute | solution.py:247
  86.9 1.9 %collective-permute-done.13.refs_5_ = bf16[2,32,768]{2,1,0:T(8,128)(2,1)S(1)} collective-permute-done((bf16[2,32,768]{2,1,0:T(8,128)(2,1)S(1)}, bf16[2,32,768]{2,1,0:T(8,128)(2,1)S(1)}, u32[]{:S(2)}, u32[]{:S(2)}) %collective-permute-start.13) | collective-permute-done | bytes 98336 | tf_op jit(solution)/shard_map/ppermute | solution.py:247
  88.7 4.4 %collective-permute-start.51 = (bf16[2,32,768]{2,1,0:T(8,128)(2,1)S(1)}, bf16[2,32,768]{2,1,0:T(8,128)(2,1)S(1)}, u32[]{:S(2)}, u32[]{:S(2)}) collective-permute-start(bf16[2,32,768]{2,1,0:T(8,128)(2,1)S(1)} %get-tuple-element.135), channel_id=1, source_target_pairs={{0,4},{1,5},{2,6},{3,7},{4,0},{5,1},{6,2},{7,3},{8,12},{9,13},{10,... | collective-permute-start | bytes 294920 | tf_op jit(solution)/shard_map/ppermute | solution.py:247
  93.1 4.1 %collective-permute-start.52 = (bf16[2,32,768]{2,1,0:T(8,128)(2,1)S(1)}, bf16[2,32,768]{2,1,0:T(8,128)(2,1)S(1)}, u32[]{:S(2)}, u32[]{:S(2)}) collective-permute-start(bf16[2,32,768]{2,1,0:T(8,128)(2,1)S(1)} %get-tuple-element.136), channel_id=1, source_target_pairs={{0,5},{1,4},{2,7},{3,6},{4,1},{5,0},{6,3},{7,2},{8,13},{9,12},{10,... | collective-permute-start | bytes 294920 | tf_op jit(solution)/shard_map/ppermute | solution.py:247
  97.2 2.1 %collective-permute-start.53 = (bf16[2,32,768]{2,1,0:T(8,128)(2,1)S(1)}, bf16[2,32,768]{2,1,0:T(8,128)(2,1)S(1)}, u32[]{:S(2)}, u32[]{:S(2)}) collective-permute-start(bf16[2,32,768]{2,1,0:T(8,128)(2,1)S(1)} %get-tuple-element.137), channel_id=1, source_target_pairs={{0,6},{1,7},{2,4},{3,5},{4,2},{5,3},{6,0},{7,1},{8,14},{9,15},{10,... | collective-permute-start | bytes 294920 | tf_op jit(solution)/shard_map/ppermute | solution.py:247
  99.2 1.4 shard_map.59
  100.7 2.3 %collective-permute-start.54 = (bf16[2,32,768]{2,1,0:T(8,128)(2,1)S(1)}, bf16[2,32,768]{2,1,0:T(8,128)(2,1)S(1)}, u32[]{:S(2)}, u32[]{:S(2)}) collective-permute-start(bf16[2,32,768]{2,1,0:T(8,128)(2,1)S(1)} %get-tuple-element.138), channel_id=1, source_target_pairs={{0,7},{1,6},{2,5},{3,4},{4,3},{5,2},{6,1},{7,0},{8,15},{9,14},{10,... | collective-permute-start | bytes 294920 | tf_op jit(solution)/shard_map/ppermute | solution.py:247
  103.0 1.0 collective-permute-start.16
  104.0 2.2 %collective-permute-done.52.refs_5_ = bf16[2,32,768]{2,1,0:T(8,128)(2,1)S(1)} collective-permute-done((bf16[2,32,768]{2,1,0:T(8,128)(2,1)S(1)}, bf16[2,32,768]{2,1,0:T(8,128)(2,1)S(1)}, u32[]{:S(2)}, u32[]{:S(2)}) %collective-permute-start.52) | collective-permute-done | bytes 98336 | tf_op jit(solution)/shard_map/ppermute | solution.py:247
  106.5 3.5 %collective-permute-start.19 = (bf16[2,32,768]{2,1,0:T(8,128)(2,1)S(1)}, bf16[2,32,768]{2,1,0:T(8,128)(2,1)S(1)}, u32[]{:S(2)}, u32[]{:S(2)}) collective-permute-start(bf16[2,32,768]{2,1,0:T(8,128)(2,1)S(1)} %get-tuple-element.99), channel_id=1, source_target_pairs={{0,4},{1,5},{2,6},{3,7},{4,0},{5,1},{6,2},{7,3},{8,12},{9,13},{10,... | collective-permute-start | bytes 294920 | tf_op jit(solution)/shard_map/ppermute | solution.py:247
  110.0 4.1 %collective-permute-start.20 = (bf16[2,32,768]{2,1,0:T(8,128)(2,1)S(1)}, bf16[2,32,768]{2,1,0:T(8,128)(2,1)S(1)}, u32[]{:S(2)}, u32[]{:S(2)}) collective-permute-start(bf16[2,32,768]{2,1,0:T(8,128)(2,1)S(1)} %get-tuple-element.100), channel_id=1, source_target_pairs={{0,5},{1,4},{2,7},{3,6},{4,1},{5,0},{6,3},{7,2},{8,13},{9,12},{10,... | collective-permute-start | bytes 294920 | tf_op jit(solution)/shard_map/ppermute | solution.py:247
  114.1 2.1 %collective-permute-start.21 = (bf16[2,32,768]{2,1,0:T(8,128)(2,1)S(1)}, bf16[2,32,768]{2,1,0:T(8,128)(2,1)S(1)}, u32[]{:S(2)}, u32[]{:S(2)}) collective-permute-start(bf16[2,32,768]{2,1,0:T(8,128)(2,1)S(1)} %get-tuple-element.101), channel_id=1, source_target_pairs={{0,6},{1,7},{2,4},{3,5},{4,2},{5,3},{6,0},{7,1},{8,14},{9,15},{10,... | collective-permute-start | bytes 294920 | tf_op jit(solution)/shard_map/ppermute | solution.py:247
  116.1 2.2 %collective-permute-start.22 = (bf16[2,32,768]{2,1,0:T(8,128)(2,1)S(1)}, bf16[2,32,768]{2,1,0:T(8,128)(2,1)S(1)}, u32[]{:S(2)}, u32[]{:S(2)}) collective-permute-start(bf16[2,32,768]{2,1,0:T(8,128)(2,1)S(1)} %get-tuple-element.102), channel_id=1, source_target_pairs={{0,7},{1,6},{2,5},{3,4},{4,3},{5,2},{6,1},{7,0},{8,15},{9,14},{10,... | collective-permute-start | bytes 294920 | tf_op jit(solution)/shard_map/ppermute | solution.py:247
  118.4 2.3 %collective-permute-done.19.refs_4_ = bf16[2,32,768]{2,1,0:T(8,128)(2,1)S(1)} collective-permute-done((bf16[2,32,768]{2,1,0:T(8,128)(2,1)S(1)}, bf16[2,32,768]{2,1,0:T(8,128)(2,1)S(1)}, u32[]{:S(2)}, u32[]{:S(2)}) %collective-permute-start.19) | collective-permute-done | bytes 98336 | tf_op jit(solution)/shard_map/ppermute | solution.py:247
  120.7 3.4 %collective-permute-done.20.refs_5_ = bf16[2,32,768]{2,1,0:T(8,128)(2,1)S(1)} collective-permute-done((bf16[2,32,768]{2,1,0:T(8,128)(2,1)S(1)}, bf16[2,32,768]{2,1,0:T(8,128)(2,1)S(1)}, u32[]{:S(2)}, u32[]{:S(2)}) %collective-permute-start.20) | collective-permute-done | bytes 98336 | tf_op jit(solution)/shard_map/ppermute | solution.py:247
  124.2 1.7 %collective-permute-start.24 = (bf16[8,2,32,128]{3,2,1,0:T(8,128)(2,1)S(1)}, bf16[8,2,32,128]{3,2,1,0:T(8,128)(2,1)S(1)}, u32[]{:S(2)}, u32[]{:S(2)}) collective-permute-start(bf16[8,2,32,128]{3,2,1,0:T(8,128)(2,1)S(1)} %get-tuple-element.104), channel_id=1, source_target_pairs={{8,0},{16,8},{24,16},{0,24},{9,1},{17,9},{25,17},{1,25},{10,2},{18... | collective-permute-start | bytes 393224 | tf_op jit(solution)/shard_map/ppermute | solution.py:304
  126.0 1.8 %shard_map.67 = (bf16[2,32,768]{2,1,0:T(8,128)(2,1)S(1)}, bf16[2,32,768]{2,1,0:T(8,128)(2,1)S(1)}, bf16[2,32,768]{2,1,0:T(8,128)(2,1)S(1)}, bf16[2,32,768]{2,1,0...) custom-call(bf16[2,32,768]{2,1,0:T(8,128)(2,1)S(1)} %get-tuple-eleme, ...), custom_call_target="tpu_custom_call" | custom-call | flops 1207959552 | bytes 1048576 | tf_op jit(solution)/shard_map/pallas_call | solution.py:305
  128.5 1.2 collective-permute-start.57
  129.7 3.6 %collective-permute-start.58 = (bf16[2,32,768]{2,1,0:T(8,128)(2,1)S(1)}, bf16[2,32,768]{2,1,0:T(8,128)(2,1)S(1)}, u32[]{:S(2)}, u32[]{:S(2)}) collective-permute-start(bf16[2,32,768]{2,1,0:T(8,128)(2,1)S(1)} %get-tuple-element.143), channel_id=1, source_target_pairs={{0,2},{1,3},{2,0},{3,1},{4,6},{5,7},{6,4},{7,5},{8,10},{9,11},{10,... | collective-permute-start | bytes 294920 | tf_op jit(solution)/shard_map/ppermute | solution.py:247
  133.6 2.5 %collective-permute-start.60 = (bf16[2,32,768]{2,1,0:T(8,128)(2,1)S(1)}, bf16[2,32,768]{2,1,0:T(8,128)(2,1)S(1)}, u32[]{:S(2)}, u32[]{:S(2)}) collective-permute-start(bf16[2,32,768]{2,1,0:T(8,128)(2,1)S(1)} %get-tuple-element.145), channel_id=1, source_target_pairs={{0,4},{1,5},{2,6},{3,7},{4,0},{5,1},{6,2},{7,3},{8,12},{9,13},{10,... | collective-permute-start | bytes 294920 | tf_op jit(solution)/shard_map/ppermute | solution.py:247
  137.2 1.8 %shard_map.61 = (bf16[2,32,768]{2,1,0:T(8,128)(2,1)S(1)}, bf16[2,32,768]{2,1,0:T(8,128)(2,1)S(1)}, bf16[2,32,768]{2,1,0:T(8,128)(2,1)S(1)}, bf16[2,32,768]{2,1,0...) custom-call(bf16[2,32,768]{2,1,0:T(8,128)(2,1)S(1)} %get-tuple-eleme, ...), custom_call_target="tpu_custom_call" | custom-call | flops 1207959552 | bytes 1048576 | tf_op jit(solution)/shard_map/pallas_call | solution.py:305
  139.7 1.9 %collective-permute-start.62 = (bf16[2,32,768]{2,1,0:T(8,128)(2,1)S(1)}, bf16[2,32,768]{2,1,0:T(8,128)(2,1)S(1)}, u32[]{:S(2)}, u32[]{:S(2)}) collective-permute-start(bf16[2,32,768]{2,1,0:T(8,128)(2,1)S(1)} %get-tuple-element.147), channel_id=1, source_target_pairs={{0,6},{1,7},{2,4},{3,5},{4,2},{5,3},{6,0},{7,1},{8,14},{9,15},{10,... | collective-permute-start | bytes 294920 | tf_op jit(solution)/shard_map/ppermute | solution.py:247
  141.5 2.2 %collective-permute-start.63 = (bf16[2,32,768]{2,1,0:T(8,128)(2,1)S(1)}, bf16[2,32,768]{2,1,0:T(8,128)(2,1)S(1)}, u32[]{:S(2)}, u32[]{:S(2)}) collective-permute-start(bf16[2,32,768]{2,1,0:T(8,128)(2,1)S(1)} %get-tuple-element.148), channel_id=1, source_target_pairs={{0,7},{1,6},{2,5},{3,4},{4,3},{5,2},{6,1},{7,0},{8,15},{9,14},{10,... | collective-permute-start | bytes 294920 | tf_op jit(solution)/shard_map/ppermute | solution.py:247
  143.8 1.2 collective-permute-start.25
  144.9 1.9 %collective-permute-done.60.refs_12_ = bf16[2,32,768]{2,1,0:T(8,128)(2,1)S(1)} collective-permute-done((bf16[2,32,768]{2,1,0:T(8,128)(2,1)S(1)}, bf16[2,32,768]{2,1,0:T(8,128)(2,1)S(1)}, u32[]{:S(2)}, u32[]{:S(2)}) %collective-permute-start.60) | collective-permute-done | bytes 98336 | tf_op jit(solution)/shard_map/ppermute | solution.py:247
  146.8 3.9 %collective-permute-done.61.refs_13_ = bf16[2,32,768]{2,1,0:T(8,128)(2,1)S(1)} collective-permute-done((bf16[2,32,768]{2,1,0:T(8,128)(2,1)S(1)}, bf16[2,32,768]{2,1,0:T(8,128)(2,1)S(1)}, u32[]{:S(2)}, u32[]{:S(2)}) %collective-permute-start.61) | collective-permute-done | bytes 98336 | tf_op jit(solution)/shard_map/ppermute | solution.py:247
  150.7 2.8 %collective-permute-start.28 = (bf16[2,32,768]{2,1,0:T(8,128)(2,1)S(1)}, bf16[2,32,768]{2,1,0:T(8,128)(2,1)S(1)}, u32[]{:S(2)}, u32[]{:S(2)}) collective-permute-start(bf16[2,32,768]{2,1,0:T(8,128)(2,1)S(1)} %get-tuple-element.109), channel_id=1, source_target_pairs={{0,4},{1,5},{2,6},{3,7},{4,0},{5,1},{6,2},{7,3},{8,12},{9,13},{10,... | collective-permute-start | bytes 294920 | tf_op jit(solution)/shard_map/ppermute | solution.py:247
  153.6 3.8 %collective-permute-start.29 = (bf16[2,32,768]{2,1,0:T(8,128)(2,1)S(1)}, bf16[2,32,768]{2,1,0:T(8,128)(2,1)S(1)}, u32[]{:S(2)}, u32[]{:S(2)}) collective-permute-start(bf16[2,32,768]{2,1,0:T(8,128)(2,1)S(1)} %get-tuple-element.110), channel_id=1, source_target_pairs={{0,5},{1,4},{2,7},{3,6},{4,1},{5,0},{6,3},{7,2},{8,13},{9,12},{10,... | collective-permute-start | bytes 294920 | tf_op jit(solution)/shard_map/ppermute | solution.py:247
  157.4 1.9 %collective-permute-start.30 = (bf16[2,32,768]{2,1,0:T(8,128)(2,1)S(1)}, bf16[2,32,768]{2,1,0:T(8,128)(2,1)S(1)}, u32[]{:S(2)}, u32[]{:S(2)}) collective-permute-start(bf16[2,32,768]{2,1,0:T(8,128)(2,1)S(1)} %get-tuple-element.111), channel_id=1, source_target_pairs={{0,6},{1,7},{2,4},{3,5},{4,2},{5,3},{6,0},{7,1},{8,14},{9,15},{10,... | collective-permute-start | bytes 294920 | tf_op jit(solution)/shard_map/ppermute | solution.py:247
  159.3 2.4 %collective-permute-start.31 = (bf16[2,32,768]{2,1,0:T(8,128)(2,1)S(1)}, bf16[2,32,768]{2,1,0:T(8,128)(2,1)S(1)}, u32[]{:S(2)}, u32[]{:S(2)}) collective-permute-start(bf16[2,32,768]{2,1,0:T(8,128)(2,1)S(1)} %get-tuple-element.112), channel_id=1, source_target_pairs={{0,7},{1,6},{2,5},{3,4},{4,3},{5,2},{6,1},{7,0},{8,15},{9,14},{10,... | collective-permute-start | bytes 294920 | tf_op jit(solution)/shard_map/ppermute | solution.py:247
  161.7 1.1 collective-permute-done.28.refs_4_
  162.8 4.7 %collective-permute-done.29.refs_5_ = bf16[2,32,768]{2,1,0:T(8,128)(2,1)S(1)} collective-permute-done((bf16[2,32,768]{2,1,0:T(8,128)(2,1)S(1)}, bf16[2,32,768]{2,1,0:T(8,128)(2,1)S(1)}, u32[]{:S(2)}, u32[]{:S(2)}) %collective-permute-start.29) | collective-permute-done | bytes 98336 | tf_op jit(solution)/shard_map/ppermute | solution.py:247
  168.3 2.7 %shard_map.68 = bf16[2,512,768]{2,1,0:T(8,128)(2,1)} custom-call(bf16[2,32,768]{2,1,0:T(8,128)(2,1)} %copy-done.6, bf16[2,32,768]{2,1,0:T(8,128)(2,1)} %copy-done.16, bf16[2,32,768]{2,1,0:T(8,128)(2,1)} %copy-done.17, bf16[2,32,768]{2,1,0:T(8,128)(2,1)} %copy-done.18, bf16[2,32,768]{2,1,0:T(8,128)(2,1)} %copy-done.19, bf16[2,32,768]{2,1,0:T(8,128)(2,1)} %copy-done.20, ...), custom_call_target="tpu_custom_call" | custom-call | tf_op jit(solution)/shard_map/pallas_call | solution.py:312
  (127 shorter events, 10.1 us)
Async XLA Ops:
  5.9 8.9 %collective-permute-start.32 = (bf16[2,32,768]{2,1,0:T(8,128)(2,1)S(1)}, bf16[2,32,768]{2,1,0:T(8,128)(2,1)S(1)}, u32[]{:S(2)}, u32[]{:S(2)}) collective-permute-start(bf16[2,32,768]{2,1,0:T(8,128)(2,1)S(1)} %get-tuple-element.114), channel_id=1, source_target_pairs={{0,1},{1,0},{2,3},{3,2},{4,5},{5,4},{6,7},{7,6},{8,9},{9,8},{10,11... | collective-permute-start | bytes 294920 | tf_op jit(solution)/shard_map/ppermute | solution.py:247
  8.9 9.5 %collective-permute-start.33 = (bf16[2,32,768]{2,1,0:T(8,128)(2,1)S(1)}, bf16[2,32,768]{2,1,0:T(8,128)(2,1)S(1)}, u32[]{:S(2)}, u32[]{:S(2)}) collective-permute-start(bf16[2,32,768]{2,1,0:T(8,128)(2,1)S(1)} %get-tuple-element.115), channel_id=1, source_target_pairs={{0,2},{1,3},{2,0},{3,1},{4,6},{5,7},{6,4},{7,5},{8,10},{9,11},{10,... | collective-permute-start | bytes 294920 | tf_op jit(solution)/shard_map/ppermute | solution.py:247
  10.5 9.3 %collective-permute-start.34 = (bf16[2,32,768]{2,1,0:T(8,128)(2,1)S(1)}, bf16[2,32,768]{2,1,0:T(8,128)(2,1)S(1)}, u32[]{:S(2)}, u32[]{:S(2)}) collective-permute-start(bf16[2,32,768]{2,1,0:T(8,128)(2,1)S(1)} %get-tuple-element.116), channel_id=1, source_target_pairs={{0,3},{1,2},{2,1},{3,0},{4,7},{5,6},{6,5},{7,4},{8,11},{9,10},{10,... | collective-permute-start | bytes 294920 | tf_op jit(solution)/shard_map/ppermute | solution.py:247
  10.5 11.4 %collective-permute-start.35 = (bf16[2,32,768]{2,1,0:T(8,128)(2,1)S(1)}, bf16[2,32,768]{2,1,0:T(8,128)(2,1)S(1)}, u32[]{:S(2)}, u32[]{:S(2)}) collective-permute-start(bf16[2,32,768]{2,1,0:T(8,128)(2,1)S(1)} %get-tuple-element.117), channel_id=1, source_target_pairs={{0,4},{1,5},{2,6},{3,7},{4,0},{5,1},{6,2},{7,3},{8,12},{9,13},{10,... | collective-permute-start | bytes 294920 | tf_op jit(solution)/shard_map/ppermute | solution.py:247
  13.5 15.2 %collective-permute-start.36 = (bf16[2,32,768]{2,1,0:T(8,128)(2,1)S(1)}, bf16[2,32,768]{2,1,0:T(8,128)(2,1)S(1)}, u32[]{:S(2)}, u32[]{:S(2)}) collective-permute-start(bf16[2,32,768]{2,1,0:T(8,128)(2,1)S(1)} %get-tuple-element.118), channel_id=1, source_target_pairs={{0,5},{1,4},{2,7},{3,6},{4,1},{5,0},{6,3},{7,2},{8,13},{9,12},{10,... | collective-permute-start | bytes 294920 | tf_op jit(solution)/shard_map/ppermute | solution.py:247
  14.8 14.0 %collective-permute-start.37 = (bf16[2,32,768]{2,1,0:T(8,128)(2,1)S(1)}, bf16[2,32,768]{2,1,0:T(8,128)(2,1)S(1)}, u32[]{:S(2)}, u32[]{:S(2)}) collective-permute-start(bf16[2,32,768]{2,1,0:T(8,128)(2,1)S(1)} %get-tuple-element.119), channel_id=1, source_target_pairs={{0,6},{1,7},{2,4},{3,5},{4,2},{5,3},{6,0},{7,1},{8,14},{9,15},{10,... | collective-permute-start | bytes 294920 | tf_op jit(solution)/shard_map/ppermute | solution.py:247
  18.4 13.9 %collective-permute-start.38 = (bf16[2,32,768]{2,1,0:T(8,128)(2,1)S(1)}, bf16[2,32,768]{2,1,0:T(8,128)(2,1)S(1)}, u32[]{:S(2)}, u32[]{:S(2)}) collective-permute-start(bf16[2,32,768]{2,1,0:T(8,128)(2,1)S(1)} %get-tuple-element.120), channel_id=1, source_target_pairs={{0,7},{1,6},{2,5},{3,4},{4,3},{5,2},{6,1},{7,0},{8,15},{9,14},{10,... | collective-permute-start | bytes 294920 | tf_op jit(solution)/shard_map/ppermute | solution.py:247
  19.8 15.4 %collective-permute-start = (bf16[2,32,768]{2,1,0:T(8,128)(2,1)S(1)}, bf16[2,32,768]{2,1,0:T(8,128)(2,1)S(1)}, u32[]{:S(2)}, u32[]{:S(2)}) collective-permute-start(bf16[2,32,768]{2,1,0:T(8,128)(2,1)S(1)} %get-tuple-element.78), channel_id=1, source_target_pairs={{0,1},{1,0},{2,3},{3,2},{4,5},{5,4},{6,7},{7,6},{8,9},{9,8},{10,11... | collective-permute-start | bytes 294920 | tf_op jit(solution)/shard_map/ppermute | solution.py:247
  21.9 14.1 %collective-permute-start.1 = (bf16[2,32,768]{2,1,0:T(8,128)(2,1)S(1)}, bf16[2,32,768]{2,1,0:T(8,128)(2,1)S(1)}, u32[]{:S(2)}, u32[]{:S(2)}) collective-permute-start(bf16[2,32,768]{2,1,0:T(8,128)(2,1)S(1)} %get-tuple-element.79), channel_id=1, source_target_pairs={{0,2},{1,3},{2,0},{3,1},{4,6},{5,7},{6,4},{7,5},{8,10},{9,11},{10,... | collective-permute-start | bytes 294920 | tf_op jit(solution)/shard_map/ppermute | solution.py:247
  28.7 11.9 %collective-permute-start.2 = (bf16[2,32,768]{2,1,0:T(8,128)(2,1)S(1)}, bf16[2,32,768]{2,1,0:T(8,128)(2,1)S(1)}, u32[]{:S(2)}, u32[]{:S(2)}) collective-permute-start(bf16[2,32,768]{2,1,0:T(8,128)(2,1)S(1)} %get-tuple-element.80), channel_id=1, source_target_pairs={{0,3},{1,2},{2,1},{3,0},{4,7},{5,6},{6,5},{7,4},{8,11},{9,10},{10,... | collective-permute-start | bytes 294920 | tf_op jit(solution)/shard_map/ppermute | solution.py:247
  28.8 13.1 %collective-permute-start.3 = (bf16[2,32,768]{2,1,0:T(8,128)(2,1)S(1)}, bf16[2,32,768]{2,1,0:T(8,128)(2,1)S(1)}, u32[]{:S(2)}, u32[]{:S(2)}) collective-permute-start(bf16[2,32,768]{2,1,0:T(8,128)(2,1)S(1)} %get-tuple-element.81), channel_id=1, source_target_pairs={{0,4},{1,5},{2,6},{3,7},{4,0},{5,1},{6,2},{7,3},{8,12},{9,13},{10,... | collective-permute-start | bytes 294920 | tf_op jit(solution)/shard_map/ppermute | solution.py:247
  32.3 13.8 %collective-permute-start.4 = (bf16[2,32,768]{2,1,0:T(8,128)(2,1)S(1)}, bf16[2,32,768]{2,1,0:T(8,128)(2,1)S(1)}, u32[]{:S(2)}, u32[]{:S(2)}) collective-permute-start(bf16[2,32,768]{2,1,0:T(8,128)(2,1)S(1)} %get-tuple-element.82), channel_id=1, source_target_pairs={{0,5},{1,4},{2,7},{3,6},{4,1},{5,0},{6,3},{7,2},{8,13},{9,12},{10,... | collective-permute-start | bytes 294920 | tf_op jit(solution)/shard_map/ppermute | solution.py:247
  35.2 10.9 %collective-permute-start.5 = (bf16[2,32,768]{2,1,0:T(8,128)(2,1)S(1)}, bf16[2,32,768]{2,1,0:T(8,128)(2,1)S(1)}, u32[]{:S(2)}, u32[]{:S(2)}) collective-permute-start(bf16[2,32,768]{2,1,0:T(8,128)(2,1)S(1)} %get-tuple-element.83), channel_id=1, source_target_pairs={{0,6},{1,7},{2,4},{3,5},{4,2},{5,3},{6,0},{7,1},{8,14},{9,15},{10,... | collective-permute-start | bytes 294920 | tf_op jit(solution)/shard_map/ppermute | solution.py:247
  36.0 10.2 %collective-permute-start.6 = (bf16[2,32,768]{2,1,0:T(8,128)(2,1)S(1)}, bf16[2,32,768]{2,1,0:T(8,128)(2,1)S(1)}, u32[]{:S(2)}, u32[]{:S(2)}) collective-permute-start(bf16[2,32,768]{2,1,0:T(8,128)(2,1)S(1)} %get-tuple-element.84), channel_id=1, source_target_pairs={{0,7},{1,6},{2,5},{3,4},{4,3},{5,2},{6,1},{7,0},{8,15},{9,14},{10,... | collective-permute-start | bytes 294920 | tf_op jit(solution)/shard_map/ppermute | solution.py:247
  40.6 7.3 %collective-permute-start.39 = (bf16[8,2,32,128]{3,2,1,0:T(8,128)(2,1)S(1)}, bf16[8,2,32,128]{3,2,1,0:T(8,128)(2,1)S(1)}, u32[]{:S(2)}, u32[]{:S(2)}) collective-permute-start(bf16[8,2,32,128]{3,2,1,0:T(8,128)(2,1)S(1)} %get-tuple-element.121), channel_id=1, source_target_pairs={{0,8},{8,16},{16,24},{24,0},{1,9},{9,17},{17,25},{25,1},{2,10},{10... | collective-permute-start | bytes 393224 | tf_op jit(solution)/shard_map/ppermute | solution.py:303
  41.9 6.1 %collective-permute-start.40 = (bf16[8,2,32,128]{3,2,1,0:T(8,128)(2,1)S(1)}, bf16[8,2,32,128]{3,2,1,0:T(8,128)(2,1)S(1)}, u32[]{:S(2)}, u32[]{:S(2)}) collective-permute-start(bf16[8,2,32,128]{3,2,1,0:T(8,128)(2,1)S(1)} %get-tuple-element.122), channel_id=1, source_target_pairs={{8,0},{16,8},{24,16},{0,24},{9,1},{17,9},{25,17},{1,25},{10,2},{18... | collective-permute-start | bytes 393224 | tf_op jit(solution)/shard_map/ppermute | solution.py:304
  46.2 9.4 %collective-permute-start.7 = (bf16[8,2,32,128]{3,2,1,0:T(8,128)(2,1)S(1)}, bf16[8,2,32,128]{3,2,1,0:T(8,128)(2,1)S(1)}, u32[]{:S(2)}, u32[]{:S(2)}) collective-permute-start(bf16[8,2,32,128]{3,2,1,0:T(8,128)(2,1)S(1)} %get-tuple-element.85), channel_id=1, source_target_pairs={{0,8},{8,16},{16,24},{24,0},{1,9},{9,17},{17,25},{25,1},{2,10},{10... | collective-permute-start | bytes 393224 | tf_op jit(solution)/shard_map/ppermute | solution.py:303
  46.2 12.5 %collective-permute-start.8 = (bf16[8,2,32,128]{3,2,1,0:T(8,128)(2,1)S(1)}, bf16[8,2,32,128]{3,2,1,0:T(8,128)(2,1)S(1)}, u32[]{:S(2)}, u32[]{:S(2)}) collective-permute-start(bf16[8,2,32,128]{3,2,1,0:T(8,128)(2,1)S(1)} %get-tuple-element.86), channel_id=1, source_target_pairs={{8,0},{16,8},{24,16},{0,24},{9,1},{17,9},{25,17},{1,25},{10,2},{18... | collective-permute-start | bytes 393224 | tf_op jit(solution)/shard_map/ppermute | solution.py:304
  50.6 8.4 %collective-permute-start.41 = (bf16[2,32,768]{2,1,0:T(8,128)(2,1)S(1)}, bf16[2,32,768]{2,1,0:T(8,128)(2,1)S(1)}, u32[]{:S(2)}, u32[]{:S(2)}) collective-permute-start(bf16[2,32,768]{2,1,0:T(8,128)(2,1)S(1)} %get-tuple-element.124), channel_id=1, source_target_pairs={{0,1},{1,0},{2,3},{3,2},{4,5},{5,4},{6,7},{7,6},{8,9},{9,8},{10,11... | collective-permute-start | bytes 294920 | tf_op jit(solution)/shard_map/ppermute | solution.py:247
  51.0 10.1 %collective-permute-start.42 = (bf16[2,32,768]{2,1,0:T(8,128)(2,1)S(1)}, bf16[2,32,768]{2,1,0:T(8,128)(2,1)S(1)}, u32[]{:S(2)}, u32[]{:S(2)}) collective-permute-start(bf16[2,32,768]{2,1,0:T(8,128)(2,1)S(1)} %get-tuple-element.125), channel_id=1, source_target_pairs={{0,2},{1,3},{2,0},{3,1},{4,6},{5,7},{6,4},{7,5},{8,10},{9,11},{10,... | collective-permute-start | bytes 294920 | tf_op jit(solution)/shard_map/ppermute | solution.py:247
  55.1 10.3 %collective-permute-start.43 = (bf16[2,32,768]{2,1,0:T(8,128)(2,1)S(1)}, bf16[2,32,768]{2,1,0:T(8,128)(2,1)S(1)}, u32[]{:S(2)}, u32[]{:S(2)}) collective-permute-start(bf16[2,32,768]{2,1,0:T(8,128)(2,1)S(1)} %get-tuple-element.126), channel_id=1, source_target_pairs={{0,3},{1,2},{2,1},{3,0},{4,7},{5,6},{6,5},{7,4},{8,11},{9,10},{10,... | collective-permute-start | bytes 294920 | tf_op jit(solution)/shard_map/ppermute | solution.py:247
  55.6 14.0 %collective-permute-start.44 = (bf16[2,32,768]{2,1,0:T(8,128)(2,1)S(1)}, bf16[2,32,768]{2,1,0:T(8,128)(2,1)S(1)}, u32[]{:S(2)}, u32[]{:S(2)}) collective-permute-start(bf16[2,32,768]{2,1,0:T(8,128)(2,1)S(1)} %get-tuple-element.127), channel_id=1, source_target_pairs={{0,4},{1,5},{2,6},{3,7},{4,0},{5,1},{6,2},{7,3},{8,12},{9,13},{10,... | collective-permute-start | bytes 294920 | tf_op jit(solution)/shard_map/ppermute | solution.py:247
  58.7 14.5 %collective-permute-start.45 = (bf16[2,32,768]{2,1,0:T(8,128)(2,1)S(1)}, bf16[2,32,768]{2,1,0:T(8,128)(2,1)S(1)}, u32[]{:S(2)}, u32[]{:S(2)}) collective-permute-start(bf16[2,32,768]{2,1,0:T(8,128)(2,1)S(1)} %get-tuple-element.128), channel_id=1, source_target_pairs={{0,5},{1,4},{2,7},{3,6},{4,1},{5,0},{6,3},{7,2},{8,13},{9,12},{10,... | collective-permute-start | bytes 294920 | tf_op jit(solution)/shard_map/ppermute | solution.py:247
  58.9 14.3 %collective-permute-start.46 = (bf16[2,32,768]{2,1,0:T(8,128)(2,1)S(1)}, bf16[2,32,768]{2,1,0:T(8,128)(2,1)S(1)}, u32[]{:S(2)}, u32[]{:S(2)}) collective-permute-start(bf16[2,32,768]{2,1,0:T(8,128)(2,1)S(1)} %get-tuple-element.129), channel_id=1, source_target_pairs={{0,6},{1,7},{2,4},{3,5},{4,2},{5,3},{6,0},{7,1},{8,14},{9,15},{10,... | collective-permute-start | bytes 294920 | tf_op jit(solution)/shard_map/ppermute | solution.py:247
  61.1 15.4 %collective-permute-start.47 = (bf16[2,32,768]{2,1,0:T(8,128)(2,1)S(1)}, bf16[2,32,768]{2,1,0:T(8,128)(2,1)S(1)}, u32[]{:S(2)}, u32[]{:S(2)}) collective-permute-start(bf16[2,32,768]{2,1,0:T(8,128)(2,1)S(1)} %get-tuple-element.130), channel_id=1, source_target_pairs={{0,7},{1,6},{2,5},{3,4},{4,3},{5,2},{6,1},{7,0},{8,15},{9,14},{10,... | collective-permute-start | bytes 294920 | tf_op jit(solution)/shard_map/ppermute | solution.py:247
  65.4 16.1 %collective-permute-start.9 = (bf16[2,32,768]{2,1,0:T(8,128)(2,1)S(1)}, bf16[2,32,768]{2,1,0:T(8,128)(2,1)S(1)}, u32[]{:S(2)}, u32[]{:S(2)}) collective-permute-start(bf16[2,32,768]{2,1,0:T(8,128)(2,1)S(1)} %get-tuple-element.88), channel_id=1, source_target_pairs={{0,1},{1,0},{2,3},{3,2},{4,5},{5,4},{6,7},{7,6},{8,9},{9,8},{10,11... | collective-permute-start | bytes 294920 | tf_op jit(solution)/shard_map/ppermute | solution.py:247
  69.5 12.6 %collective-permute-start.10 = (bf16[2,32,768]{2,1,0:T(8,128)(2,1)S(1)}, bf16[2,32,768]{2,1,0:T(8,128)(2,1)S(1)}, u32[]{:S(2)}, u32[]{:S(2)}) collective-permute-start(bf16[2,32,768]{2,1,0:T(8,128)(2,1)S(1)} %get-tuple-element.89), channel_id=1, source_target_pairs={{0,2},{1,3},{2,0},{3,1},{4,6},{5,7},{6,4},{7,5},{8,10},{9,11},{10,... | collective-permute-start | bytes 294920 | tf_op jit(solution)/shard_map/ppermute | solution.py:247
  73.2 11.5 %collective-permute-start.11 = (bf16[2,32,768]{2,1,0:T(8,128)(2,1)S(1)}, bf16[2,32,768]{2,1,0:T(8,128)(2,1)S(1)}, u32[]{:S(2)}, u32[]{:S(2)}) collective-permute-start(bf16[2,32,768]{2,1,0:T(8,128)(2,1)S(1)} %get-tuple-element.90), channel_id=1, source_target_pairs={{0,3},{1,2},{2,1},{3,0},{4,7},{5,6},{6,5},{7,4},{8,11},{9,10},{10,... | collective-permute-start | bytes 294920 | tf_op jit(solution)/shard_map/ppermute | solution.py:247
  73.2 13.6 %collective-permute-start.12 = (bf16[2,32,768]{2,1,0:T(8,128)(2,1)S(1)}, bf16[2,32,768]{2,1,0:T(8,128)(2,1)S(1)}, u32[]{:S(2)}, u32[]{:S(2)}) collective-permute-start(bf16[2,32,768]{2,1,0:T(8,128)(2,1)S(1)} %get-tuple-element.91), channel_id=1, source_target_pairs={{0,4},{1,5},{2,6},{3,7},{4,0},{5,1},{6,2},{7,3},{8,12},{9,13},{10,... | collective-permute-start | bytes 294920 | tf_op jit(solution)/shard_map/ppermute | solution.py:247
  76.6 12.2 %collective-permute-start.13 = (bf16[2,32,768]{2,1,0:T(8,128)(2,1)S(1)}, bf16[2,32,768]{2,1,0:T(8,128)(2,1)S(1)}, u32[]{:S(2)}, u32[]{:S(2)}) collective-permute-start(bf16[2,32,768]{2,1,0:T(8,128)(2,1)S(1)} %get-tuple-element.92), channel_id=1, source_target_pairs={{0,5},{1,4},{2,7},{3,6},{4,1},{5,0},{6,3},{7,2},{8,13},{9,12},{10,... | collective-permute-start | bytes 294920 | tf_op jit(solution)/shard_map/ppermute | solution.py:247
  81.5 7.2 %collective-permute-start.14 = (bf16[2,32,768]{2,1,0:T(8,128)(2,1)S(1)}, bf16[2,32,768]{2,1,0:T(8,128)(2,1)S(1)}, u32[]{:S(2)}, u32[]{:S(2)}) collective-permute-start(bf16[2,32,768]{2,1,0:T(8,128)(2,1)S(1)} %get-tuple-element.93), channel_id=1, source_target_pairs={{0,6},{1,7},{2,4},{3,5},{4,2},{5,3},{6,0},{7,1},{8,14},{9,15},{10,... | collective-permute-start | bytes 294920 | tf_op jit(solution)/shard_map/ppermute | solution.py:247
  82.1 11.0 %collective-permute-start.15 = (bf16[2,32,768]{2,1,0:T(8,128)(2,1)S(1)}, bf16[2,32,768]{2,1,0:T(8,128)(2,1)S(1)}, u32[]{:S(2)}, u32[]{:S(2)}) collective-permute-start(bf16[2,32,768]{2,1,0:T(8,128)(2,1)S(1)} %get-tuple-element.94), channel_id=1, source_target_pairs={{0,7},{1,6},{2,5},{3,4},{4,3},{5,2},{6,1},{7,0},{8,15},{9,14},{10,... | collective-permute-start | bytes 294920 | tf_op jit(solution)/shard_map/ppermute | solution.py:247
  84.7 12.4 %collective-permute-start.48 = (bf16[2,32,768]{2,1,0:T(8,128)(2,1)S(1)}, bf16[2,32,768]{2,1,0:T(8,128)(2,1)S(1)}, u32[]{:S(2)}, u32[]{:S(2)}) collective-permute-start(bf16[2,32,768]{2,1,0:T(8,128)(2,1)S(1)} %get-tuple-element.132), channel_id=1, source_target_pairs={{0,1},{1,0},{2,3},{3,2},{4,5},{5,4},{6,7},{7,6},{8,9},{9,8},{10,11... | collective-permute-start | bytes 294920 | tf_op jit(solution)/shard_map/ppermute | solution.py:247
  86.9 13.8 %collective-permute-start.49 = (bf16[2,32,768]{2,1,0:T(8,128)(2,1)S(1)}, bf16[2,32,768]{2,1,0:T(8,128)(2,1)S(1)}, u32[]{:S(2)}, u32[]{:S(2)}) collective-permute-start(bf16[2,32,768]{2,1,0:T(8,128)(2,1)S(1)} %get-tuple-element.133), channel_id=1, source_target_pairs={{0,2},{1,3},{2,0},{3,1},{4,6},{5,7},{6,4},{7,5},{8,10},{9,11},{10,... | collective-permute-start | bytes 294920 | tf_op jit(solution)/shard_map/ppermute | solution.py:247
  88.7 14.2 %collective-permute-start.50 = (bf16[2,32,768]{2,1,0:T(8,128)(2,1)S(1)}, bf16[2,32,768]{2,1,0:T(8,128)(2,1)S(1)}, u32[]{:S(2)}, u32[]{:S(2)}) collective-permute-start(bf16[2,32,768]{2,1,0:T(8,128)(2,1)S(1)} %get-tuple-element.134), channel_id=1, source_target_pairs={{0,3},{1,2},{2,1},{3,0},{4,7},{5,6},{6,5},{7,4},{8,11},{9,10},{10,... | collective-permute-start | bytes 294920 | tf_op jit(solution)/shard_map/ppermute | solution.py:247
  88.7 15.2 %collective-permute-start.51 = (bf16[2,32,768]{2,1,0:T(8,128)(2,1)S(1)}, bf16[2,32,768]{2,1,0:T(8,128)(2,1)S(1)}, u32[]{:S(2)}, u32[]{:S(2)}) collective-permute-start(bf16[2,32,768]{2,1,0:T(8,128)(2,1)S(1)} %get-tuple-element.135), channel_id=1, source_target_pairs={{0,4},{1,5},{2,6},{3,7},{4,0},{5,1},{6,2},{7,3},{8,12},{9,13},{10,... | collective-permute-start | bytes 294920 | tf_op jit(solution)/shard_map/ppermute | solution.py:247
  93.1 13.1 %collective-permute-start.52 = (bf16[2,32,768]{2,1,0:T(8,128)(2,1)S(1)}, bf16[2,32,768]{2,1,0:T(8,128)(2,1)S(1)}, u32[]{:S(2)}, u32[]{:S(2)}) collective-permute-start(bf16[2,32,768]{2,1,0:T(8,128)(2,1)S(1)} %get-tuple-element.136), channel_id=1, source_target_pairs={{0,5},{1,4},{2,7},{3,6},{4,1},{5,0},{6,3},{7,2},{8,13},{9,12},{10,... | collective-permute-start | bytes 294920 | tf_op jit(solution)/shard_map/ppermute | solution.py:247
  97.2 9.3 %collective-permute-start.53 = (bf16[2,32,768]{2,1,0:T(8,128)(2,1)S(1)}, bf16[2,32,768]{2,1,0:T(8,128)(2,1)S(1)}, u32[]{:S(2)}, u32[]{:S(2)}) collective-permute-start(bf16[2,32,768]{2,1,0:T(8,128)(2,1)S(1)} %get-tuple-element.137), channel_id=1, source_target_pairs={{0,6},{1,7},{2,4},{3,5},{4,2},{5,3},{6,0},{7,1},{8,14},{9,15},{10,... | collective-permute-start | bytes 294920 | tf_op jit(solution)/shard_map/ppermute | solution.py:247
  100.7 9.3 %collective-permute-start.54 = (bf16[2,32,768]{2,1,0:T(8,128)(2,1)S(1)}, bf16[2,32,768]{2,1,0:T(8,128)(2,1)S(1)}, u32[]{:S(2)}, u32[]{:S(2)}) collective-permute-start(bf16[2,32,768]{2,1,0:T(8,128)(2,1)S(1)} %get-tuple-element.138), channel_id=1, source_target_pairs={{0,7},{1,6},{2,5},{3,4},{4,3},{5,2},{6,1},{7,0},{8,15},{9,14},{10,... | collective-permute-start | bytes 294920 | tf_op jit(solution)/shard_map/ppermute | solution.py:247
  103.0 11.1 %collective-permute-start.16 = (bf16[2,32,768]{2,1,0:T(8,128)(2,1)S(1)}, bf16[2,32,768]{2,1,0:T(8,128)(2,1)S(1)}, u32[]{:S(2)}, u32[]{:S(2)}) collective-permute-start(bf16[2,32,768]{2,1,0:T(8,128)(2,1)S(1)} %get-tuple-element.96), channel_id=1, source_target_pairs={{0,1},{1,0},{2,3},{3,2},{4,5},{5,4},{6,7},{7,6},{8,9},{9,8},{10,11... | collective-permute-start | bytes 294920 | tf_op jit(solution)/shard_map/ppermute | solution.py:247
  103.9 12.2 %collective-permute-start.17 = (bf16[2,32,768]{2,1,0:T(8,128)(2,1)S(1)}, bf16[2,32,768]{2,1,0:T(8,128)(2,1)S(1)}, u32[]{:S(2)}, u32[]{:S(2)}) collective-permute-start(bf16[2,32,768]{2,1,0:T(8,128)(2,1)S(1)} %get-tuple-element.97), channel_id=1, source_target_pairs={{0,2},{1,3},{2,0},{3,1},{4,6},{5,7},{6,4},{7,5},{8,10},{9,11},{10,... | collective-permute-start | bytes 294920 | tf_op jit(solution)/shard_map/ppermute | solution.py:247
  106.2 12.2 %collective-permute-start.18 = (bf16[2,32,768]{2,1,0:T(8,128)(2,1)S(1)}, bf16[2,32,768]{2,1,0:T(8,128)(2,1)S(1)}, u32[]{:S(2)}, u32[]{:S(2)}) collective-permute-start(bf16[2,32,768]{2,1,0:T(8,128)(2,1)S(1)} %get-tuple-element.98), channel_id=1, source_target_pairs={{0,3},{1,2},{2,1},{3,0},{4,7},{5,6},{6,5},{7,4},{8,11},{9,10},{10,... | collective-permute-start | bytes 294920 | tf_op jit(solution)/shard_map/ppermute | solution.py:247
  106.5 14.3 %collective-permute-start.19 = (bf16[2,32,768]{2,1,0:T(8,128)(2,1)S(1)}, bf16[2,32,768]{2,1,0:T(8,128)(2,1)S(1)}, u32[]{:S(2)}, u32[]{:S(2)}) collective-permute-start(bf16[2,32,768]{2,1,0:T(8,128)(2,1)S(1)} %get-tuple-element.99), channel_id=1, source_target_pairs={{0,4},{1,5},{2,6},{3,7},{4,0},{5,1},{6,2},{7,3},{8,12},{9,13},{10,... | collective-permute-start | bytes 294920 | tf_op jit(solution)/shard_map/ppermute | solution.py:247
  110.0 14.1 %collective-permute-start.20 = (bf16[2,32,768]{2,1,0:T(8,128)(2,1)S(1)}, bf16[2,32,768]{2,1,0:T(8,128)(2,1)S(1)}, u32[]{:S(2)}, u32[]{:S(2)}) collective-permute-start(bf16[2,32,768]{2,1,0:T(8,128)(2,1)S(1)} %get-tuple-element.100), channel_id=1, source_target_pairs={{0,5},{1,4},{2,7},{3,6},{4,1},{5,0},{6,3},{7,2},{8,13},{9,12},{10,... | collective-permute-start | bytes 294920 | tf_op jit(solution)/shard_map/ppermute | solution.py:247
  114.1 10.1 %collective-permute-start.21 = (bf16[2,32,768]{2,1,0:T(8,128)(2,1)S(1)}, bf16[2,32,768]{2,1,0:T(8,128)(2,1)S(1)}, u32[]{:S(2)}, u32[]{:S(2)}) collective-permute-start(bf16[2,32,768]{2,1,0:T(8,128)(2,1)S(1)} %get-tuple-element.101), channel_id=1, source_target_pairs={{0,6},{1,7},{2,4},{3,5},{4,2},{5,3},{6,0},{7,1},{8,14},{9,15},{10,... | collective-permute-start | bytes 294920 | tf_op jit(solution)/shard_map/ppermute | solution.py:247
  116.1 8.0 %collective-permute-start.22 = (bf16[2,32,768]{2,1,0:T(8,128)(2,1)S(1)}, bf16[2,32,768]{2,1,0:T(8,128)(2,1)S(1)}, u32[]{:S(2)}, u32[]{:S(2)}) collective-permute-start(bf16[2,32,768]{2,1,0:T(8,128)(2,1)S(1)} %get-tuple-element.102), channel_id=1, source_target_pairs={{0,7},{1,6},{2,5},{3,4},{4,3},{5,2},{6,1},{7,0},{8,15},{9,14},{10,... | collective-permute-start | bytes 294920 | tf_op jit(solution)/shard_map/ppermute | solution.py:247
  118.4 7.6 %collective-permute-start.55 = (bf16[8,2,32,128]{3,2,1,0:T(8,128)(2,1)S(1)}, bf16[8,2,32,128]{3,2,1,0:T(8,128)(2,1)S(1)}, u32[]{:S(2)}, u32[]{:S(2)}) collective-permute-start(bf16[8,2,32,128]{3,2,1,0:T(8,128)(2,1)S(1)} %get-tuple-element.139), channel_id=1, source_target_pairs={{0,8},{8,16},{16,24},{24,0},{1,9},{9,17},{17,25},{25,1},{2,10},{10... | collective-permute-start | bytes 393224 | tf_op jit(solution)/shard_map/ppermute | solution.py:303
  120.7 5.2 %collective-permute-start.56 = (bf16[8,2,32,128]{3,2,1,0:T(8,128)(2,1)S(1)}, bf16[8,2,32,128]{3,2,1,0:T(8,128)(2,1)S(1)}, u32[]{:S(2)}, u32[]{:S(2)}) collective-permute-start(bf16[8,2,32,128]{3,2,1,0:T(8,128)(2,1)S(1)} %get-tuple-element.140), channel_id=1, source_target_pairs={{8,0},{16,8},{24,16},{0,24},{9,1},{17,9},{25,17},{1,25},{10,2},{18... | collective-permute-start | bytes 393224 | tf_op jit(solution)/shard_map/ppermute | solution.py:304
  124.2 9.5 %collective-permute-start.23 = (bf16[8,2,32,128]{3,2,1,0:T(8,128)(2,1)S(1)}, bf16[8,2,32,128]{3,2,1,0:T(8,128)(2,1)S(1)}, u32[]{:S(2)}, u32[]{:S(2)}) collective-permute-start(bf16[8,2,32,128]{3,2,1,0:T(8,128)(2,1)S(1)} %get-tuple-element.103), channel_id=1, source_target_pairs={{0,8},{8,16},{16,24},{24,0},{1,9},{9,17},{17,25},{25,1},{2,10},{10... | collective-permute-start | bytes 393224 | tf_op jit(solution)/shard_map/ppermute | solution.py:303
  124.2 12.0 %collective-permute-start.24 = (bf16[8,2,32,128]{3,2,1,0:T(8,128)(2,1)S(1)}, bf16[8,2,32,128]{3,2,1,0:T(8,128)(2,1)S(1)}, u32[]{:S(2)}, u32[]{:S(2)}) collective-permute-start(bf16[8,2,32,128]{3,2,1,0:T(8,128)(2,1)S(1)} %get-tuple-element.104), channel_id=1, source_target_pairs={{8,0},{16,8},{24,16},{0,24},{9,1},{17,9},{25,17},{1,25},{10,2},{18... | collective-permute-start | bytes 393224 | tf_op jit(solution)/shard_map/ppermute | solution.py:304
  128.5 11.2 %collective-permute-start.57 = (bf16[2,32,768]{2,1,0:T(8,128)(2,1)S(1)}, bf16[2,32,768]{2,1,0:T(8,128)(2,1)S(1)}, u32[]{:S(2)}, u32[]{:S(2)}) collective-permute-start(bf16[2,32,768]{2,1,0:T(8,128)(2,1)S(1)} %get-tuple-element.142), channel_id=1, source_target_pairs={{0,1},{1,0},{2,3},{3,2},{4,5},{5,4},{6,7},{7,6},{8,9},{9,8},{10,11... | collective-permute-start | bytes 294920 | tf_op jit(solution)/shard_map/ppermute | solution.py:247
  129.7 11.8 %collective-permute-start.58 = (bf16[2,32,768]{2,1,0:T(8,128)(2,1)S(1)}, bf16[2,32,768]{2,1,0:T(8,128)(2,1)S(1)}, u32[]{:S(2)}, u32[]{:S(2)}) collective-permute-start(bf16[2,32,768]{2,1,0:T(8,128)(2,1)S(1)} %get-tuple-element.143), channel_id=1, source_target_pairs={{0,2},{1,3},{2,0},{3,1},{4,6},{5,7},{6,4},{7,5},{8,10},{9,11},{10,... | collective-permute-start | bytes 294920 | tf_op jit(solution)/shard_map/ppermute | solution.py:247
  133.3 10.5 %collective-permute-start.59 = (bf16[2,32,768]{2,1,0:T(8,128)(2,1)S(1)}, bf16[2,32,768]{2,1,0:T(8,128)(2,1)S(1)}, u32[]{:S(2)}, u32[]{:S(2)}) collective-permute-start(bf16[2,32,768]{2,1,0:T(8,128)(2,1)S(1)} %get-tuple-element.144), channel_id=1, source_target_pairs={{0,3},{1,2},{2,1},{3,0},{4,7},{5,6},{6,5},{7,4},{8,11},{9,10},{10,... | collective-permute-start | bytes 294920 | tf_op jit(solution)/shard_map/ppermute | solution.py:247
  133.6 13.2 %collective-permute-start.60 = (bf16[2,32,768]{2,1,0:T(8,128)(2,1)S(1)}, bf16[2,32,768]{2,1,0:T(8,128)(2,1)S(1)}, u32[]{:S(2)}, u32[]{:S(2)}) collective-permute-start(bf16[2,32,768]{2,1,0:T(8,128)(2,1)S(1)} %get-tuple-element.145), channel_id=1, source_target_pairs={{0,4},{1,5},{2,6},{3,7},{4,0},{5,1},{6,2},{7,3},{8,12},{9,13},{10,... | collective-permute-start | bytes 294920 | tf_op jit(solution)/shard_map/ppermute | solution.py:247
  136.2 14.5 %collective-permute-start.61 = (bf16[2,32,768]{2,1,0:T(8,128)(2,1)S(1)}, bf16[2,32,768]{2,1,0:T(8,128)(2,1)S(1)}, u32[]{:S(2)}, u32[]{:S(2)}) collective-permute-start(bf16[2,32,768]{2,1,0:T(8,128)(2,1)S(1)} %get-tuple-element.146), channel_id=1, source_target_pairs={{0,5},{1,4},{2,7},{3,6},{4,1},{5,0},{6,3},{7,2},{8,13},{9,12},{10,... | collective-permute-start | bytes 294920 | tf_op jit(solution)/shard_map/ppermute | solution.py:247
  139.7 11.1 %collective-permute-start.62 = (bf16[2,32,768]{2,1,0:T(8,128)(2,1)S(1)}, bf16[2,32,768]{2,1,0:T(8,128)(2,1)S(1)}, u32[]{:S(2)}, u32[]{:S(2)}) collective-permute-start(bf16[2,32,768]{2,1,0:T(8,128)(2,1)S(1)} %get-tuple-element.147), channel_id=1, source_target_pairs={{0,6},{1,7},{2,4},{3,5},{4,2},{5,3},{6,0},{7,1},{8,14},{9,15},{10,... | collective-permute-start | bytes 294920 | tf_op jit(solution)/shard_map/ppermute | solution.py:247
  141.5 12.0 %collective-permute-start.63 = (bf16[2,32,768]{2,1,0:T(8,128)(2,1)S(1)}, bf16[2,32,768]{2,1,0:T(8,128)(2,1)S(1)}, u32[]{:S(2)}, u32[]{:S(2)}) collective-permute-start(bf16[2,32,768]{2,1,0:T(8,128)(2,1)S(1)} %get-tuple-element.148), channel_id=1, source_target_pairs={{0,7},{1,6},{2,5},{3,4},{4,3},{5,2},{6,1},{7,0},{8,15},{9,14},{10,... | collective-permute-start | bytes 294920 | tf_op jit(solution)/shard_map/ppermute | solution.py:247
  143.8 13.6 %collective-permute-start.25 = (bf16[2,32,768]{2,1,0:T(8,128)(2,1)S(1)}, bf16[2,32,768]{2,1,0:T(8,128)(2,1)S(1)}, u32[]{:S(2)}, u32[]{:S(2)}) collective-permute-start(bf16[2,32,768]{2,1,0:T(8,128)(2,1)S(1)} %get-tuple-element.106), channel_id=1, source_target_pairs={{0,1},{1,0},{2,3},{3,2},{4,5},{5,4},{6,7},{7,6},{8,9},{9,8},{10,11... | collective-permute-start | bytes 294920 | tf_op jit(solution)/shard_map/ppermute | solution.py:247
  146.8 12.5 %collective-permute-start.26 = (bf16[2,32,768]{2,1,0:T(8,128)(2,1)S(1)}, bf16[2,32,768]{2,1,0:T(8,128)(2,1)S(1)}, u32[]{:S(2)}, u32[]{:S(2)}) collective-permute-start(bf16[2,32,768]{2,1,0:T(8,128)(2,1)S(1)} %get-tuple-element.107), channel_id=1, source_target_pairs={{0,2},{1,3},{2,0},{3,1},{4,6},{5,7},{6,4},{7,5},{8,10},{9,11},{10,... | collective-permute-start | bytes 294920 | tf_op jit(solution)/shard_map/ppermute | solution.py:247
  150.7 11.0 %collective-permute-start.27 = (bf16[2,32,768]{2,1,0:T(8,128)(2,1)S(1)}, bf16[2,32,768]{2,1,0:T(8,128)(2,1)S(1)}, u32[]{:S(2)}, u32[]{:S(2)}) collective-permute-start(bf16[2,32,768]{2,1,0:T(8,128)(2,1)S(1)} %get-tuple-element.108), channel_id=1, source_target_pairs={{0,3},{1,2},{2,1},{3,0},{4,7},{5,6},{6,5},{7,4},{8,11},{9,10},{10,... | collective-permute-start | bytes 294920 | tf_op jit(solution)/shard_map/ppermute | solution.py:247
  150.7 12.1 %collective-permute-start.28 = (bf16[2,32,768]{2,1,0:T(8,128)(2,1)S(1)}, bf16[2,32,768]{2,1,0:T(8,128)(2,1)S(1)}, u32[]{:S(2)}, u32[]{:S(2)}) collective-permute-start(bf16[2,32,768]{2,1,0:T(8,128)(2,1)S(1)} %get-tuple-element.109), channel_id=1, source_target_pairs={{0,4},{1,5},{2,6},{3,7},{4,0},{5,1},{6,2},{7,3},{8,12},{9,13},{10,... | collective-permute-start | bytes 294920 | tf_op jit(solution)/shard_map/ppermute | solution.py:247
  153.6 14.0 %collective-permute-start.29 = (bf16[2,32,768]{2,1,0:T(8,128)(2,1)S(1)}, bf16[2,32,768]{2,1,0:T(8,128)(2,1)S(1)}, u32[]{:S(2)}, u32[]{:S(2)}) collective-permute-start(bf16[2,32,768]{2,1,0:T(8,128)(2,1)S(1)} %get-tuple-element.110), channel_id=1, source_target_pairs={{0,5},{1,4},{2,7},{3,6},{4,1},{5,0},{6,3},{7,2},{8,13},{9,12},{10,... | collective-permute-start | bytes 294920 | tf_op jit(solution)/shard_map/ppermute | solution.py:247
  157.4 10.1 %collective-permute-start.30 = (bf16[2,32,768]{2,1,0:T(8,128)(2,1)S(1)}, bf16[2,32,768]{2,1,0:T(8,128)(2,1)S(1)}, u32[]{:S(2)}, u32[]{:S(2)}) collective-permute-start(bf16[2,32,768]{2,1,0:T(8,128)(2,1)S(1)} %get-tuple-element.111), channel_id=1, source_target_pairs={{0,6},{1,7},{2,4},{3,5},{4,2},{5,3},{6,0},{7,1},{8,14},{9,15},{10,... | collective-permute-start | bytes 294920 | tf_op jit(solution)/shard_map/ppermute | solution.py:247
  159.3 8.2 %collective-permute-start.31 = (bf16[2,32,768]{2,1,0:T(8,128)(2,1)S(1)}, bf16[2,32,768]{2,1,0:T(8,128)(2,1)S(1)}, u32[]{:S(2)}, u32[]{:S(2)}) collective-permute-start(bf16[2,32,768]{2,1,0:T(8,128)(2,1)S(1)} %get-tuple-element.112), channel_id=1, source_target_pairs={{0,7},{1,6},{2,5},{3,4},{4,3},{5,2},{6,1},{7,0},{8,15},{9,14},{10,... | collective-permute-start | bytes 294920 | tf_op jit(solution)/shard_map/ppermute | solution.py:247
  (24 other events, 261.2 us)

commit v2 on v0

--- a/solution.py
+++ b/solution.py
@@ -1,6 +1,10 @@
+import functools
+
 import jax
 import jax.numpy as jnp
 from jax import lax
+from jax.experimental import pallas as pl
+from jax.experimental.pallas import tpu as pltpu
 from jax.sharding import PartitionSpec as P
 
 SWEEPS = 2
@@ -20,7 +24,7 @@
     return block
 
 
-def on_device(traces, sources, local_ops, plane_coupling, face_owner):
+def many_subdomains(traces, sources, local_ops, plane_coupling, face_owner):
     columns_all = local_ops.shape[-1]
     slab_width = columns_all // 6
     slab_rows = traces.shape[4]
@@ -40,7 +44,7 @@
         select,
         precision=lax.Precision.HIGHEST,
     ).astype(jnp.bfloat16)
-    for sweep_step in range(SWEEPS):
+    for _ in range(SWEEPS):
         real_part = (
             jnp.dot(incoming[0], operators[0], preferred_element_type=jnp.float32)
             - jnp.dot(incoming[1], operators[1], preferred_element_type=jnp.float32)
@@ -86,6 +90,332 @@
     return incoming.reshape(traces.shape)
 
 
+VMEM = pl.BlockSpec(memory_space=pltpu.VMEM)
+SMEM = pl.BlockSpec(memory_space=pltpu.SMEM)
+HBM = pl.BlockSpec(memory_space=pltpu.HBM)
+KERNEL_BYTES = 24 << 20
+FIRST_BYTES = 50 << 20
+KERNEL_FLOPS = 1 << 31
+
+
+def plane_position():
+    return lax.axis_index("gy") * lax.axis_size("gz") + lax.axis_index("gz")
+
+
+def call(kernel, in_specs, out_shape, out_specs=None, aliases=None, scratch=(), limit=KERNEL_BYTES):
+    return pl.pallas_call(
+        kernel,
+        in_specs=in_specs,
+        out_shape=out_shape,
+        out_specs=out_specs if out_specs is not None else jax.tree.map(lambda _: VMEM, out_shape),
+        scratch_shapes=scratch,
+        input_output_aliases=aliases or {},
+        cost_estimate=pl.CostEstimate(
+            flops=KERNEL_FLOPS, bytes_accessed=1 << 20, transcendentals=0
+        ),
+        compiler_params=pltpu.CompilerParams(vmem_limit_bytes=limit),
+    )
+
+
+def row_start(k, rows):
+    return pl.multiple_of((plane_position() ^ k) * rows, rows)
+
+
+def part_products(part, real, imag, operators):
+    if part == 0:
+        return jnp.dot(real, operators[0], preferred_element_type=jnp.float32) - jnp.dot(
+            imag, operators[1], preferred_element_type=jnp.float32
+        )
+    return jnp.dot(real, operators[1], preferred_element_type=jnp.float32) + jnp.dot(
+        imag, operators[0], preferred_element_type=jnp.float32
+    )
+
+
+def load_and_solve(ks, plane_size, rows, first, columns, traces_ref, sources_ref, operators_ref, *refs):
+    blocks, (traces, sources, operators, sems) = refs[: len(ks)], refs[len(ks) :]
+    wanted = [slice(first, first + columns)]
+    unwanted = [slice(0, first), slice(first + columns, operators.shape[-1])]
+    unwanted = [c for c in unwanted if c.stop > c.start]
+    others = [k for k in range(plane_size) if k not in ks]
+
+    def rows_of(source, target, which):
+        return [
+            (source.at[:, pl.ds(row_start(k, rows), rows), :], target.at[k]) for k in which
+        ]
+
+    def operators_of(which):
+        return [
+            (operators_ref.at[part, :, c], operators.at[part, :, c])
+            for c in which
+            for part in range(2)
+        ]
+
+    needed = rows_of(traces_ref, traces, ks) + operators_of(wanted)
+    late = rows_of(sources_ref, sources, ks)
+    rest = rows_of(traces_ref, traces, others) + operators_of(unwanted)
+    rest += rows_of(sources_ref, sources, others)
+    copies = [
+        pltpu.make_async_copy(source, target, sems.at[n])
+        for n, (source, target) in enumerate(needed + late + rest)
+    ]
+    for copy in copies:
+        copy.start()
+    for copy in copies[: len(needed)]:
+        copy.wait()
+    real, imag = (jnp.concatenate([traces[k, part] for k in ks], axis=0) for part in range(2))
+    results = [
+        part_products(part, real, imag, [operators[p, :, wanted[0]] for p in range(2)])
+        for part in range(2)
+    ]
+    for copy in copies[len(needed) : len(needed) + len(late)]:
+        copy.wait()
+    finish(ks, rows, wanted[0], pick_block, results, sources, blocks)
+    for copy in copies[len(needed) + len(late) :]:
+        copy.wait()
+
+
+def finish(ks, rows, wanted, pick, results, sources, outputs):
+    for part, result in enumerate(results):
+        for n, k in enumerate(ks):
+            block = result[n * rows : (n + 1) * rows] + sources[k, part, :, wanted].astype(
+                jnp.float32
+            )
+            pick(outputs, part, n, block.astype(outputs[0].dtype))
+
+
+def solve_blocks(ks, rows, first, columns, pick, count, *refs):
+    wanted = slice(first, first + columns)
+    if count == 1:
+        traces, sources, operators_ref = refs[:3]
+        outputs = refs[3:]
+        pieces = [[jnp.concatenate([traces[k, part] for k in ks], axis=0) for part in range(2)]]
+    else:
+        incoming, (sources, operators_ref) = refs[: 2 * len(ks)], refs[2 * len(ks) : 2 * len(ks) + 2]
+        outputs = refs[2 * len(ks) + 2 :]
+        pieces = [
+            [jnp.concatenate([b[part] for b in group], axis=0) for part in range(2)]
+            for group in (incoming[: len(ks)], incoming[len(ks) :])
+        ]
+    results = [0.0, 0.0]
+    start = 0
+    for real, imag in pieces:
+        depth = slice(start, start + real.shape[-1])
+        start = depth.stop
+        operators = [operators_ref[part, depth, wanted] for part in range(2)]
+        for part in range(2):
+            results[part] = results[part] + part_products(part, real, imag, operators)
+    finish(ks, rows, wanted, pick, results, sources, outputs)
+
+
+def pick_block(outputs, part, k, block):
+    outputs[k][part] = block
+
+
+def pick_face(outputs, part, k, block):
+    width = block.shape[-1] // 2
+    outputs[0][k, part] = block[:, :width]
+    outputs[1][k, part] = block[:, width:]
+
+
+def pack_faces(from_low_ref, from_high_ref, *outputs):
+    width = from_low_ref.shape[-1]
+    for k, output in enumerate(outputs):
+        output[:, :, :width] = from_low_ref[k]
+        output[:, :, width:] = from_high_ref[k]
+
+
+def make_weights(count_y, count_z, coupling_ref, owner_ref, weights_ref, column_ref):
+    plane_size = count_y * count_z
+    me = plane_position()
+
+    def clear(q, carry):
+        for p in range(plane_size):
+            column_ref[p, q] = jnp.where(p == q, jnp.float32(1), jnp.float32(0))
+        return carry
+
+    def couple(q, carry):
+        owner = owner_ref[q]
+        for p in range(plane_size):
+            column_ref[p, owner] = column_ref[p, owner] - coupling_ref[p, q]
+        return carry
+
+    lax.fori_loop(0, plane_size, clear, 0)
+    lax.fori_loop(0, plane_size, couple, 0)
+
+    def fill(m, carry):
+        source = me ^ m
+        y, z = source // count_z, source % count_z
+        receivers = (
+            source,
+            ((y + 1) % count_y) * count_z + z,
+            ((y + count_y - 1) % count_y) * count_z + z,
+            y * count_z + (z + 1) % count_z,
+            y * count_z + (z + count_z - 1) % count_z,
+        )
+        for face, receiver in enumerate(receivers):
+            for k in range(plane_size):
+                weights_ref[face, k, m] = column_ref[me ^ k, receiver]
+        return carry
+
+    lax.fori_loop(0, plane_size, fill, 0)
+
+
+def mix_blocks(plane_size, plan, *refs):
+    blocks, weights_ref, outputs = refs[:plane_size], refs[plane_size], refs[plane_size + 1 :]
+    width = blocks[0].shape[-1] // len(plan)
+    for face, (kind, source_face) in enumerate(plan):
+        columns = slice(source_face * width, (source_face + 1) * width)
+        for part in range(2):
+            values = [b[part, :, columns].astype(jnp.float32) for b in blocks]
+            for k, output in enumerate(outputs):
+                total = values[0] * weights_ref[kind, k, 0]
+                for m in range(1, plane_size):
+                    total = total + values[m] * weights_ref[kind, k, m]
+                output[part, :, face * width : (face + 1) * width] = total.astype(output.dtype)
+
+
+def store_rows(plane_size, rows, first, *refs):
+    blocks, out_ref, sems = refs[:plane_size], refs[-2], refs[-1]
+    columns = blocks[0].shape[-1]
+    copies = [
+        pltpu.make_async_copy(
+            blocks[k],
+            out_ref.at[:, pl.ds(row_start(k, rows), rows), pl.ds(first, columns)],
+            sems.at[k],
+        )
+        for k in range(plane_size)
+    ]
+    for copy in copies:
+        copy.start()
+    for copy in copies:
+        copy.wait()
+
+
+def partners(count_y, count_z):
+    across = range(1, count_y * count_z)
+    return sorted(across, key=lambda k: (2 * (k // count_z) < count_y, k % count_z, k))
+
+
+def far_and_near(count_y, count_z):
+    ks = partners(count_y, count_z)
+    far = tuple(k for k in ks if 2 * (k // count_z) >= count_y)
+    return far, tuple(k for k in ks if k not in far)
+
+
+def row_groups(count_y, count_z):
+    far, near = far_and_near(count_y, count_z)
+    half = len(far) // 2
+    return [ks for ks in (far[:half], far[half:], (0,) + near) if ks]
+
+
+def exchange(blocks, count_y, count_z):
+    plane_size = count_y * count_z
+    received = [blocks[0]] + [None] * (plane_size - 1)
+    for k in partners(count_y, count_z):
+        received[k] = lax.ppermute(blocks[k], ("gy", "gz"), [(p, p ^ k) for p in range(plane_size)])
+    return received
+
+
+def few_subdomains(traces, sources, local_ops, plane_coupling, face_owner):
+    columns_all = local_ops.shape[-1]
+    width = columns_all // 6
+    slab_rows = traces.shape[4]
+    count_x, count_y, count_z = (lax.axis_size(a) for a in ("gx", "gy", "gz"))
+    plane_size = count_y * count_z
+    rows = slab_rows // plane_size
+    operators = local_ops.reshape(2, columns_all, columns_all)
+    source_rows = sources.reshape(2, slab_rows, columns_all)
+    trace_rows = traces.reshape(2, slab_rows, columns_all)
+    dtype = traces.dtype
+    forward = [(i, (i + 1) % count_x) for i in range(count_x)]
+    backward = [(target, source) for source, target in forward]
+    whole = jax.ShapeDtypeStruct((2, slab_rows, columns_all), dtype)
+    groups = {"x": (0, 2 * width), "yz": (2 * width, 4 * width)}
+    plans = {"x": ((0, 0), (0, 1)), "yz": ((1, 1), (2, 0), (3, 3), (4, 2))}
+    face = jax.ShapeDtypeStruct((plane_size, 2, rows, width), dtype)
+    blocks_of = {
+        g: [jax.ShapeDtypeStruct((2, rows, columns), dtype)] * plane_size
+        for g, (_, columns) in groups.items()
+    }
+    solved = {"x": ([face] * 2, pick_face), "yz": (blocks_of["yz"], pick_block)}
+
+    placed = []
+
+    def solve(group, sweep, ks, incoming):
+        first, columns = groups[group]
+        out_shape, pick = solved[group]
+        if group == "yz":
+            out_shape = out_shape[: len(ks)]
+        if not placed:
+            by_block = jax.ShapeDtypeStruct((plane_size, 2, rows, columns_all), dtype)
+            results = call(
+                functools.partial(load_and_solve, ks, plane_size, rows, first, columns),
+                [HBM] * 3,
+                out_shape
+                + [by_block, by_block, jax.ShapeDtypeStruct(operators.shape, dtype)],
+                scratch=[pltpu.SemaphoreType.DMA((2 * plane_size + 6,))],
+                limit=FIRST_BYTES,
+            )(trace_rows, source_rows, operators)
+            placed.extend(results[len(ks) :])
+            return results[: len(ks)]
+        if sweep == 0:
+            arrays = [placed[0]]
+        else:
+            arrays = [incoming[g][k] for g in ("x", "yz") for k in ks]
+        return call(
+            functools.partial(solve_blocks, ks, rows, first, columns, pick, 1 if sweep == 0 else 2),
+            [VMEM] * (len(arrays) + 2),
+            out_shape,
+        )(*arrays, *placed[1:])
+
+    def mix(group, gathered, weights):
+        return call(
+            functools.partial(mix_blocks, plane_size, plans[group]),
+            [VMEM] * plane_size + [SMEM],
+            blocks_of[group],
+        )(*gathered, weights)
+
+    def store(group, blocks, so_far):
+        before = [] if so_far is None else [so_far]
+        return call(
+            functools.partial(store_rows, plane_size, rows, groups[group][0]),
+            [VMEM] * plane_size + [HBM] * len(before),
+            whole,
+            out_specs=HBM,
+            aliases={plane_size: 0} if before else None,
+            scratch=[pltpu.SemaphoreType.DMA((plane_size,))],
+        )(*blocks, *before)
+
+    weights = call(
+        functools.partial(make_weights, count_y, count_z),
+        [SMEM, SMEM],
+        jax.ShapeDtypeStruct((5, plane_size, plane_size), jnp.float32),
+        out_specs=SMEM,
+        scratch=[pltpu.SMEM((plane_size, plane_size), jnp.float32)],
+    )(
+        plane_coupling.reshape(plane_size, plane_size).astype(jnp.float32),
+        face_owner.reshape(plane_size),
+    )
+    incoming = None
+    for sweep in range(SWEEPS):
+        out_yz = [None] * plane_size
+        for ks in row_groups(count_y, count_z):
+            for k, block in zip(ks, solve("yz", sweep, ks, incoming)):
+                out_yz[k] = block
+        gathered_yz = exchange(out_yz, count_y, count_z)
+        low, high = solve("x", sweep, tuple(range(plane_size)), incoming)
+        from_low = lax.ppermute(high, "gx", forward)
+        from_high = lax.ppermute(low, "gx", backward)
+        packed = call(pack_faces, [VMEM] * 2, blocks_of["x"])(from_low, from_high)
+        gathered_x = exchange(packed, count_y, count_z)
+        mixed_yz = mix("yz", gathered_yz, weights)
+        incoming = {"yz": exchange(mixed_yz, count_y, count_z)}
+        mixed_x = mix("x", gathered_x, weights)
+        incoming["x"] = exchange(mixed_x, count_y, count_z)
+    result = store("x", incoming["x"], store("yz", incoming["yz"], None))
+    return result.reshape(traces.shape)
+
+
 def solution(mesh):
     placed = (
         P(None, "gx", "gy", "gz", None, None),
@@ -94,8 +424,10 @@
         P("gx", None, None),
         P("gx", None),
     )
+    counts = [mesh.shape[a] for a in ("gy", "gz")]
+    few = counts[0] * counts[1] <= 8 and all(c & (c - 1) == 0 for c in counts)
     return jax.shard_map(
-        on_device,
+        few_subdomains if few else many_subdomains,
         mesh=mesh,
         in_specs=placed,
         out_specs=P(None, "gx", "gy", "gz", None, None),

time: 246 us -> 174 us (0.71)
  blocking collectives: 123 us -> 0 us
  starting transfers between devices: 10.3 us -> 98.6 us
  local copies, waits for them, and re-layouts: 36.5 us -> 1.68 us
  Pallas kernels: 0 us -> 21.8 us
  matrix products: 21.5 us -> 0 us
  other arithmetic: 3.27 us -> 0.01 us
    all_to_all x3 -> x0, blocking collectives: 123 us -> none  [the longest x2 81.3 us: on_device(): lax.all_to_all(updated, ('gy', 'gz'), split_axis=1, concat_axis=1, tiled=...]
    ppermute x4 -> x60, starting transfers between devices: 4.31 us -> 98.6 us  [the longest x56 96.7 us: exchange(): lax.ppermute(blocks[k], ('gy', 'gz'), [(p, p ^ k) for p in range(plane_si...]
    ppermute x4 -> x60, waiting for transfers between devices: 12.5 us -> 51.6 us  [the longest x56 47.5 us: exchange(): lax.ppermute(blocks[k], ('gy', 'gz'), [(p, p ^ k) for p in range(plane_si...]
    all_to_all x1 -> x0, waiting for transfers between devices: 37.8 us -> none  [on_device(): lax.all_to_all(blocks, ('gy', 'gz'), split_axis=1, concat_axis=1, tiled=T...]
    pallas_call x0 -> x17, Pallas kernels: none -> 21.8 us  [the longest x4 7.15 us: mix(): call(functools.partial(mix_blocks, plane_size, plans[group]), [VMEM] * pl...]
    dot_general x11 -> x0, matrix products: 21.5 us -> none  [the longest x2 5.54 us: on_device(): jnp.dot(incoming[1], operators[1], preferred_element_type=jnp.float32)]
    another operation x7 -> x0, local copies, waits for them, and re-layouts: 15.1 us -> none
    reshape x6 -> x0, local copies, waits for them, and re-layouts: 10.1 us -> none  [the longest x2 6.42 us: on_device(): block_rows = moved.reshape(2, plane_size, row_count * columns_all)]
  transfers between devices with their start and end apart: 5 -> 60, of which waited for: 5 -> 15; matrix products, arithmetic and copies ran while one was open for 0% -> 0% of each run, Pallas kernels for 0% -> 10%
where the time goes in v2:
time: 174 us
  starting transfers between devices  98.6 us (57%)
  waiting for transfers between devices  51.6 us (30%)
  Pallas kernels  21.8 us (13%)
    ppermute x56, starting transfers between devices, exchange(): lax.ppermute(blocks[k], ('gy', 'gz'), [(p, p ^ k) for p in range(plane_si...  96.7 us
    ppermute x56, waiting for transfers between devices, exchange(): lax.ppermute(blocks[k], ('gy', 'gz'), [(p, p ^ k) for p in range(plane_si...  47.5 us
    pallas_call x4, Pallas kernels, mix(): call(functools.partial(mix_blocks, plane_size, plans[group]), [VMEM] * pl...  7.15 us
    pallas_call x7, Pallas kernels, solve(): call(functools.partial(solve_blocks, ks, rows, first, columns, pick, 1 if...  5.75 us
    pallas_call x1, Pallas kernels, solve(): call(functools.partial(load_and_solve, ks, plane_size, rows, first, colum...  4.19 us
    ppermute x2, waiting for transfers between devices, few_subdomains(): from_low = lax.ppermute(high, 'gx', forward)  4.06 us
  transfers between devices with their start and end apart: 60, of which 15 were waited for; matrix products, arithmetic and copies ran while one was open for 0% of the time, Pallas kernels for 10%

profile of v2, /device:TPU:0, one launch (start us, length us, event | category | flops | bytes accessed | tf_op | source)
XLA Modules:
  0.0 174.1 jit_solution(17816070976845920726)
XLA Ops:
  0.0 4.2 %shard_map.55 = (bf16[2,64,512]{2,1,0:T(8,128)(2,1)S(1)}, bf16[2,64,512]{2,1,0:T(8,128)(2,1)S(1)}, bf16[8,2,64,768]{3,2,1,0:T(8,128)(2,1)S(1)}, bf16[8,2,64,768]{3,2,1,0:T(8,128)(2,1)S(1)}, bf16[2,768,768]{2,1,0:T(8,128)(2,1)}) custom-call(bf16[2,512,768]{2,1,0:T(8,128)(2,1)} %bitcast.12, bf16[2,512,768]{2,1,0:T(8,128)(2,1)} %bitcast.13, ...), custom_call_target="tpu_custom_call" | custom-call | flops 2147483648 | bytes 1048576 | tf_op jit(solution)/shard_map/pallas_call | solution.py:351
  4.2 4.1 %collective-permute-start.19 = (bf16[2,64,512]{2,1,0:T(8,128)(2,1)S(1)}, bf16[2,64,512]{2,1,0:T(8,128)(2,1)S(1)}, u32[]{:S(2)}, u32[]{:S(2)}) collective-permute-start(bf16[2,64,512]{2,1,0:T(8,128)(2,1)S(1)} %get-tuple-element.101), channel_id=1, source_target_pairs={{0,4},{1,5},{2,6},{3,7},{4,0},{5,1},{6,2},{7,3},{8,12},{9,13},{10,... | collective-permute-start | bytes 393224 | tf_op jit(solution)/shard_map/ppermute | solution.py:315
  8.3 1.3 collective-permute-start.21
  9.7 1.7 copy-done.1
  11.9 2.7 %collective-permute-start.20 = (bf16[2,64,512]{2,1,0:T(8,128)(2,1)S(1)}, bf16[2,64,512]{2,1,0:T(8,128)(2,1)S(1)}, u32[]{:S(2)}, u32[]{:S(2)}) collective-permute-start(bf16[2,64,512]{2,1,0:T(8,128)(2,1)S(1)} %get-tuple-element.102), channel_id=1, source_target_pairs={{0,5},{1,4},{2,7},{3,6},{4,1},{5,0},{6,3},{7,2},{8,13},{9,12},{10,... | collective-permute-start | bytes 393224 | tf_op jit(solution)/shard_map/ppermute | solution.py:315
  15.7 1.7 collective-permute-start.1
  18.4 4.1 %collective-permute-done.from_low_ref = bf16[8,2,64,128]{3,2,1,0:T(8,128)(2,1)S(1)} collective-permute-done((bf16[8,2,64,128]{3,2,1,0:T(8,128)(2,1)S(1)}, bf16[8,2,64,128]{3,2,1,0:T(8,128)(2,1)S(1)}, u32[]{:S(2)}, u32[]{:S(2)}) %collective-permute-start) | collective-permute-done | bytes 262176 | tf_op jit(solution)/shard_map/ppermute | solution.py:407
  23.3 1.5 collective-permute-start.16
  25.9 1.1 collective-permute-start.18
  27.0 1.5 collective-permute-start.2
  28.5 3.1 %collective-permute-done.22.refs_7_ = bf16[2,64,512]{2,1,0:T(8,128)(2,1)S(1)} collective-permute-done((bf16[2,64,512]{2,1,0:T(8,128)(2,1)S(1)}, bf16[2,64,512]{2,1,0:T(8,128)(2,1)S(1)}, u32[]{:S(2)}, u32[]{:S(2)}) %collective-permute-start.22) | collective-permute-done | bytes 131104 | tf_op jit(solution)/shard_map/ppermute | solution.py:315
  31.6 2.0 %collective-permute-start.3 = (bf16[2,64,256]{2,1,0:T(8,128)(2,1)S(1)}, bf16[2,64,256]{2,1,0:T(8,128)(2,1)S(1)}, u32[]{:S(2)}, u32[]{:S(2)}) collective-permute-start(bf16[2,64,256]{2,1,0:T(8,128)(2,1)S(1)} %get-tuple-element.83), channel_id=1, source_target_pairs={{0,2},{1,3},{2,0},{3,1},{4,6},{5,7},{6,4},{7,5},{8,10},{9,11},{10,... | collective-permute-start | bytes 196616 | tf_op jit(solution)/shard_map/ppermute | solution.py:315
  33.6 2.7 %shard_map.58.refs_8_ = f32[5,8,8]{2,1,0:T(8,128)S(1)} custom-call(f32[8,8]{1,0:T(8,128)S(1)} %bitcast_convert_fusion.coupling_ref, s32[8]{0:T(128)S(1)} %bitcast.10), custom_call_target="tpu_custom_call" | custom-call | flops 2147483648 | bytes 1048576 | tf_op jit(solution)/shard_map/pallas_call | solution.py:389
  36.5 4.9 %collective-permute-start.5 = (bf16[2,64,256]{2,1,0:T(8,128)(2,1)S(1)}, bf16[2,64,256]{2,1,0:T(8,128)(2,1)S(1)}, u32[]{:S(2)}, u32[]{:S(2)}) collective-permute-start(bf16[2,64,256]{2,1,0:T(8,128)(2,1)S(1)} %get-tuple-element.85), channel_id=1, source_target_pairs={{0,4},{1,5},{2,6},{3,7},{4,0},{5,1},{6,2},{7,3},{8,12},{9,13},{10,... | collective-permute-start | bytes 196616 | tf_op jit(solution)/shard_map/ppermute | solution.py:315
  41.4 1.0 collective-permute-start.6
  42.5 2.3 %collective-permute-start.7 = (bf16[2,64,256]{2,1,0:T(8,128)(2,1)S(1)}, bf16[2,64,256]{2,1,0:T(8,128)(2,1)S(1)}, u32[]{:S(2)}, u32[]{:S(2)}) collective-permute-start(bf16[2,64,256]{2,1,0:T(8,128)(2,1)S(1)} %get-tuple-element.87), channel_id=1, source_target_pairs={{0,6},{1,7},{2,4},{3,5},{4,2},{5,3},{6,0},{7,1},{8,14},{9,15},{10,... | collective-permute-start | bytes 196616 | tf_op jit(solution)/shard_map/ppermute | solution.py:315
  44.8 1.5 collective-permute-start.8
  46.3 2.1 %shard_map.62 = (bf16[2,64,512]{2,1,0:T(8,128)(2,1)S(1)}, bf16[2,64,512]{2,1,0:T(8,128)(2,1)S(1)}, bf16[2,64,512]{2,1,0:T(8,128)(2,1)S(1)}, bf16[2,64,512]{2,1,0...) custom-call(bf16[2,64,512]{2,1,0:T(8,128)(2,1)S(1)} %get-tuple-eleme, ...), custom_call_target="tpu_custom_call" | custom-call | flops 2147483648 | bytes 1048576 | tf_op jit(solution)/shard_map/pallas_call | solution.py:372
  48.4 1.5 collective-permute-start.23
  50.6 1.3 collective-permute-start.25
  52.3 1.5 shard_map.59
  53.8 1.2 collective-permute-start.9
  55.0 2.1 %collective-permute-start.10 = (bf16[2,64,256]{2,1,0:T(8,128)(2,1)S(1)}, bf16[2,64,256]{2,1,0:T(8,128)(2,1)S(1)}, u32[]{:S(2)}, u32[]{:S(2)}) collective-permute-start(bf16[2,64,256]{2,1,0:T(8,128)(2,1)S(1)} %get-tuple-element.91), channel_id=1, source_target_pairs={{0,2},{1,3},{2,0},{3,1},{4,6},{5,7},{6,4},{7,5},{8,10},{9,11},{10,... | collective-permute-start | bytes 196616 | tf_op jit(solution)/shard_map/ppermute | solution.py:315
  57.1 1.1 collective-permute-start.11
  58.2 2.4 %collective-permute-start.26 = (bf16[2,64,512]{2,1,0:T(8,128)(2,1)S(1)}, bf16[2,64,512]{2,1,0:T(8,128)(2,1)S(1)}, u32[]{:S(2)}, u32[]{:S(2)}) collective-permute-start(bf16[2,64,512]{2,1,0:T(8,128)(2,1)S(1)} %get-tuple-element.109), channel_id=1, source_target_pairs={{0,4},{1,5},{2,6},{3,7},{4,0},{5,1},{6,2},{7,3},{8,12},{9,13},{10,... | collective-permute-start | bytes 393224 | tf_op jit(solution)/shard_map/ppermute | solution.py:315
  61.3 2.3 %collective-permute-start.28 = (bf16[2,64,512]{2,1,0:T(8,128)(2,1)S(1)}, bf16[2,64,512]{2,1,0:T(8,128)(2,1)S(1)}, u32[]{:S(2)}, u32[]{:S(2)}) collective-permute-start(bf16[2,64,512]{2,1,0:T(8,128)(2,1)S(1)} %get-tuple-element.111), channel_id=1, source_target_pairs={{0,6},{1,7},{2,4},{3,5},{4,2},{5,3},{6,0},{7,1},{8,14},{9,15},{10,... | collective-permute-start | bytes 393224 | tf_op jit(solution)/shard_map/ppermute | solution.py:315
  64.4 2.6 %collective-permute-start.14 = (bf16[2,64,256]{2,1,0:T(8,128)(2,1)S(1)}, bf16[2,64,256]{2,1,0:T(8,128)(2,1)S(1)}, u32[]{:S(2)}, u32[]{:S(2)}) collective-permute-start(bf16[2,64,256]{2,1,0:T(8,128)(2,1)S(1)} %get-tuple-element.95), channel_id=1, source_target_pairs={{0,6},{1,7},{2,4},{3,5},{4,2},{5,3},{6,0},{7,1},{8,14},{9,15},{10,... | collective-permute-start | bytes 196616 | tf_op jit(solution)/shard_map/ppermute | solution.py:315
  67.1 1.0 shard_map.66
  68.1 9.5 %collective-permute-done.26.refs_12_.refs_2_ = bf16[2,64,512]{2,1,0:T(8,128)(2,1)S(1)} collective-permute-done((bf16[2,64,512]{2,1,0:T(8,128)(2,1)S(1)}, bf16[2,64,512]{2,1,0:T(8,128)(2,1)S(1)}, u32[]{:S(2)}, u32[]{:S(2)}) %collective-permute-start.26) | collective-permute-done | bytes 131104 | tf_op jit(solution)/shard_map/ppermute | solution.py:315
  77.5 1.7 collective-permute-start.29
  79.2 4.7 %collective-permute-start.13 = (bf16[2,64,256]{2,1,0:T(8,128)(2,1)S(1)}, bf16[2,64,256]{2,1,0:T(8,128)(2,1)S(1)}, u32[]{:S(2)}, u32[]{:S(2)}) collective-permute-start(bf16[2,64,256]{2,1,0:T(8,128)(2,1)S(1)} %get-tuple-element.94), channel_id=1, source_target_pairs={{0,5},{1,4},{2,7},{3,6},{4,1},{5,0},{6,3},{7,2},{8,13},{9,12},{10,... | collective-permute-start | bytes 196616 | tf_op jit(solution)/shard_map/ppermute | solution.py:315
  83.9 3.4 %collective-permute-done.12.refs_4_.refs_0_ = bf16[2,64,256]{2,1,0:T(8,128)(2,1)S(1)} collective-permute-done((bf16[2,64,256]{2,1,0:T(8,128)(2,1)S(1)}, bf16[2,64,256]{2,1,0:T(8,128)(2,1)S(1)}, u32[]{:S(2)}, u32[]{:S(2)}) %collective-permute-start.12) | collective-permute-done | bytes 65568 | tf_op jit(solution)/shard_map/ppermute | solution.py:315
  87.4 1.7 collective-permute-start.15
  89.1 1.2 collective-permute-start.46
  91.0 2.4 %collective-permute-start.48 = (bf16[2,64,512]{2,1,0:T(8,128)(2,1)S(1)}, bf16[2,64,512]{2,1,0:T(8,128)(2,1)S(1)}, u32[]{:S(2)}, u32[]{:S(2)}) collective-permute-start(bf16[2,64,512]{2,1,0:T(8,128)(2,1)S(1)} %get-tuple-element.134), channel_id=1, source_target_pairs={{0,3},{1,2},{2,1},{3,0},{4,7},{5,6},{6,5},{7,4},{8,11},{9,10},{10,... | collective-permute-start | bytes 393224 | tf_op jit(solution)/shard_map/ppermute | solution.py:315
  95.1 1.5 collective-permute-start.51
  97.2 2.1 %collective-permute-start.50 = (bf16[2,64,512]{2,1,0:T(8,128)(2,1)S(1)}, bf16[2,64,512]{2,1,0:T(8,128)(2,1)S(1)}, u32[]{:S(2)}, u32[]{:S(2)}) collective-permute-start(bf16[2,64,512]{2,1,0:T(8,128)(2,1)S(1)} %get-tuple-element.136), channel_id=1, source_target_pairs={{0,5},{1,4},{2,7},{3,6},{4,1},{5,0},{6,3},{7,2},{8,13},{9,12},{10,... | collective-permute-start | bytes 393224 | tf_op jit(solution)/shard_map/ppermute | solution.py:315
  99.3 1.6 collective-permute-start.52
  100.9 1.0 shard_map.63
  102.0 7.5 %collective-permute-done.49.refs_4_ = bf16[2,64,512]{2,1,0:T(8,128)(2,1)S(1)} collective-permute-done((bf16[2,64,512]{2,1,0:T(8,128)(2,1)S(1)}, bf16[2,64,512]{2,1,0:T(8,128)(2,1)S(1)}, u32[]{:S(2)}, u32[]{:S(2)}) %collective-permute-start.49) | collective-permute-done | bytes 131104 | tf_op jit(solution)/shard_map/ppermute | solution.py:315
  109.5 6.1 %collective-permute-done.50.refs_5_ = bf16[2,64,512]{2,1,0:T(8,128)(2,1)S(1)} collective-permute-done((bf16[2,64,512]{2,1,0:T(8,128)(2,1)S(1)}, bf16[2,64,512]{2,1,0:T(8,128)(2,1)S(1)}, u32[]{:S(2)}, u32[]{:S(2)}) %collective-permute-start.50) | collective-permute-done | bytes 131104 | tf_op jit(solution)/shard_map/ppermute | solution.py:315
  115.6 2.1 %shard_map.69 = (bf16[2,64,512]{2,1,0:T(8,128)(2,1)S(1)}, bf16[2,64,512]{2,1,0:T(8,128)(2,1)S(1)}, bf16[2,64,512]{2,1,0:T(8,128)(2,1)S(1)}, bf16[2,64,512]{2,1,0...) custom-call(bf16[2,64,512]{2,1,0:T(8,128)(2,1)S(1)} %get-tuple-eleme, ...), custom_call_target="tpu_custom_call" | custom-call | flops 2147483648 | bytes 1048576 | tf_op jit(solution)/shard_map/pallas_call | solution.py:372
  117.7 1.0 collective-permute-start.53
  118.7 2.0 %collective-permute-start.54 = (bf16[2,64,512]{2,1,0:T(8,128)(2,1)S(1)}, bf16[2,64,512]{2,1,0:T(8,128)(2,1)S(1)}, u32[]{:S(2)}, u32[]{:S(2)}) collective-permute-start(bf16[2,64,512]{2,1,0:T(8,128)(2,1)S(1)} %get-tuple-element.141), channel_id=1, source_target_pairs={{0,2},{1,3},{2,0},{3,1},{4,6},{5,7},{6,4},{7,5},{8,10},{9,11},{10,... | collective-permute-start | bytes 393224 | tf_op jit(solution)/shard_map/ppermute | solution.py:315
  120.8 1.1 collective-permute-start.32
  122.0 2.4 %collective-permute-start.34 = (bf16[2,64,256]{2,1,0:T(8,128)(2,1)S(1)}, bf16[2,64,256]{2,1,0:T(8,128)(2,1)S(1)}, u32[]{:S(2)}, u32[]{:S(2)}) collective-permute-start(bf16[2,64,256]{2,1,0:T(8,128)(2,1)S(1)} %get-tuple-element.118), channel_id=1, source_target_pairs={{0,3},{1,2},{2,1},{3,0},{4,7},{5,6},{6,5},{7,4},{8,11},{9,10},{10,... | collective-permute-start | bytes 196616 | tf_op jit(solution)/shard_map/ppermute | solution.py:315
  125.3 2.5 %collective-permute-start.36 = (bf16[2,64,256]{2,1,0:T(8,128)(2,1)S(1)}, bf16[2,64,256]{2,1,0:T(8,128)(2,1)S(1)}, u32[]{:S(2)}, u32[]{:S(2)}) collective-permute-start(bf16[2,64,256]{2,1,0:T(8,128)(2,1)S(1)} %get-tuple-element.120), channel_id=1, source_target_pairs={{0,5},{1,4},{2,7},{3,6},{4,1},{5,0},{6,3},{7,2},{8,13},{9,12},{10,... | collective-permute-start | bytes 196616 | tf_op jit(solution)/shard_map/ppermute | solution.py:315
  127.8 1.9 %collective-permute-start.37 = (bf16[2,64,256]{2,1,0:T(8,128)(2,1)S(1)}, bf16[2,64,256]{2,1,0:T(8,128)(2,1)S(1)}, u32[]{:S(2)}, u32[]{:S(2)}) collective-permute-start(bf16[2,64,256]{2,1,0:T(8,128)(2,1)S(1)} %get-tuple-element.121), channel_id=1, source_target_pairs={{0,6},{1,7},{2,4},{3,5},{4,2},{5,3},{6,0},{7,1},{8,14},{9,15},{10,... | collective-permute-start | bytes 196616 | tf_op jit(solution)/shard_map/ppermute | solution.py:315
  129.7 2.3 %collective-permute-start.38 = (bf16[2,64,256]{2,1,0:T(8,128)(2,1)S(1)}, bf16[2,64,256]{2,1,0:T(8,128)(2,1)S(1)}, u32[]{:S(2)}, u32[]{:S(2)}) collective-permute-start(bf16[2,64,256]{2,1,0:T(8,128)(2,1)S(1)} %get-tuple-element.122), channel_id=1, source_target_pairs={{0,7},{1,6},{2,5},{3,4},{4,3},{5,2},{6,1},{7,0},{8,15},{9,14},{10,... | collective-permute-start | bytes 196616 | tf_op jit(solution)/shard_map/ppermute | solution.py:315
  132.8 2.3 %collective-permute-start.56 = (bf16[2,64,512]{2,1,0:T(8,128)(2,1)S(1)}, bf16[2,64,512]{2,1,0:T(8,128)(2,1)S(1)}, u32[]{:S(2)}, u32[]{:S(2)}) collective-permute-start(bf16[2,64,512]{2,1,0:T(8,128)(2,1)S(1)} %get-tuple-element.143), channel_id=1, source_target_pairs={{0,4},{1,5},{2,6},{3,7},{4,0},{5,1},{6,2},{7,3},{8,12},{9,13},{10,... | collective-permute-start | bytes 393224 | tf_op jit(solution)/shard_map/ppermute | solution.py:315
  135.0 4.8 %collective-permute-done.36.refs_5_ = bf16[2,64,256]{2,1,0:T(8,128)(2,1)S(1)} collective-permute-done((bf16[2,64,256]{2,1,0:T(8,128)(2,1)S(1)}, bf16[2,64,256]{2,1,0:T(8,128)(2,1)S(1)}, u32[]{:S(2)}, u32[]{:S(2)}) %collective-permute-start.36) | collective-permute-done | bytes 65568 | tf_op jit(solution)/shard_map/ppermute | solution.py:315
  139.9 1.2 collective-permute-start.58
  141.1 3.0 %collective-permute-start.59 = (bf16[2,64,512]{2,1,0:T(8,128)(2,1)S(1)}, bf16[2,64,512]{2,1,0:T(8,128)(2,1)S(1)}, u32[]{:S(2)}, u32[]{:S(2)}) collective-permute-start(bf16[2,64,512]{2,1,0:T(8,128)(2,1)S(1)} %get-tuple-element.146), channel_id=1, source_target_pairs={{0,7},{1,6},{2,5},{3,4},{4,3},{5,2},{6,1},{7,0},{8,15},{9,14},{10,... | collective-permute-start | bytes 393224 | tf_op jit(solution)/shard_map/ppermute | solution.py:315
  144.1 1.5 shard_map.65
  145.6 1.1 collective-permute-start.39
  146.7 5.8 %collective-permute-done.56.refs_4_ = bf16[2,64,512]{2,1,0:T(8,128)(2,1)S(1)} collective-permute-done((bf16[2,64,512]{2,1,0:T(8,128)(2,1)S(1)}, bf16[2,64,512]{2,1,0:T(8,128)(2,1)S(1)}, u32[]{:S(2)}, u32[]{:S(2)}) %collective-permute-start.56) | collective-permute-done | bytes 131104 | tf_op jit(solution)/shard_map/ppermute | solution.py:315
  152.5 2.1 %collective-permute-start.40 = (bf16[2,64,256]{2,1,0:T(8,128)(2,1)S(1)}, bf16[2,64,256]{2,1,0:T(8,128)(2,1)S(1)}, u32[]{:S(2)}, u32[]{:S(2)}) collective-permute-start(bf16[2,64,256]{2,1,0:T(8,128)(2,1)S(1)} %get-tuple-element.125), channel_id=1, source_target_pairs={{0,2},{1,3},{2,0},{3,1},{4,6},{5,7},{6,4},{7,5},{8,10},{9,11},{10,... | collective-permute-start | bytes 196616 | tf_op jit(solution)/shard_map/ppermute | solution.py:315
  154.5 1.4 collective-permute-done.57.refs_5_
  155.9 3.9 %collective-permute-start.42 = (bf16[2,64,256]{2,1,0:T(8,128)(2,1)S(1)}, bf16[2,64,256]{2,1,0:T(8,128)(2,1)S(1)}, u32[]{:S(2)}, u32[]{:S(2)}) collective-permute-start(bf16[2,64,256]{2,1,0:T(8,128)(2,1)S(1)} %get-tuple-element.127), channel_id=1, source_target_pairs={{0,4},{1,5},{2,6},{3,7},{4,0},{5,1},{6,2},{7,3},{8,12},{9,13},{10,... | collective-permute-start | bytes 196616 | tf_op jit(solution)/shard_map/ppermute | solution.py:315
  159.8 4.5 %collective-permute-start.43 = (bf16[2,64,256]{2,1,0:T(8,128)(2,1)S(1)}, bf16[2,64,256]{2,1,0:T(8,128)(2,1)S(1)}, u32[]{:S(2)}, u32[]{:S(2)}) collective-permute-start(bf16[2,64,256]{2,1,0:T(8,128)(2,1)S(1)} %get-tuple-element.128), channel_id=1, source_target_pairs={{0,5},{1,4},{2,7},{3,6},{4,1},{5,0},{6,3},{7,2},{8,13},{9,12},{10,... | collective-permute-start | bytes 196616 | tf_op jit(solution)/shard_map/ppermute | solution.py:315
  164.4 1.8 %collective-permute-start.44 = (bf16[2,64,256]{2,1,0:T(8,128)(2,1)S(1)}, bf16[2,64,256]{2,1,0:T(8,128)(2,1)S(1)}, u32[]{:S(2)}, u32[]{:S(2)}) collective-permute-start(bf16[2,64,256]{2,1,0:T(8,128)(2,1)S(1)} %get-tuple-element.129), channel_id=1, source_target_pairs={{0,6},{1,7},{2,4},{3,5},{4,2},{5,3},{6,0},{7,1},{8,14},{9,15},{10,... | collective-permute-start | bytes 196616 | tf_op jit(solution)/shard_map/ppermute | solution.py:315
  166.1 2.7 %collective-permute-start.45 = (bf16[2,64,256]{2,1,0:T(8,128)(2,1)S(1)}, bf16[2,64,256]{2,1,0:T(8,128)(2,1)S(1)}, u32[]{:S(2)}, u32[]{:S(2)}) collective-permute-start(bf16[2,64,256]{2,1,0:T(8,128)(2,1)S(1)} %get-tuple-element.130), channel_id=1, source_target_pairs={{0,7},{1,6},{2,5},{3,4},{4,3},{5,2},{6,1},{7,0},{8,15},{9,14},{10,... | collective-permute-start | bytes 196616 | tf_op jit(solution)/shard_map/ppermute | solution.py:315
  168.8 1.0 shard_map.70.refs_8_
  170.4 2.7 %collective-permute-done.45.refs_7_ = bf16[2,64,256]{2,1,0:T(8,128)(2,1)S(1)} collective-permute-done((bf16[2,64,256]{2,1,0:T(8,128)(2,1)S(1)}, bf16[2,64,256]{2,1,0:T(8,128)(2,1)S(1)}, u32[]{:S(2)}, u32[]{:S(2)}) %collective-permute-start.45) | collective-permute-done | bytes 65568 | tf_op jit(solution)/shard_map/ppermute | solution.py:315
  (82 shorter events, 13.5 us)
Async XLA Ops:
  4.2 20.8 %collective-permute-start.19 = (bf16[2,64,512]{2,1,0:T(8,128)(2,1)S(1)}, bf16[2,64,512]{2,1,0:T(8,128)(2,1)S(1)}, u32[]{:S(2)}, u32[]{:S(2)}) collective-permute-start(bf16[2,64,512]{2,1,0:T(8,128)(2,1)S(1)} %get-tuple-element.101), channel_id=1, source_target_pairs={{0,4},{1,5},{2,6},{3,7},{4,0},{5,1},{6,2},{7,3},{8,12},{9,13},{10,... | collective-permute-start | bytes 393224 | tf_op jit(solution)/shard_map/ppermute | solution.py:315
  8.3 17.6 %collective-permute-start.21 = (bf16[2,64,512]{2,1,0:T(8,128)(2,1)S(1)}, bf16[2,64,512]{2,1,0:T(8,128)(2,1)S(1)}, u32[]{:S(2)}, u32[]{:S(2)}) collective-permute-start(bf16[2,64,512]{2,1,0:T(8,128)(2,1)S(1)} %get-tuple-element.103), channel_id=1, source_target_pairs={{0,6},{1,7},{2,4},{3,5},{4,2},{5,3},{6,0},{7,1},{8,14},{9,15},{10,... | collective-permute-start | bytes 393224 | tf_op jit(solution)/shard_map/ppermute | solution.py:315
  9.7 1.7 copy-start.1
  11.9 15.1 %collective-permute-start.20 = (bf16[2,64,512]{2,1,0:T(8,128)(2,1)S(1)}, bf16[2,64,512]{2,1,0:T(8,128)(2,1)S(1)}, u32[]{:S(2)}, u32[]{:S(2)}) collective-permute-start(bf16[2,64,512]{2,1,0:T(8,128)(2,1)S(1)} %get-tuple-element.102), channel_id=1, source_target_pairs={{0,5},{1,4},{2,7},{3,6},{4,1},{5,0},{6,3},{7,2},{8,13},{9,12},{10,... | collective-permute-start | bytes 393224 | tf_op jit(solution)/shard_map/ppermute | solution.py:315
  15.6 6.9 %collective-permute-start = (bf16[8,2,64,128]{3,2,1,0:T(8,128)(2,1)S(1)}, bf16[8,2,64,128]{3,2,1,0:T(8,128)(2,1)S(1)}, u32[]{:S(2)}, u32[]{:S(2)}) collective-permute-start(bf16[8,2,64,128]{3,2,1,0:T(8,128)(2,1)S(1)} %get-tuple-element.79), channel_id=1, source_target_pairs={{0,8},{8,16},{16,24},{24,0},{1,9},{9,17},{17,25},{25,1},{2,10},{10... | collective-permute-start | bytes 786440 | tf_op jit(solution)/shard_map/ppermute | solution.py:407
  15.7 2.7 %copy-start.3 = (bf16[1,8,8]{2,1,0:T(8,128)(2,1)S(1)}, bf16[1,8,8]{2,1,0:T(8,128)(2,1)}, u32[]{:S(2)}) copy-start(bf16[1,8,8]{2,1,0:T(8,128)(2,1)} %param.8) | copy-start | bytes 388
  15.7 7.6 %collective-permute-start.1 = (bf16[8,2,64,128]{3,2,1,0:T(8,128)(2,1)S(1)}, bf16[8,2,64,128]{3,2,1,0:T(8,128)(2,1)S(1)}, u32[]{:S(2)}, u32[]{:S(2)}) collective-permute-start(bf16[8,2,64,128]{3,2,1,0:T(8,128)(2,1)S(1)} %get-tuple-element.80), channel_id=1, source_target_pairs={{8,0},{16,8},{24,16},{0,24},{9,1},{17,9},{25,17},{1,25},{10,2},{18... | collective-permute-start | bytes 786440 | tf_op jit(solution)/shard_map/ppermute | solution.py:408
  22.5 9.1 %collective-permute-start.22 = (bf16[2,64,512]{2,1,0:T(8,128)(2,1)S(1)}, bf16[2,64,512]{2,1,0:T(8,128)(2,1)S(1)}, u32[]{:S(2)}, u32[]{:S(2)}) collective-permute-start(bf16[2,64,512]{2,1,0:T(8,128)(2,1)S(1)} %get-tuple-element.104), channel_id=1, source_target_pairs={{0,7},{1,6},{2,5},{3,4},{4,3},{5,2},{6,1},{7,0},{8,15},{9,14},{10,... | collective-permute-start | bytes 393224 | tf_op jit(solution)/shard_map/ppermute | solution.py:315
  23.3 10.2 %copy-start = (s32[1,8]{1,0:T(1,128)S(1)}, s32[1,8]{1,0:T(1,128)}, u32[]{:S(2)}) copy-start(s32[1,8]{1,0:T(1,128)} %param.9) | copy-start | bytes 100
  23.3 12.9 %collective-permute-start.16 = (bf16[2,64,512]{2,1,0:T(8,128)(2,1)S(1)}, bf16[2,64,512]{2,1,0:T(8,128)(2,1)S(1)}, u32[]{:S(2)}, u32[]{:S(2)}) collective-permute-start(bf16[2,64,512]{2,1,0:T(8,128)(2,1)S(1)} %get-tuple-element.98), channel_id=1, source_target_pairs={{0,1},{1,0},{2,3},{3,2},{4,5},{5,4},{6,7},{7,6},{8,9},{9,8},{10,11... | collective-permute-start | bytes 393224 | tf_op jit(solution)/shard_map/ppermute | solution.py:315
  25.0 11.5 %collective-permute-start.17 = (bf16[2,64,512]{2,1,0:T(8,128)(2,1)S(1)}, bf16[2,64,512]{2,1,0:T(8,128)(2,1)S(1)}, u32[]{:S(2)}, u32[]{:S(2)}) collective-permute-start(bf16[2,64,512]{2,1,0:T(8,128)(2,1)S(1)} %get-tuple-element.99), channel_id=1, source_target_pairs={{0,2},{1,3},{2,0},{3,1},{4,6},{5,7},{6,4},{7,5},{8,10},{9,11},{10,... | collective-permute-start | bytes 393224 | tf_op jit(solution)/shard_map/ppermute | solution.py:315
  25.9 15.5 %collective-permute-start.18 = (bf16[2,64,512]{2,1,0:T(8,128)(2,1)S(1)}, bf16[2,64,512]{2,1,0:T(8,128)(2,1)S(1)}, u32[]{:S(2)}, u32[]{:S(2)}) collective-permute-start(bf16[2,64,512]{2,1,0:T(8,128)(2,1)S(1)} %get-tuple-element.100), channel_id=1, source_target_pairs={{0,3},{1,2},{2,1},{3,0},{4,7},{5,6},{6,5},{7,4},{8,11},{9,10},{10,... | collective-permute-start | bytes 393224 | tf_op jit(solution)/shard_map/ppermute | solution.py:315
  27.0 15.4 %collective-permute-start.2 = (bf16[2,64,256]{2,1,0:T(8,128)(2,1)S(1)}, bf16[2,64,256]{2,1,0:T(8,128)(2,1)S(1)}, u32[]{:S(2)}, u32[]{:S(2)}) collective-permute-start(bf16[2,64,256]{2,1,0:T(8,128)(2,1)S(1)} %get-tuple-element.82), channel_id=1, source_target_pairs={{0,1},{1,0},{2,3},{3,2},{4,5},{5,4},{6,7},{7,6},{8,9},{9,8},{10,11... | collective-permute-start | bytes 196616 | tf_op jit(solution)/shard_map/ppermute | solution.py:315
  31.6 13.1 %collective-permute-start.3 = (bf16[2,64,256]{2,1,0:T(8,128)(2,1)S(1)}, bf16[2,64,256]{2,1,0:T(8,128)(2,1)S(1)}, u32[]{:S(2)}, u32[]{:S(2)}) collective-permute-start(bf16[2,64,256]{2,1,0:T(8,128)(2,1)S(1)} %get-tuple-element.83), channel_id=1, source_target_pairs={{0,2},{1,3},{2,0},{3,1},{4,6},{5,7},{6,4},{7,5},{8,10},{9,11},{10,... | collective-permute-start | bytes 196616 | tf_op jit(solution)/shard_map/ppermute | solution.py:315
  36.3 12.1 %collective-permute-start.4 = (bf16[2,64,256]{2,1,0:T(8,128)(2,1)S(1)}, bf16[2,64,256]{2,1,0:T(8,128)(2,1)S(1)}, u32[]{:S(2)}, u32[]{:S(2)}) collective-permute-start(bf16[2,64,256]{2,1,0:T(8,128)(2,1)S(1)} %get-tuple-element.84), channel_id=1, source_target_pairs={{0,3},{1,2},{2,1},{3,0},{4,7},{5,6},{6,5},{7,4},{8,11},{9,10},{10,... | collective-permute-start | bytes 196616 | tf_op jit(solution)/shard_map/ppermute | solution.py:315
  36.5 13.4 %collective-permute-start.5 = (bf16[2,64,256]{2,1,0:T(8,128)(2,1)S(1)}, bf16[2,64,256]{2,1,0:T(8,128)(2,1)S(1)}, u32[]{:S(2)}, u32[]{:S(2)}) collective-permute-start(bf16[2,64,256]{2,1,0:T(8,128)(2,1)S(1)} %get-tuple-element.85), channel_id=1, source_target_pairs={{0,4},{1,5},{2,6},{3,7},{4,0},{5,1},{6,2},{7,3},{8,12},{9,13},{10,... | collective-permute-start | bytes 196616 | tf_op jit(solution)/shard_map/ppermute | solution.py:315
  41.4 9.2 %collective-permute-start.6 = (bf16[2,64,256]{2,1,0:T(8,128)(2,1)S(1)}, bf16[2,64,256]{2,1,0:T(8,128)(2,1)S(1)}, u32[]{:S(2)}, u32[]{:S(2)}) collective-permute-start(bf16[2,64,256]{2,1,0:T(8,128)(2,1)S(1)} %get-tuple-element.86), channel_id=1, source_target_pairs={{0,5},{1,4},{2,7},{3,6},{4,1},{5,0},{6,3},{7,2},{8,13},{9,12},{10,... | collective-permute-start | bytes 196616 | tf_op jit(solution)/shard_map/ppermute | solution.py:315
  42.5 9.5 %collective-permute-start.7 = (bf16[2,64,256]{2,1,0:T(8,128)(2,1)S(1)}, bf16[2,64,256]{2,1,0:T(8,128)(2,1)S(1)}, u32[]{:S(2)}, u32[]{:S(2)}) collective-permute-start(bf16[2,64,256]{2,1,0:T(8,128)(2,1)S(1)} %get-tuple-element.87), channel_id=1, source_target_pairs={{0,6},{1,7},{2,4},{3,5},{4,2},{5,3},{6,0},{7,1},{8,14},{9,15},{10,... | collective-permute-start | bytes 196616 | tf_op jit(solution)/shard_map/ppermute | solution.py:315
  44.8 7.5 %collective-permute-start.8 = (bf16[2,64,256]{2,1,0:T(8,128)(2,1)S(1)}, bf16[2,64,256]{2,1,0:T(8,128)(2,1)S(1)}, u32[]{:S(2)}, u32[]{:S(2)}) collective-permute-start(bf16[2,64,256]{2,1,0:T(8,128)(2,1)S(1)} %get-tuple-element.88), channel_id=1, source_target_pairs={{0,7},{1,6},{2,5},{3,4},{4,3},{5,2},{6,1},{7,0},{8,15},{9,14},{10,... | collective-permute-start | bytes 196616 | tf_op jit(solution)/shard_map/ppermute | solution.py:315
  48.4 8.7 %collective-permute-start.23 = (bf16[2,64,512]{2,1,0:T(8,128)(2,1)S(1)}, bf16[2,64,512]{2,1,0:T(8,128)(2,1)S(1)}, u32[]{:S(2)}, u32[]{:S(2)}) collective-permute-start(bf16[2,64,512]{2,1,0:T(8,128)(2,1)S(1)} %get-tuple-element.106), channel_id=1, source_target_pairs={{0,1},{1,0},{2,3},{3,2},{4,5},{5,4},{6,7},{7,6},{8,9},{9,8},{10,11... | collective-permute-start | bytes 393224 | tf_op jit(solution)/shard_map/ppermute | solution.py:315
  49.9 8.3 %collective-permute-start.24 = (bf16[2,64,512]{2,1,0:T(8,128)(2,1)S(1)}, bf16[2,64,512]{2,1,0:T(8,128)(2,1)S(1)}, u32[]{:S(2)}, u32[]{:S(2)}) collective-permute-start(bf16[2,64,512]{2,1,0:T(8,128)(2,1)S(1)} %get-tuple-element.107), channel_id=1, source_target_pairs={{0,2},{1,3},{2,0},{3,1},{4,6},{5,7},{6,4},{7,5},{8,10},{9,11},{10,... | collective-permute-start | bytes 393224 | tf_op jit(solution)/shard_map/ppermute | solution.py:315
  50.6 10.0 %collective-permute-start.25 = (bf16[2,64,512]{2,1,0:T(8,128)(2,1)S(1)}, bf16[2,64,512]{2,1,0:T(8,128)(2,1)S(1)}, u32[]{:S(2)}, u32[]{:S(2)}) collective-permute-start(bf16[2,64,512]{2,1,0:T(8,128)(2,1)S(1)} %get-tuple-element.108), channel_id=1, source_target_pairs={{0,3},{1,2},{2,1},{3,0},{4,7},{5,6},{6,5},{7,4},{8,11},{9,10},{10,... | collective-permute-start | bytes 393224 | tf_op jit(solution)/shard_map/ppermute | solution.py:315
  52.3 14.8 %copy-start.2 = (bf16[2,768,768]{2,1,0:T(8,128)(2,1)S(1)}, bf16[2,768,768]{2,1,0:T(8,128)(2,1)}, u32[]{:S(2)}) copy-start(bf16[2,768,768]{2,1,0:T(8,128)(2,1)} %get-tuple-element.78.refs_2_.refs_17_.refs_9_.refs_5_) | copy-start | bytes 7077892
  53.8 7.5 %collective-permute-start.9 = (bf16[2,64,256]{2,1,0:T(8,128)(2,1)S(1)}, bf16[2,64,256]{2,1,0:T(8,128)(2,1)S(1)}, u32[]{:S(2)}, u32[]{:S(2)}) collective-permute-start(bf16[2,64,256]{2,1,0:T(8,128)(2,1)S(1)} %get-tuple-element.90), channel_id=1, source_target_pairs={{0,1},{1,0},{2,3},{3,2},{4,5},{5,4},{6,7},{7,6},{8,9},{9,8},{10,11... | collective-permute-start | bytes 196616 | tf_op jit(solution)/shard_map/ppermute | solution.py:315
  55.0 8.6 %collective-permute-start.10 = (bf16[2,64,256]{2,1,0:T(8,128)(2,1)S(1)}, bf16[2,64,256]{2,1,0:T(8,128)(2,1)S(1)}, u32[]{:S(2)}, u32[]{:S(2)}) collective-permute-start(bf16[2,64,256]{2,1,0:T(8,128)(2,1)S(1)} %get-tuple-element.91), channel_id=1, source_target_pairs={{0,2},{1,3},{2,0},{3,1},{4,6},{5,7},{6,4},{7,5},{8,10},{9,11},{10,... | collective-permute-start | bytes 196616 | tf_op jit(solution)/shard_map/ppermute | solution.py:315
  57.1 7.3 %collective-permute-start.11 = (bf16[2,64,256]{2,1,0:T(8,128)(2,1)S(1)}, bf16[2,64,256]{2,1,0:T(8,128)(2,1)S(1)}, u32[]{:S(2)}, u32[]{:S(2)}) collective-permute-start(bf16[2,64,256]{2,1,0:T(8,128)(2,1)S(1)} %get-tuple-element.92), channel_id=1, source_target_pairs={{0,3},{1,2},{2,1},{3,0},{4,7},{5,6},{6,5},{7,4},{8,11},{9,10},{10,... | collective-permute-start | bytes 196616 | tf_op jit(solution)/shard_map/ppermute | solution.py:315
  58.2 19.3 %collective-permute-start.26 = (bf16[2,64,512]{2,1,0:T(8,128)(2,1)S(1)}, bf16[2,64,512]{2,1,0:T(8,128)(2,1)S(1)}, u32[]{:S(2)}, u32[]{:S(2)}) collective-permute-start(bf16[2,64,512]{2,1,0:T(8,128)(2,1)S(1)} %get-tuple-element.109), channel_id=1, source_target_pairs={{0,4},{1,5},{2,6},{3,7},{4,0},{5,1},{6,2},{7,3},{8,12},{9,13},{10,... | collective-permute-start | bytes 393224 | tf_op jit(solution)/shard_map/ppermute | solution.py:315
  60.6 30.3 %collective-permute-start.27 = (bf16[2,64,512]{2,1,0:T(8,128)(2,1)S(1)}, bf16[2,64,512]{2,1,0:T(8,128)(2,1)S(1)}, u32[]{:S(2)}, u32[]{:S(2)}) collective-permute-start(bf16[2,64,512]{2,1,0:T(8,128)(2,1)S(1)} %get-tuple-element.110), channel_id=1, source_target_pairs={{0,5},{1,4},{2,7},{3,6},{4,1},{5,0},{6,3},{7,2},{8,13},{9,12},{10,... | collective-permute-start | bytes 393224 | tf_op jit(solution)/shard_map/ppermute | solution.py:315
  61.3 18.0 %collective-permute-start.28 = (bf16[2,64,512]{2,1,0:T(8,128)(2,1)S(1)}, bf16[2,64,512]{2,1,0:T(8,128)(2,1)S(1)}, u32[]{:S(2)}, u32[]{:S(2)}) collective-permute-start(bf16[2,64,512]{2,1,0:T(8,128)(2,1)S(1)} %get-tuple-element.111), channel_id=1, source_target_pairs={{0,6},{1,7},{2,4},{3,5},{4,2},{5,3},{6,0},{7,1},{8,14},{9,15},{10,... | collective-permute-start | bytes 393224 | tf_op jit(solution)/shard_map/ppermute | solution.py:315
  63.6 23.8 %collective-permute-start.12 = (bf16[2,64,256]{2,1,0:T(8,128)(2,1)S(1)}, bf16[2,64,256]{2,1,0:T(8,128)(2,1)S(1)}, u32[]{:S(2)}, u32[]{:S(2)}) collective-permute-start(bf16[2,64,256]{2,1,0:T(8,128)(2,1)S(1)} %get-tuple-element.93), channel_id=1, source_target_pairs={{0,4},{1,5},{2,6},{3,7},{4,0},{5,1},{6,2},{7,3},{8,12},{9,13},{10,... | collective-permute-start | bytes 196616 | tf_op jit(solution)/shard_map/ppermute | solution.py:315
  64.4 24.7 %collective-permute-start.14 = (bf16[2,64,256]{2,1,0:T(8,128)(2,1)S(1)}, bf16[2,64,256]{2,1,0:T(8,128)(2,1)S(1)}, u32[]{:S(2)}, u32[]{:S(2)}) collective-permute-start(bf16[2,64,256]{2,1,0:T(8,128)(2,1)S(1)} %get-tuple-element.95), channel_id=1, source_target_pairs={{0,6},{1,7},{2,4},{3,5},{4,2},{5,3},{6,0},{7,1},{8,14},{9,15},{10,... | collective-permute-start | bytes 196616 | tf_op jit(solution)/shard_map/ppermute | solution.py:315
  77.5 13.5 %collective-permute-start.29 = (bf16[2,64,512]{2,1,0:T(8,128)(2,1)S(1)}, bf16[2,64,512]{2,1,0:T(8,128)(2,1)S(1)}, u32[]{:S(2)}, u32[]{:S(2)}) collective-permute-start(bf16[2,64,512]{2,1,0:T(8,128)(2,1)S(1)} %get-tuple-element.112), channel_id=1, source_target_pairs={{0,7},{1,6},{2,5},{3,4},{4,3},{5,2},{6,1},{7,0},{8,15},{9,14},{10,... | collective-permute-start | bytes 393224 | tf_op jit(solution)/shard_map/ppermute | solution.py:315
  79.2 14.2 %collective-permute-start.13 = (bf16[2,64,256]{2,1,0:T(8,128)(2,1)S(1)}, bf16[2,64,256]{2,1,0:T(8,128)(2,1)S(1)}, u32[]{:S(2)}, u32[]{:S(2)}) collective-permute-start(bf16[2,64,256]{2,1,0:T(8,128)(2,1)S(1)} %get-tuple-element.94), channel_id=1, source_target_pairs={{0,5},{1,4},{2,7},{3,6},{4,1},{5,0},{6,3},{7,2},{8,13},{9,12},{10,... | collective-permute-start | bytes 196616 | tf_op jit(solution)/shard_map/ppermute | solution.py:315
  87.4 7.7 %collective-permute-start.15 = (bf16[2,64,256]{2,1,0:T(8,128)(2,1)S(1)}, bf16[2,64,256]{2,1,0:T(8,128)(2,1)S(1)}, u32[]{:S(2)}, u32[]{:S(2)}) collective-permute-start(bf16[2,64,256]{2,1,0:T(8,128)(2,1)S(1)} %get-tuple-element.96), channel_id=1, source_target_pairs={{0,7},{1,6},{2,5},{3,4},{4,3},{5,2},{6,1},{7,0},{8,15},{9,14},{10,... | collective-permute-start | bytes 196616 | tf_op jit(solution)/shard_map/ppermute | solution.py:315
  89.1 8.1 %collective-permute-start.46 = (bf16[2,64,512]{2,1,0:T(8,128)(2,1)S(1)}, bf16[2,64,512]{2,1,0:T(8,128)(2,1)S(1)}, u32[]{:S(2)}, u32[]{:S(2)}) collective-permute-start(bf16[2,64,512]{2,1,0:T(8,128)(2,1)S(1)} %get-tuple-element.132), channel_id=1, source_target_pairs={{0,1},{1,0},{2,3},{3,2},{4,5},{5,4},{6,7},{7,6},{8,9},{9,8},{10,11... | collective-permute-start | bytes 393224 | tf_op jit(solution)/shard_map/ppermute | solution.py:315
  90.9 8.4 %collective-permute-start.47 = (bf16[2,64,512]{2,1,0:T(8,128)(2,1)S(1)}, bf16[2,64,512]{2,1,0:T(8,128)(2,1)S(1)}, u32[]{:S(2)}, u32[]{:S(2)}) collective-permute-start(bf16[2,64,512]{2,1,0:T(8,128)(2,1)S(1)} %get-tuple-element.133), channel_id=1, source_target_pairs={{0,2},{1,3},{2,0},{3,1},{4,6},{5,7},{6,4},{7,5},{8,10},{9,11},{10,... | collective-permute-start | bytes 393224 | tf_op jit(solution)/shard_map/ppermute | solution.py:315
  91.0 10.9 %collective-permute-start.48 = (bf16[2,64,512]{2,1,0:T(8,128)(2,1)S(1)}, bf16[2,64,512]{2,1,0:T(8,128)(2,1)S(1)}, u32[]{:S(2)}, u32[]{:S(2)}) collective-permute-start(bf16[2,64,512]{2,1,0:T(8,128)(2,1)S(1)} %get-tuple-element.134), channel_id=1, source_target_pairs={{0,3},{1,2},{2,1},{3,0},{4,7},{5,6},{6,5},{7,4},{8,11},{9,10},{10,... | collective-permute-start | bytes 393224 | tf_op jit(solution)/shard_map/ppermute | solution.py:315
  93.4 16.1 %collective-permute-start.49 = (bf16[2,64,512]{2,1,0:T(8,128)(2,1)S(1)}, bf16[2,64,512]{2,1,0:T(8,128)(2,1)S(1)}, u32[]{:S(2)}, u32[]{:S(2)}) collective-permute-start(bf16[2,64,512]{2,1,0:T(8,128)(2,1)S(1)} %get-tuple-element.135), channel_id=1, source_target_pairs={{0,4},{1,5},{2,6},{3,7},{4,0},{5,1},{6,2},{7,3},{8,12},{9,13},{10,... | collective-permute-start | bytes 393224 | tf_op jit(solution)/shard_map/ppermute | solution.py:315
  95.1 14.4 %collective-permute-start.51 = (bf16[2,64,512]{2,1,0:T(8,128)(2,1)S(1)}, bf16[2,64,512]{2,1,0:T(8,128)(2,1)S(1)}, u32[]{:S(2)}, u32[]{:S(2)}) collective-permute-start(bf16[2,64,512]{2,1,0:T(8,128)(2,1)S(1)} %get-tuple-element.137), channel_id=1, source_target_pairs={{0,6},{1,7},{2,4},{3,5},{4,2},{5,3},{6,0},{7,1},{8,14},{9,15},{10,... | collective-permute-start | bytes 393224 | tf_op jit(solution)/shard_map/ppermute | solution.py:315
  97.2 18.4 %collective-permute-start.50 = (bf16[2,64,512]{2,1,0:T(8,128)(2,1)S(1)}, bf16[2,64,512]{2,1,0:T(8,128)(2,1)S(1)}, u32[]{:S(2)}, u32[]{:S(2)}) collective-permute-start(bf16[2,64,512]{2,1,0:T(8,128)(2,1)S(1)} %get-tuple-element.136), channel_id=1, source_target_pairs={{0,5},{1,4},{2,7},{3,6},{4,1},{5,0},{6,3},{7,2},{8,13},{9,12},{10,... | collective-permute-start | bytes 393224 | tf_op jit(solution)/shard_map/ppermute | solution.py:315
  99.3 16.3 %collective-permute-start.52 = (bf16[2,64,512]{2,1,0:T(8,128)(2,1)S(1)}, bf16[2,64,512]{2,1,0:T(8,128)(2,1)S(1)}, u32[]{:S(2)}, u32[]{:S(2)}) collective-permute-start(bf16[2,64,512]{2,1,0:T(8,128)(2,1)S(1)} %get-tuple-element.138), channel_id=1, source_target_pairs={{0,7},{1,6},{2,5},{3,4},{4,3},{5,2},{6,1},{7,0},{8,15},{9,14},{10,... | collective-permute-start | bytes 393224 | tf_op jit(solution)/shard_map/ppermute | solution.py:315
  101.9 18.9 %collective-permute-start.30 = (bf16[8,2,64,128]{3,2,1,0:T(8,128)(2,1)S(1)}, bf16[8,2,64,128]{3,2,1,0:T(8,128)(2,1)S(1)}, u32[]{:S(2)}, u32[]{:S(2)}) collective-permute-start(bf16[8,2,64,128]{3,2,1,0:T(8,128)(2,1)S(1)} %get-tuple-element.113), channel_id=1, source_target_pairs={{0,8},{8,16},{16,24},{24,0},{1,9},{9,17},{17,25},{25,1},{2,10},{10... | collective-permute-start | bytes 786440 | tf_op jit(solution)/shard_map/ppermute | solution.py:407
  109.5 11.2 %collective-permute-start.31 = (bf16[8,2,64,128]{3,2,1,0:T(8,128)(2,1)S(1)}, bf16[8,2,64,128]{3,2,1,0:T(8,128)(2,1)S(1)}, u32[]{:S(2)}, u32[]{:S(2)}) collective-permute-start(bf16[8,2,64,128]{3,2,1,0:T(8,128)(2,1)S(1)} %get-tuple-element.114), channel_id=1, source_target_pairs={{8,0},{16,8},{24,16},{0,24},{9,1},{17,9},{25,17},{1,25},{10,2},{18... | collective-permute-start | bytes 786440 | tf_op jit(solution)/shard_map/ppermute | solution.py:408
  117.7 6.7 %collective-permute-start.53 = (bf16[2,64,512]{2,1,0:T(8,128)(2,1)S(1)}, bf16[2,64,512]{2,1,0:T(8,128)(2,1)S(1)}, u32[]{:S(2)}, u32[]{:S(2)}) collective-permute-start(bf16[2,64,512]{2,1,0:T(8,128)(2,1)S(1)} %get-tuple-element.140), channel_id=1, source_target_pairs={{0,1},{1,0},{2,3},{3,2},{4,5},{5,4},{6,7},{7,6},{8,9},{9,8},{10,11... | collective-permute-start | bytes 393224 | tf_op jit(solution)/shard_map/ppermute | solution.py:315
  118.7 6.6 %collective-permute-start.54 = (bf16[2,64,512]{2,1,0:T(8,128)(2,1)S(1)}, bf16[2,64,512]{2,1,0:T(8,128)(2,1)S(1)}, u32[]{:S(2)}, u32[]{:S(2)}) collective-permute-start(bf16[2,64,512]{2,1,0:T(8,128)(2,1)S(1)} %get-tuple-element.141), channel_id=1, source_target_pairs={{0,2},{1,3},{2,0},{3,1},{4,6},{5,7},{6,4},{7,5},{8,10},{9,11},{10,... | collective-permute-start | bytes 393224 | tf_op jit(solution)/shard_map/ppermute | solution.py:315
  120.8 7.0 %collective-permute-start.32 = (bf16[2,64,256]{2,1,0:T(8,128)(2,1)S(1)}, bf16[2,64,256]{2,1,0:T(8,128)(2,1)S(1)}, u32[]{:S(2)}, u32[]{:S(2)}) collective-permute-start(bf16[2,64,256]{2,1,0:T(8,128)(2,1)S(1)} %get-tuple-element.116), channel_id=1, source_target_pairs={{0,1},{1,0},{2,3},{3,2},{4,5},{5,4},{6,7},{7,6},{8,9},{9,8},{10,11... | collective-permute-start | bytes 196616 | tf_op jit(solution)/shard_map/ppermute | solution.py:315
  121.9 7.8 %collective-permute-start.33 = (bf16[2,64,256]{2,1,0:T(8,128)(2,1)S(1)}, bf16[2,64,256]{2,1,0:T(8,128)(2,1)S(1)}, u32[]{:S(2)}, u32[]{:S(2)}) collective-permute-start(bf16[2,64,256]{2,1,0:T(8,128)(2,1)S(1)} %get-tuple-element.117), channel_id=1, source_target_pairs={{0,2},{1,3},{2,0},{3,1},{4,6},{5,7},{6,4},{7,5},{8,10},{9,11},{10,... | collective-permute-start | bytes 196616 | tf_op jit(solution)/shard_map/ppermute | solution.py:315
  122.0 10.1 %collective-permute-start.34 = (bf16[2,64,256]{2,1,0:T(8,128)(2,1)S(1)}, bf16[2,64,256]{2,1,0:T(8,128)(2,1)S(1)}, u32[]{:S(2)}, u32[]{:S(2)}) collective-permute-start(bf16[2,64,256]{2,1,0:T(8,128)(2,1)S(1)} %get-tuple-element.118), channel_id=1, source_target_pairs={{0,3},{1,2},{2,1},{3,0},{4,7},{5,6},{6,5},{7,4},{8,11},{9,10},{10,... | collective-permute-start | bytes 196616 | tf_op jit(solution)/shard_map/ppermute | solution.py:315
  124.4 8.4 %collective-permute-start.35 = (bf16[2,64,256]{2,1,0:T(8,128)(2,1)S(1)}, bf16[2,64,256]{2,1,0:T(8,128)(2,1)S(1)}, u32[]{:S(2)}, u32[]{:S(2)}) collective-permute-start(bf16[2,64,256]{2,1,0:T(8,128)(2,1)S(1)} %get-tuple-element.119), channel_id=1, source_target_pairs={{0,4},{1,5},{2,6},{3,7},{4,0},{5,1},{6,2},{7,3},{8,12},{9,13},{10,... | collective-permute-start | bytes 196616 | tf_op jit(solution)/shard_map/ppermute | solution.py:315
  125.3 14.5 %collective-permute-start.36 = (bf16[2,64,256]{2,1,0:T(8,128)(2,1)S(1)}, bf16[2,64,256]{2,1,0:T(8,128)(2,1)S(1)}, u32[]{:S(2)}, u32[]{:S(2)}) collective-permute-start(bf16[2,64,256]{2,1,0:T(8,128)(2,1)S(1)} %get-tuple-element.120), channel_id=1, source_target_pairs={{0,5},{1,4},{2,7},{3,6},{4,1},{5,0},{6,3},{7,2},{8,13},{9,12},{10,... | collective-permute-start | bytes 196616 | tf_op jit(solution)/shard_map/ppermute | solution.py:315
  127.8 12.1 %collective-permute-start.37 = (bf16[2,64,256]{2,1,0:T(8,128)(2,1)S(1)}, bf16[2,64,256]{2,1,0:T(8,128)(2,1)S(1)}, u32[]{:S(2)}, u32[]{:S(2)}) collective-permute-start(bf16[2,64,256]{2,1,0:T(8,128)(2,1)S(1)} %get-tuple-element.121), channel_id=1, source_target_pairs={{0,6},{1,7},{2,4},{3,5},{4,2},{5,3},{6,0},{7,1},{8,14},{9,15},{10,... | collective-permute-start | bytes 196616 | tf_op jit(solution)/shard_map/ppermute | solution.py:315
  129.7 11.4 %collective-permute-start.38 = (bf16[2,64,256]{2,1,0:T(8,128)(2,1)S(1)}, bf16[2,64,256]{2,1,0:T(8,128)(2,1)S(1)}, u32[]{:S(2)}, u32[]{:S(2)}) collective-permute-start(bf16[2,64,256]{2,1,0:T(8,128)(2,1)S(1)} %get-tuple-element.122), channel_id=1, source_target_pairs={{0,7},{1,6},{2,5},{3,4},{4,3},{5,2},{6,1},{7,0},{8,15},{9,14},{10,... | collective-permute-start | bytes 196616 | tf_op jit(solution)/shard_map/ppermute | solution.py:315
  132.1 13.5 %collective-permute-start.55 = (bf16[2,64,512]{2,1,0:T(8,128)(2,1)S(1)}, bf16[2,64,512]{2,1,0:T(8,128)(2,1)S(1)}, u32[]{:S(2)}, u32[]{:S(2)}) collective-permute-start(bf16[2,64,512]{2,1,0:T(8,128)(2,1)S(1)} %get-tuple-element.142), channel_id=1, source_target_pairs={{0,3},{1,2},{2,1},{3,0},{4,7},{5,6},{6,5},{7,4},{8,11},{9,10},{10,... | collective-permute-start | bytes 393224 | tf_op jit(solution)/shard_map/ppermute | solution.py:315
  132.8 19.7 %collective-permute-start.56 = (bf16[2,64,512]{2,1,0:T(8,128)(2,1)S(1)}, bf16[2,64,512]{2,1,0:T(8,128)(2,1)S(1)}, u32[]{:S(2)}, u32[]{:S(2)}) collective-permute-start(bf16[2,64,512]{2,1,0:T(8,128)(2,1)S(1)} %get-tuple-element.143), channel_id=1, source_target_pairs={{0,4},{1,5},{2,6},{3,7},{4,0},{5,1},{6,2},{7,3},{8,12},{9,13},{10,... | collective-permute-start | bytes 393224 | tf_op jit(solution)/shard_map/ppermute | solution.py:315
  139.9 16.1 %collective-permute-start.57 = (bf16[2,64,512]{2,1,0:T(8,128)(2,1)S(1)}, bf16[2,64,512]{2,1,0:T(8,128)(2,1)S(1)}, u32[]{:S(2)}, u32[]{:S(2)}) collective-permute-start(bf16[2,64,512]{2,1,0:T(8,128)(2,1)S(1)} %get-tuple-element.144), channel_id=1, source_target_pairs={{0,5},{1,4},{2,7},{3,6},{4,1},{5,0},{6,3},{7,2},{8,13},{9,12},{10,... | collective-permute-start | bytes 393224 | tf_op jit(solution)/shard_map/ppermute | solution.py:315
  139.9 16.1 %collective-permute-start.58 = (bf16[2,64,512]{2,1,0:T(8,128)(2,1)S(1)}, bf16[2,64,512]{2,1,0:T(8,128)(2,1)S(1)}, u32[]{:S(2)}, u32[]{:S(2)}) collective-permute-start(bf16[2,64,512]{2,1,0:T(8,128)(2,1)S(1)} %get-tuple-element.145), channel_id=1, source_target_pairs={{0,6},{1,7},{2,4},{3,5},{4,2},{5,3},{6,0},{7,1},{8,14},{9,15},{10,... | collective-permute-start | bytes 393224 | tf_op jit(solution)/shard_map/ppermute | solution.py:315
  141.1 18.7 %collective-permute-start.59 = (bf16[2,64,512]{2,1,0:T(8,128)(2,1)S(1)}, bf16[2,64,512]{2,1,0:T(8,128)(2,1)S(1)}, u32[]{:S(2)}, u32[]{:S(2)}) collective-permute-start(bf16[2,64,512]{2,1,0:T(8,128)(2,1)S(1)} %get-tuple-element.146), channel_id=1, source_target_pairs={{0,7},{1,6},{2,5},{3,4},{4,3},{5,2},{6,1},{7,0},{8,15},{9,14},{10,... | collective-permute-start | bytes 393224 | tf_op jit(solution)/shard_map/ppermute | solution.py:315
  145.6 18.8 %collective-permute-start.39 = (bf16[2,64,256]{2,1,0:T(8,128)(2,1)S(1)}, bf16[2,64,256]{2,1,0:T(8,128)(2,1)S(1)}, u32[]{:S(2)}, u32[]{:S(2)}) collective-permute-start(bf16[2,64,256]{2,1,0:T(8,128)(2,1)S(1)} %get-tuple-element.124), channel_id=1, source_target_pairs={{0,1},{1,0},{2,3},{3,2},{4,5},{5,4},{6,7},{7,6},{8,9},{9,8},{10,11... | collective-permute-start | bytes 196616 | tf_op jit(solution)/shard_map/ppermute | solution.py:315
  152.5 13.7 %collective-permute-start.40 = (bf16[2,64,256]{2,1,0:T(8,128)(2,1)S(1)}, bf16[2,64,256]{2,1,0:T(8,128)(2,1)S(1)}, u32[]{:S(2)}, u32[]{:S(2)}) collective-permute-start(bf16[2,64,256]{2,1,0:T(8,128)(2,1)S(1)} %get-tuple-element.125), channel_id=1, source_target_pairs={{0,2},{1,3},{2,0},{3,1},{4,6},{5,7},{6,4},{7,5},{8,10},{9,11},{10,... | collective-permute-start | bytes 196616 | tf_op jit(solution)/shard_map/ppermute | solution.py:315
  155.9 13.9 %collective-permute-start.41 = (bf16[2,64,256]{2,1,0:T(8,128)(2,1)S(1)}, bf16[2,64,256]{2,1,0:T(8,128)(2,1)S(1)}, u32[]{:S(2)}, u32[]{:S(2)}) collective-permute-start(bf16[2,64,256]{2,1,0:T(8,128)(2,1)S(1)} %get-tuple-element.126), channel_id=1, source_target_pairs={{0,3},{1,2},{2,1},{3,0},{4,7},{5,6},{6,5},{7,4},{8,11},{9,10},{10,... | collective-permute-start | bytes 196616 | tf_op jit(solution)/shard_map/ppermute | solution.py:315
  155.9 13.9 %collective-permute-start.42 = (bf16[2,64,256]{2,1,0:T(8,128)(2,1)S(1)}, bf16[2,64,256]{2,1,0:T(8,128)(2,1)S(1)}, u32[]{:S(2)}, u32[]{:S(2)}) collective-permute-start(bf16[2,64,256]{2,1,0:T(8,128)(2,1)S(1)} %get-tuple-element.127), channel_id=1, source_target_pairs={{0,4},{1,5},{2,6},{3,7},{4,0},{5,1},{6,2},{7,3},{8,12},{9,13},{10,... | collective-permute-start | bytes 196616 | tf_op jit(solution)/shard_map/ppermute | solution.py:315
  159.8 10.1 %collective-permute-start.43 = (bf16[2,64,256]{2,1,0:T(8,128)(2,1)S(1)}, bf16[2,64,256]{2,1,0:T(8,128)(2,1)S(1)}, u32[]{:S(2)}, u32[]{:S(2)}) collective-permute-start(bf16[2,64,256]{2,1,0:T(8,128)(2,1)S(1)} %get-tuple-element.128), channel_id=1, source_target_pairs={{0,5},{1,4},{2,7},{3,6},{4,1},{5,0},{6,3},{7,2},{8,13},{9,12},{10,... | collective-permute-start | bytes 196616 | tf_op jit(solution)/shard_map/ppermute | solution.py:315
  164.4 6.1 %collective-permute-start.44 = (bf16[2,64,256]{2,1,0:T(8,128)(2,1)S(1)}, bf16[2,64,256]{2,1,0:T(8,128)(2,1)S(1)}, u32[]{:S(2)}, u32[]{:S(2)}) collective-permute-start(bf16[2,64,256]{2,1,0:T(8,128)(2,1)S(1)} %get-tuple-element.129), channel_id=1, source_target_pairs={{0,6},{1,7},{2,4},{3,5},{4,2},{5,3},{6,0},{7,1},{8,14},{9,15},{10,... | collective-permute-start | bytes 196616 | tf_op jit(solution)/shard_map/ppermute | solution.py:315
  166.1 7.0 %collective-permute-start.45 = (bf16[2,64,256]{2,1,0:T(8,128)(2,1)S(1)}, bf16[2,64,256]{2,1,0:T(8,128)(2,1)S(1)}, u32[]{:S(2)}, u32[]{:S(2)}) collective-permute-start(bf16[2,64,256]{2,1,0:T(8,128)(2,1)S(1)} %get-tuple-element.130), channel_id=1, source_target_pairs={{0,7},{1,6},{2,5},{3,4},{4,3},{5,2},{6,1},{7,0},{8,15},{9,14},{10,... | collective-permute-start | bytes 196616 | tf_op jit(solution)/shard_map/ppermute | solution.py:315

commit v3 on v2

--- a/solution.py
+++ b/solution.py
@@ -94,7 +94,9 @@
 SMEM = pl.BlockSpec(memory_space=pltpu.SMEM)
 HBM = pl.BlockSpec(memory_space=pltpu.HBM)
 KERNEL_BYTES = 24 << 20
-FIRST_BYTES = 50 << 20
+FIRST_BYTES = 53 << 20
+LOAD_BYTES = 50 << 20
+PIECES = 1
 KERNEL_FLOPS = 1 << 31
 
 
@@ -131,46 +133,56 @@
     )
 
 
-def load_and_solve(ks, plane_size, rows, first, columns, traces_ref, sources_ref, operators_ref, *refs):
-    blocks, (traces, sources, operators, sems) = refs[: len(ks)], refs[len(ks) :]
-    wanted = [slice(first, first + columns)]
-    unwanted = [slice(0, first), slice(first + columns, operators.shape[-1])]
-    unwanted = [c for c in unwanted if c.stop > c.start]
-    others = [k for k in range(plane_size) if k not in ks]
-
-    def rows_of(source, target, which):
-        return [
-            (source.at[:, pl.ds(row_start(k, rows), rows), :], target.at[k]) for k in which
-        ]
-
-    def operators_of(which):
-        return [
-            (operators_ref.at[part, :, c], operators.at[part, :, c])
-            for c in which
-            for part in range(2)
-        ]
-
-    needed = rows_of(traces_ref, traces, ks) + operators_of(wanted)
-    late = rows_of(sources_ref, sources, ks)
-    rest = rows_of(traces_ref, traces, others) + operators_of(unwanted)
-    rest += rows_of(sources_ref, sources, others)
+def start_all(pairs, sems):
     copies = [
-        pltpu.make_async_copy(source, target, sems.at[n])
-        for n, (source, target) in enumerate(needed + late + rest)
+        pltpu.make_async_copy(source, target, sems.at[n]) for n, (source, target) in enumerate(pairs)
     ]
     for copy in copies:
         copy.start()
-    for copy in copies[: len(needed)]:
+    return copies
+
+
+def load_and_solve(ks, rows, first, columns, traces_ref, sources_ref, operators_ref, *refs):
+    blocks, operators, (traces, sources, sems) = refs[: len(ks)], refs[len(ks)], refs[-3:]
+    wanted = pl.ds(first, columns)
+    here = [pl.ds(row_start(k, rows), rows) for k in ks]
+    depth = operators.shape[1] // PIECES
+    depths = [slice(n * depth, (n + 1) * depth) for n in range(PIECES)]
+    pairs = [(traces_ref.at[:, r, :], traces.at[n]) for n, r in enumerate(here)]
+    for d in depths:
+        for part in range(2):
+            pairs.append((operators_ref.at[part, d, wanted], operators.at[part, d]))
+    pairs += [(sources_ref.at[:, r, wanted], sources.at[n]) for n, r in enumerate(here)]
+    copies = start_all(pairs, sems)
+    rows_here, pieces, late = copies[: len(ks)], copies[len(ks) : -len(ks)], copies[-len(ks) :]
+    for copy in rows_here:
         copy.wait()
-    real, imag = (jnp.concatenate([traces[k, part] for k in ks], axis=0) for part in range(2))
-    results = [
-        part_products(part, real, imag, [operators[p, :, wanted[0]] for p in range(2)])
-        for part in range(2)
-    ]
-    for copy in copies[len(needed) : len(needed) + len(late)]:
+    results = [0.0, 0.0]
+    for n, d in enumerate(depths):
+        for copy in pieces[2 * n : 2 * n + 2]:
+            copy.wait()
+        real, imag = (
+            jnp.concatenate([traces[k, part, :, d] for k in range(len(ks))], axis=0)
+            for part in range(2)
+        )
+        for part in range(2):
+            results[part] = results[part] + part_products(
+                part, real, imag, [operators[p, d] for p in range(2)]
+            )
+    for copy in late:
         copy.wait()
-    finish(ks, rows, wanted[0], pick_block, results, sources, blocks)
-    for copy in copies[len(needed) + len(late) :]:
+    finish(range(len(ks)), rows, slice(0, columns), pick_block, results, sources, blocks)
+
+
+def load_rest(
+    plane_size, rows, first, columns, traces_ref, sources_ref, operators_ref, traces, sources, operators, sems
+):
+    pairs = []
+    for source, target in ((traces_ref, traces), (sources_ref, sources)):
+        for k in range(plane_size):
+            pairs.append((source.at[:, pl.ds(row_start(k, rows), rows), :], target.at[k]))
+    pairs.append((operators_ref.at[:, :, pl.ds(first, columns)], operators))
+    for copy in start_all(pairs, sems):
         copy.wait()
 
 
@@ -201,7 +213,7 @@
     for real, imag in pieces:
         depth = slice(start, start + real.shape[-1])
         start = depth.stop
-        operators = [operators_ref[part, depth, wanted] for part in range(2)]
+        operators = [operators_ref[part, depth] for part in range(2)]
         for part in range(2):
             results[part] = results[part] + part_products(part, real, imag, operators)
     finish(ks, rows, wanted, pick, results, sources, outputs)
@@ -339,7 +351,7 @@
     }
     solved = {"x": ([face] * 2, pick_face), "yz": (blocks_of["yz"], pick_block)}
 
-    placed = []
+    placed = {}
 
     def solve(group, sweep, ks, incoming):
         first, columns = groups[group]
@@ -347,26 +359,38 @@
         if group == "yz":
             out_shape = out_shape[: len(ks)]
         if not placed:
-            by_block = jax.ShapeDtypeStruct((plane_size, 2, rows, columns_all), dtype)
-            results = call(
-                functools.partial(load_and_solve, ks, plane_size, rows, first, columns),
+            *blocks, placed[group] = call(
+                functools.partial(load_and_solve, ks, rows, first, columns),
                 [HBM] * 3,
-                out_shape
-                + [by_block, by_block, jax.ShapeDtypeStruct(operators.shape, dtype)],
-                scratch=[pltpu.SemaphoreType.DMA((2 * plane_size + 6,))],
+                out_shape + [jax.ShapeDtypeStruct((2, columns_all, columns), dtype)],
+                scratch=[
+                    pltpu.VMEM((len(ks), 2, rows, columns_all), dtype),
+                    pltpu.VMEM((len(ks), 2, rows, columns), dtype),
+                    pltpu.SemaphoreType.DMA((2 * len(ks) + 2 * PIECES,)),
+                ],
                 limit=FIRST_BYTES,
             )(trace_rows, source_rows, operators)
-            placed.extend(results[len(ks) :])
-            return results[: len(ks)]
+            return blocks
         if sweep == 0:
-            arrays = [placed[0]]
+            arrays = [placed["traces"]]
         else:
             arrays = [incoming[g][k] for g in ("x", "yz") for k in ks]
         return call(
             functools.partial(solve_blocks, ks, rows, first, columns, pick, 1 if sweep == 0 else 2),
             [VMEM] * (len(arrays) + 2),
             out_shape,
-        )(*arrays, *placed[1:])
+        )(*arrays, placed["sources"], placed[group])
+
+    def load():
+        first, columns = groups["x"]
+        by_block = jax.ShapeDtypeStruct((plane_size, 2, rows, columns_all), dtype)
+        placed["traces"], placed["sources"], placed["x"] = call(
+            functools.partial(load_rest, plane_size, rows, first, columns),
+            [HBM] * 3,
+            [by_block, by_block, jax.ShapeDtypeStruct((2, columns_all, columns), dtype)],
+            scratch=[pltpu.SemaphoreType.DMA((2 * plane_size + 1,))],
+            limit=LOAD_BYTES,
+        )(trace_rows, source_rows, operators)
 
     def mix(group, gathered, weights):
         return call(
@@ -402,6 +426,8 @@
         for ks in row_groups(count_y, count_z):
             for k, block in zip(ks, solve("yz", sweep, ks, incoming)):
                 out_yz[k] = block
+            if len(placed) == 1:
+                load()
         gathered_yz = exchange(out_yz, count_y, count_z)
         low, high = solve("x", sweep, tuple(range(plane_size)), incoming)
         from_low = lax.ppermute(high, "gx", forward)

time: 174 us -> 173 us (level)
  waiting for transfers between devices: 51.6 us -> 48.6 us
  starting transfers between devices: 98.6 us -> 101 us
    ppermute x56, waiting for transfers between devices: 47.5 us -> 44.5 us  [exchange(): lax.ppermute(blocks[k], ('gy', 'gz'), [(p, p ^ k) for p in range(plane_si...]
    ppermute x56, starting transfers between devices: 96.7 us -> 99.1 us  [exchange(): lax.ppermute(blocks[k], ('gy', 'gz'), [(p, p ^ k) for p in range(plane_si...]
    pallas_call x1 -> x2, Pallas kernels: 4.19 us -> 5.7 us  [the longest x1 3.35 us: solve(): call(functools.partial(load_and_solve, ks, rows, first, columns), [HBM] *...]
  transfers between devices with their start and end apart: 60 -> 60, of which waited for: 15 -> 16; matrix products, arithmetic and copies ran while one was open for 0% -> 0% of each run, Pallas kernels for 10% -> 11%
where the time goes in v3:
time: 173 us
  starting transfers between devices  101 us (58%)
  waiting for transfers between devices  48.6 us (28%)
  Pallas kernels  23.3 us (13%)
    ppermute x56, starting transfers between devices, exchange(): lax.ppermute(blocks[k], ('gy', 'gz'), [(p, p ^ k) for p in range(plane_si...  99.1 us
    ppermute x56, waiting for transfers between devices, exchange(): lax.ppermute(blocks[k], ('gy', 'gz'), [(p, p ^ k) for p in range(plane_si...  44.5 us
    pallas_call x4, Pallas kernels, mix(): call(functools.partial(mix_blocks, plane_size, plans[group]), [VMEM] * pl...  7.15 us
    pallas_call x7, Pallas kernels, solve(): call(functools.partial(solve_blocks, ks, rows, first, columns, pick, 1 if...  5.74 us
    ppermute x2, waiting for transfers between devices, few_subdomains(): from_low = lax.ppermute(high, 'gx', forward)  4.07 us
  transfers between devices with their start and end apart: 60, of which 16 were waited for; matrix products, arithmetic and copies ran while one was open for 0% of the time, Pallas kernels for 11%

profile of v3, /device:TPU:0, one launch (start us, length us, event | category | flops | bytes accessed | tf_op | source)
XLA Modules:
  0.0 173.3 jit_solution(1260405686127827321)
XLA Ops:
  0.0 3.4 %shard_map.60 = (bf16[2,64,512]{2,1,0:T(8,128)(2,1)S(1)}, bf16[2,64,512]{2,1,0:T(8,128)(2,1)S(1)}, bf16[2,768,512]{2,1,0:T(8,128)(2,1)}) custom-call(bf16[2,512,768]{2,1,0:T(8,128)(2,1)} %bitcast.13, bf16[2,512,768]{2,1,0:T(8,128)(2,1)} %bitcast.15, bf16[2,768,768]{2,1,0:T(8,128)(2,1)} %bitcast.11), custom_call_target="tpu_custom_call" | custom-call | flops 2147483648 | bytes 1048576 | tf_op jit(solution)/shard_map/pallas_call | solution.py:362
  3.4 4.1 %collective-permute-start.19 = (bf16[2,64,512]{2,1,0:T(8,128)(2,1)S(1)}, bf16[2,64,512]{2,1,0:T(8,128)(2,1)S(1)}, u32[]{:S(2)}, u32[]{:S(2)}) collective-permute-start(bf16[2,64,512]{2,1,0:T(8,128)(2,1)S(1)} %get-tuple-element.103), channel_id=1, source_target_pairs={{0,4},{1,5},{2,6},{3,7},{4,0},{5,1},{6,2},{7,3},{8,12},{9,13},{10,... | collective-permute-start | bytes 393224 | tf_op jit(solution)/shard_map/ppermute | solution.py:327
  7.5 1.3 collective-permute-start.21
  8.8 2.3 %shard_map.55 = (bf16[8,2,64,768]{3,2,1,0:T(8,128)(2,1)S(1)}, bf16[8,2,64,768]{3,2,1,0:T(8,128)(2,1)S(1)}, bf16[2,768,256]{2,1,0:T(8,128)(2,1)S(1)}) custom-call(bf16[2,512,768]{2,1,0:T(8,128)(2,1)} %bitcast.14, bf16[2,512,768]{2,1,0:T(8,128)(2,1)} %bitcast.16, bf16[2,768,768]{2,1,0:T(8,128)(2,1)} %bitcast.12), custom_call_target="tpu_custom_call" | custom-call | flops 2147483648 | bytes 1048576 | tf_op jit(solution)/shard_map/pallas_call | solution.py:387
  11.8 2.7 %collective-permute-start.20 = (bf16[2,64,512]{2,1,0:T(8,128)(2,1)S(1)}, bf16[2,64,512]{2,1,0:T(8,128)(2,1)S(1)}, u32[]{:S(2)}, u32[]{:S(2)}) collective-permute-start(bf16[2,64,512]{2,1,0:T(8,128)(2,1)S(1)} %get-tuple-element.104), channel_id=1, source_target_pairs={{0,5},{1,4},{2,7},{3,6},{4,1},{5,0},{6,3},{7,2},{8,13},{9,12},{10,... | collective-permute-start | bytes 393224 | tf_op jit(solution)/shard_map/ppermute | solution.py:327
  14.5 1.0 shard_map.56
  15.6 1.7 collective-permute-start.1
  17.3 1.0 shard_map.61
  18.3 4.1 %collective-permute-done.from_low_ref = bf16[8,2,64,128]{3,2,1,0:T(8,128)(2,1)S(1)} collective-permute-done((bf16[8,2,64,128]{3,2,1,0:T(8,128)(2,1)S(1)}, bf16[8,2,64,128]{3,2,1,0:T(8,128)(2,1)S(1)}, u32[]{:S(2)}, u32[]{:S(2)}) %collective-permute-start) | collective-permute-done | bytes 262176 | tf_op jit(solution)/shard_map/ppermute | solution.py:433
  22.4 1.2 collective-permute-start.22
  23.5 1.5 collective-permute-start.16
  25.8 1.4 collective-permute-start.18
  27.2 1.5 collective-permute-start.2
  28.7 2.7 %collective-permute-done.22.refs_7_ = bf16[2,64,512]{2,1,0:T(8,128)(2,1)S(1)} collective-permute-done((bf16[2,64,512]{2,1,0:T(8,128)(2,1)S(1)}, bf16[2,64,512]{2,1,0:T(8,128)(2,1)S(1)}, u32[]{:S(2)}, u32[]{:S(2)}) %collective-permute-start.22) | collective-permute-done | bytes 131104 | tf_op jit(solution)/shard_map/ppermute | solution.py:327
  31.5 1.9 %collective-permute-start.3 = (bf16[2,64,256]{2,1,0:T(8,128)(2,1)S(1)}, bf16[2,64,256]{2,1,0:T(8,128)(2,1)S(1)}, u32[]{:S(2)}, u32[]{:S(2)}) collective-permute-start(bf16[2,64,256]{2,1,0:T(8,128)(2,1)S(1)} %get-tuple-element.84), channel_id=1, source_target_pairs={{0,2},{1,3},{2,0},{3,1},{4,6},{5,7},{6,4},{7,5},{8,10},{9,11},{10,... | collective-permute-start | bytes 196616 | tf_op jit(solution)/shard_map/ppermute | solution.py:327
  33.4 2.7 %shard_map.58.refs_8_ = f32[5,8,8]{2,1,0:T(8,128)S(1)} custom-call(f32[8,8]{1,0:T(8,128)S(1)} %bitcast_convert_fusion.coupling_ref, s32[8]{0:T(128)S(1)} %bitcast.10), custom_call_target="tpu_custom_call" | custom-call | flops 2147483648 | bytes 1048576 | tf_op jit(solution)/shard_map/pallas_call | solution.py:413
  36.2 3.5 %collective-permute-start.5 = (bf16[2,64,256]{2,1,0:T(8,128)(2,1)S(1)}, bf16[2,64,256]{2,1,0:T(8,128)(2,1)S(1)}, u32[]{:S(2)}, u32[]{:S(2)}) collective-permute-start(bf16[2,64,256]{2,1,0:T(8,128)(2,1)S(1)} %get-tuple-element.86), channel_id=1, source_target_pairs={{0,4},{1,5},{2,6},{3,7},{4,0},{5,1},{6,2},{7,3},{8,12},{9,13},{10,... | collective-permute-start | bytes 196616 | tf_op jit(solution)/shard_map/ppermute | solution.py:327
  39.8 1.1 collective-permute-start.6
  40.9 2.3 %collective-permute-start.7 = (bf16[2,64,256]{2,1,0:T(8,128)(2,1)S(1)}, bf16[2,64,256]{2,1,0:T(8,128)(2,1)S(1)}, u32[]{:S(2)}, u32[]{:S(2)}) collective-permute-start(bf16[2,64,256]{2,1,0:T(8,128)(2,1)S(1)} %get-tuple-element.88), channel_id=1, source_target_pairs={{0,6},{1,7},{2,4},{3,5},{4,2},{5,3},{6,0},{7,1},{8,14},{9,15},{10,... | collective-permute-start | bytes 196616 | tf_op jit(solution)/shard_map/ppermute | solution.py:327
  43.2 1.5 collective-permute-start.8
  44.7 2.1 %shard_map.63 = (bf16[2,64,512]{2,1,0:T(8,128)(2,1)S(1)}, bf16[2,64,512]{2,1,0:T(8,128)(2,1)S(1)}, bf16[2,64,512]{2,1,0:T(8,128)(2,1)S(1)}, bf16[2,64,512]{2,1,0...) custom-call(bf16[2,64,512]{2,1,0:T(8,128)(2,1)S(1)} %get-tuple-eleme, ...), custom_call_target="tpu_custom_call" | custom-call | flops 2147483648 | bytes 1048576 | tf_op jit(solution)/shard_map/pallas_call | solution.py:396
  46.8 1.5 collective-permute-start.23
  48.8 1.6 collective-permute-start.25
  50.7 1.5 shard_map.59
  52.2 1.2 collective-permute-start.9
  53.4 2.0 %collective-permute-start.10 = (bf16[2,64,256]{2,1,0:T(8,128)(2,1)S(1)}, bf16[2,64,256]{2,1,0:T(8,128)(2,1)S(1)}, u32[]{:S(2)}, u32[]{:S(2)}) collective-permute-start(bf16[2,64,256]{2,1,0:T(8,128)(2,1)S(1)} %get-tuple-element.92), channel_id=1, source_target_pairs={{0,2},{1,3},{2,0},{3,1},{4,6},{5,7},{6,4},{7,5},{8,10},{9,11},{10,... | collective-permute-start | bytes 196616 | tf_op jit(solution)/shard_map/ppermute | solution.py:327
  55.4 1.4 collective-permute-start.11
  56.8 2.2 %collective-permute-start.26 = (bf16[2,64,512]{2,1,0:T(8,128)(2,1)S(1)}, bf16[2,64,512]{2,1,0:T(8,128)(2,1)S(1)}, u32[]{:S(2)}, u32[]{:S(2)}) collective-permute-start(bf16[2,64,512]{2,1,0:T(8,128)(2,1)S(1)} %get-tuple-element.111), channel_id=1, source_target_pairs={{0,4},{1,5},{2,6},{3,7},{4,0},{5,1},{6,2},{7,3},{8,12},{9,13},{10,... | collective-permute-start | bytes 393224 | tf_op jit(solution)/shard_map/ppermute | solution.py:327
  59.8 3.3 %collective-permute-start.29 = (bf16[2,64,512]{2,1,0:T(8,128)(2,1)S(1)}, bf16[2,64,512]{2,1,0:T(8,128)(2,1)S(1)}, u32[]{:S(2)}, u32[]{:S(2)}) collective-permute-start(bf16[2,64,512]{2,1,0:T(8,128)(2,1)S(1)} %get-tuple-element.114), channel_id=1, source_target_pairs={{0,7},{1,6},{2,5},{3,4},{4,3},{5,2},{6,1},{7,0},{8,15},{9,14},{10,... | collective-permute-start | bytes 393224 | tf_op jit(solution)/shard_map/ppermute | solution.py:327
  63.6 3.0 %collective-permute-start.15 = (bf16[2,64,256]{2,1,0:T(8,128)(2,1)S(1)}, bf16[2,64,256]{2,1,0:T(8,128)(2,1)S(1)}, u32[]{:S(2)}, u32[]{:S(2)}) collective-permute-start(bf16[2,64,256]{2,1,0:T(8,128)(2,1)S(1)} %get-tuple-element.97), channel_id=1, source_target_pairs={{0,7},{1,6},{2,5},{3,4},{4,3},{5,2},{6,1},{7,0},{8,15},{9,14},{10,... | collective-permute-start | bytes 196616 | tf_op jit(solution)/shard_map/ppermute | solution.py:327
  66.6 1.0 shard_map.67
  67.7 10.0 %collective-permute-done.27.refs_13_.refs_2_ = bf16[2,64,512]{2,1,0:T(8,128)(2,1)S(1)} collective-permute-done((bf16[2,64,512]{2,1,0:T(8,128)(2,1)S(1)}, bf16[2,64,512]{2,1,0:T(8,128)(2,1)S(1)}, u32[]{:S(2)}, u32[]{:S(2)}) %collective-permute-start.27) | collective-permute-done | bytes 131104 | tf_op jit(solution)/shard_map/ppermute | solution.py:327
  77.7 1.5 collective-permute-start.28
  79.2 4.0 %collective-permute-start.12 = (bf16[2,64,256]{2,1,0:T(8,128)(2,1)S(1)}, bf16[2,64,256]{2,1,0:T(8,128)(2,1)S(1)}, u32[]{:S(2)}, u32[]{:S(2)}) collective-permute-start(bf16[2,64,256]{2,1,0:T(8,128)(2,1)S(1)} %get-tuple-element.94), channel_id=1, source_target_pairs={{0,4},{1,5},{2,6},{3,7},{4,0},{5,1},{6,2},{7,3},{8,12},{9,13},{10,... | collective-permute-start | bytes 196616 | tf_op jit(solution)/shard_map/ppermute | solution.py:327
  84.0 3.6 %collective-permute-start.14 = (bf16[2,64,256]{2,1,0:T(8,128)(2,1)S(1)}, bf16[2,64,256]{2,1,0:T(8,128)(2,1)S(1)}, u32[]{:S(2)}, u32[]{:S(2)}) collective-permute-start(bf16[2,64,256]{2,1,0:T(8,128)(2,1)S(1)} %get-tuple-element.96), channel_id=1, source_target_pairs={{0,6},{1,7},{2,4},{3,5},{4,2},{5,3},{6,0},{7,1},{8,14},{9,15},{10,... | collective-permute-start | bytes 196616 | tf_op jit(solution)/shard_map/ppermute | solution.py:327
  87.6 1.9 %collective-permute-start.46 = (bf16[2,64,512]{2,1,0:T(8,128)(2,1)S(1)}, bf16[2,64,512]{2,1,0:T(8,128)(2,1)S(1)}, u32[]{:S(2)}, u32[]{:S(2)}) collective-permute-start(bf16[2,64,512]{2,1,0:T(8,128)(2,1)S(1)} %get-tuple-element.134), channel_id=1, source_target_pairs={{0,1},{1,0},{2,3},{3,2},{4,5},{5,4},{6,7},{7,6},{8,9},{9,8},{10,11... | collective-permute-start | bytes 393224 | tf_op jit(solution)/shard_map/ppermute | solution.py:327
  90.6 1.2 collective-permute-start.48
  91.8 1.6 collective-permute-done.12.refs_4_.refs_0_
  94.3 1.4 collective-permute-start.52
  98.0 2.7 %collective-permute-start.51 = (bf16[2,64,512]{2,1,0:T(8,128)(2,1)S(1)}, bf16[2,64,512]{2,1,0:T(8,128)(2,1)S(1)}, u32[]{:S(2)}, u32[]{:S(2)}) collective-permute-start(bf16[2,64,512]{2,1,0:T(8,128)(2,1)S(1)} %get-tuple-element.139), channel_id=1, source_target_pairs={{0,6},{1,7},{2,4},{3,5},{4,2},{5,3},{6,0},{7,1},{8,14},{9,15},{10,... | collective-permute-start | bytes 393224 | tf_op jit(solution)/shard_map/ppermute | solution.py:327
  100.8 1.0 shard_map.64
  101.9 8.2 %collective-permute-done.50.refs_5_ = bf16[2,64,512]{2,1,0:T(8,128)(2,1)S(1)} collective-permute-done((bf16[2,64,512]{2,1,0:T(8,128)(2,1)S(1)}, bf16[2,64,512]{2,1,0:T(8,128)(2,1)S(1)}, u32[]{:S(2)}, u32[]{:S(2)}) %collective-permute-start.50) | collective-permute-done | bytes 131104 | tf_op jit(solution)/shard_map/ppermute | solution.py:327
  110.0 4.1 %collective-permute-done.49.refs_4_ = bf16[2,64,512]{2,1,0:T(8,128)(2,1)S(1)} collective-permute-done((bf16[2,64,512]{2,1,0:T(8,128)(2,1)S(1)}, bf16[2,64,512]{2,1,0:T(8,128)(2,1)S(1)}, u32[]{:S(2)}, u32[]{:S(2)}) %collective-permute-start.49) | collective-permute-done | bytes 131104 | tf_op jit(solution)/shard_map/ppermute | solution.py:327
  114.1 2.1 %shard_map.70 = (bf16[2,64,512]{2,1,0:T(8,128)(2,1)S(1)}, bf16[2,64,512]{2,1,0:T(8,128)(2,1)S(1)}, bf16[2,64,512]{2,1,0:T(8,128)(2,1)S(1)}, bf16[2,64,512]{2,1,0...) custom-call(bf16[2,64,512]{2,1,0:T(8,128)(2,1)S(1)} %get-tuple-eleme, ...), custom_call_target="tpu_custom_call" | custom-call | flops 2147483648 | bytes 1048576 | tf_op jit(solution)/shard_map/pallas_call | solution.py:396
  116.2 1.5 collective-permute-start.53
  117.7 2.0 %collective-permute-start.54 = (bf16[2,64,512]{2,1,0:T(8,128)(2,1)S(1)}, bf16[2,64,512]{2,1,0:T(8,128)(2,1)S(1)}, u32[]{:S(2)}, u32[]{:S(2)}) collective-permute-start(bf16[2,64,512]{2,1,0:T(8,128)(2,1)S(1)} %get-tuple-element.143), channel_id=1, source_target_pairs={{0,2},{1,3},{2,0},{3,1},{4,6},{5,7},{6,4},{7,5},{8,10},{9,11},{10,... | collective-permute-start | bytes 393224 | tf_op jit(solution)/shard_map/ppermute | solution.py:327
  120.5 2.8 %collective-permute-start.34 = (bf16[2,64,256]{2,1,0:T(8,128)(2,1)S(1)}, bf16[2,64,256]{2,1,0:T(8,128)(2,1)S(1)}, u32[]{:S(2)}, u32[]{:S(2)}) collective-permute-start(bf16[2,64,256]{2,1,0:T(8,128)(2,1)S(1)} %get-tuple-element.120), channel_id=1, source_target_pairs={{0,3},{1,2},{2,1},{3,0},{4,7},{5,6},{6,5},{7,4},{8,11},{9,10},{10,... | collective-permute-start | bytes 196616 | tf_op jit(solution)/shard_map/ppermute | solution.py:327
  124.1 2.3 %collective-permute-start.36 = (bf16[2,64,256]{2,1,0:T(8,128)(2,1)S(1)}, bf16[2,64,256]{2,1,0:T(8,128)(2,1)S(1)}, u32[]{:S(2)}, u32[]{:S(2)}) collective-permute-start(bf16[2,64,256]{2,1,0:T(8,128)(2,1)S(1)} %get-tuple-element.122), channel_id=1, source_target_pairs={{0,5},{1,4},{2,7},{3,6},{4,1},{5,0},{6,3},{7,2},{8,13},{9,12},{10,... | collective-permute-start | bytes 196616 | tf_op jit(solution)/shard_map/ppermute | solution.py:327
  126.5 1.7 collective-permute-start.37
  128.2 2.9 %collective-permute-start.38 = (bf16[2,64,256]{2,1,0:T(8,128)(2,1)S(1)}, bf16[2,64,256]{2,1,0:T(8,128)(2,1)S(1)}, u32[]{:S(2)}, u32[]{:S(2)}) collective-permute-start(bf16[2,64,256]{2,1,0:T(8,128)(2,1)S(1)} %get-tuple-element.124), channel_id=1, source_target_pairs={{0,7},{1,6},{2,5},{3,4},{4,3},{5,2},{6,1},{7,0},{8,15},{9,14},{10,... | collective-permute-start | bytes 196616 | tf_op jit(solution)/shard_map/ppermute | solution.py:327
  131.4 2.0 %collective-permute-start.56 = (bf16[2,64,512]{2,1,0:T(8,128)(2,1)S(1)}, bf16[2,64,512]{2,1,0:T(8,128)(2,1)S(1)}, u32[]{:S(2)}, u32[]{:S(2)}) collective-permute-start(bf16[2,64,512]{2,1,0:T(8,128)(2,1)S(1)} %get-tuple-element.145), channel_id=1, source_target_pairs={{0,4},{1,5},{2,6},{3,7},{4,0},{5,1},{6,2},{7,3},{8,12},{9,13},{10,... | collective-permute-start | bytes 393224 | tf_op jit(solution)/shard_map/ppermute | solution.py:327
  133.4 4.1 %collective-permute-done.36.refs_5_ = bf16[2,64,256]{2,1,0:T(8,128)(2,1)S(1)} collective-permute-done((bf16[2,64,256]{2,1,0:T(8,128)(2,1)S(1)}, bf16[2,64,256]{2,1,0:T(8,128)(2,1)S(1)}, u32[]{:S(2)}, u32[]{:S(2)}) %collective-permute-start.36) | collective-permute-done | bytes 65568 | tf_op jit(solution)/shard_map/ppermute | solution.py:327
  137.5 2.2 %collective-permute-start.58 = (bf16[2,64,512]{2,1,0:T(8,128)(2,1)S(1)}, bf16[2,64,512]{2,1,0:T(8,128)(2,1)S(1)}, u32[]{:S(2)}, u32[]{:S(2)}) collective-permute-start(bf16[2,64,512]{2,1,0:T(8,128)(2,1)S(1)} %get-tuple-element.147), channel_id=1, source_target_pairs={{0,6},{1,7},{2,4},{3,5},{4,2},{5,3},{6,0},{7,1},{8,14},{9,15},{10,... | collective-permute-start | bytes 393224 | tf_op jit(solution)/shard_map/ppermute | solution.py:327
  139.8 3.4 %collective-permute-start.59 = (bf16[2,64,512]{2,1,0:T(8,128)(2,1)S(1)}, bf16[2,64,512]{2,1,0:T(8,128)(2,1)S(1)}, u32[]{:S(2)}, u32[]{:S(2)}) collective-permute-start(bf16[2,64,512]{2,1,0:T(8,128)(2,1)S(1)} %get-tuple-element.148), channel_id=1, source_target_pairs={{0,7},{1,6},{2,5},{3,4},{4,3},{5,2},{6,1},{7,0},{8,15},{9,14},{10,... | collective-permute-start | bytes 393224 | tf_op jit(solution)/shard_map/ppermute | solution.py:327
  143.1 1.5 shard_map.66
  144.7 6.3 %collective-permute-done.56.refs_4_ = bf16[2,64,512]{2,1,0:T(8,128)(2,1)S(1)} collective-permute-done((bf16[2,64,512]{2,1,0:T(8,128)(2,1)S(1)}, bf16[2,64,512]{2,1,0:T(8,128)(2,1)S(1)}, u32[]{:S(2)}, u32[]{:S(2)}) %collective-permute-start.56) | collective-permute-done | bytes 131104 | tf_op jit(solution)/shard_map/ppermute | solution.py:327
  151.0 2.1 %collective-permute-start.40 = (bf16[2,64,256]{2,1,0:T(8,128)(2,1)S(1)}, bf16[2,64,256]{2,1,0:T(8,128)(2,1)S(1)}, u32[]{:S(2)}, u32[]{:S(2)}) collective-permute-start(bf16[2,64,256]{2,1,0:T(8,128)(2,1)S(1)} %get-tuple-element.127), channel_id=1, source_target_pairs={{0,2},{1,3},{2,0},{3,1},{4,6},{5,7},{6,4},{7,5},{8,10},{9,11},{10,... | collective-permute-start | bytes 196616 | tf_op jit(solution)/shard_map/ppermute | solution.py:327
  153.2 1.0 collective-permute-done.57.refs_5_
  154.2 4.1 %collective-permute-start.42 = (bf16[2,64,256]{2,1,0:T(8,128)(2,1)S(1)}, bf16[2,64,256]{2,1,0:T(8,128)(2,1)S(1)}, u32[]{:S(2)}, u32[]{:S(2)}) collective-permute-start(bf16[2,64,256]{2,1,0:T(8,128)(2,1)S(1)} %get-tuple-element.129), channel_id=1, source_target_pairs={{0,4},{1,5},{2,6},{3,7},{4,0},{5,1},{6,2},{7,3},{8,12},{9,13},{10,... | collective-permute-start | bytes 196616 | tf_op jit(solution)/shard_map/ppermute | solution.py:327
  158.3 5.1 %collective-permute-start.43 = (bf16[2,64,256]{2,1,0:T(8,128)(2,1)S(1)}, bf16[2,64,256]{2,1,0:T(8,128)(2,1)S(1)}, u32[]{:S(2)}, u32[]{:S(2)}) collective-permute-start(bf16[2,64,256]{2,1,0:T(8,128)(2,1)S(1)} %get-tuple-element.130), channel_id=1, source_target_pairs={{0,5},{1,4},{2,7},{3,6},{4,1},{5,0},{6,3},{7,2},{8,13},{9,12},{10,... | collective-permute-start | bytes 196616 | tf_op jit(solution)/shard_map/ppermute | solution.py:327
  163.4 1.9 %collective-permute-start.44 = (bf16[2,64,256]{2,1,0:T(8,128)(2,1)S(1)}, bf16[2,64,256]{2,1,0:T(8,128)(2,1)S(1)}, u32[]{:S(2)}, u32[]{:S(2)}) collective-permute-start(bf16[2,64,256]{2,1,0:T(8,128)(2,1)S(1)} %get-tuple-element.131), channel_id=1, source_target_pairs={{0,6},{1,7},{2,4},{3,5},{4,2},{5,3},{6,0},{7,1},{8,14},{9,15},{10,... | collective-permute-start | bytes 196616 | tf_op jit(solution)/shard_map/ppermute | solution.py:327
  165.3 2.3 %collective-permute-start.45 = (bf16[2,64,256]{2,1,0:T(8,128)(2,1)S(1)}, bf16[2,64,256]{2,1,0:T(8,128)(2,1)S(1)}, u32[]{:S(2)}, u32[]{:S(2)}) collective-permute-start(bf16[2,64,256]{2,1,0:T(8,128)(2,1)S(1)} %get-tuple-element.132), channel_id=1, source_target_pairs={{0,7},{1,6},{2,5},{3,4},{4,3},{5,2},{6,1},{7,0},{8,15},{9,14},{10,... | collective-permute-start | bytes 196616 | tf_op jit(solution)/shard_map/ppermute | solution.py:327
  167.6 1.0 shard_map.71.refs_8_
  169.5 2.8 %collective-permute-done.45.refs_7_ = bf16[2,64,256]{2,1,0:T(8,128)(2,1)S(1)} collective-permute-done((bf16[2,64,256]{2,1,0:T(8,128)(2,1)S(1)}, bf16[2,64,256]{2,1,0:T(8,128)(2,1)S(1)}, u32[]{:S(2)}, u32[]{:S(2)}) %collective-permute-start.45) | collective-permute-done | bytes 65568 | tf_op jit(solution)/shard_map/ppermute | solution.py:327
  (81 shorter events, 12.6 us)
Async XLA Ops:
  3.4 21.8 %collective-permute-start.19 = (bf16[2,64,512]{2,1,0:T(8,128)(2,1)S(1)}, bf16[2,64,512]{2,1,0:T(8,128)(2,1)S(1)}, u32[]{:S(2)}, u32[]{:S(2)}) collective-permute-start(bf16[2,64,512]{2,1,0:T(8,128)(2,1)S(1)} %get-tuple-element.103), channel_id=1, source_target_pairs={{0,4},{1,5},{2,6},{3,7},{4,0},{5,1},{6,2},{7,3},{8,12},{9,13},{10,... | collective-permute-start | bytes 393224 | tf_op jit(solution)/shard_map/ppermute | solution.py:327
  7.5 3.7 %copy-start.1 = (bf16[2,768,512]{2,1,0:T(8,128)(2,1)S(1)}, bf16[2,768,512]{2,1,0:T(8,128)(2,1)}, u32[]{:S(2)}) copy-start(bf16[2,768,512]{2,1,0:T(8,128)(2,1)} %get-tuple-element.98.refs_2_.refs_9_.refs_5_) | copy-start | bytes 4718596
  7.5 18.3 %collective-permute-start.21 = (bf16[2,64,512]{2,1,0:T(8,128)(2,1)S(1)}, bf16[2,64,512]{2,1,0:T(8,128)(2,1)S(1)}, u32[]{:S(2)}, u32[]{:S(2)}) collective-permute-start(bf16[2,64,512]{2,1,0:T(8,128)(2,1)S(1)} %get-tuple-element.105), channel_id=1, source_target_pairs={{0,6},{1,7},{2,4},{3,5},{4,2},{5,3},{6,0},{7,1},{8,14},{9,15},{10,... | collective-permute-start | bytes 393224 | tf_op jit(solution)/shard_map/ppermute | solution.py:327
  11.8 15.4 %collective-permute-start.20 = (bf16[2,64,512]{2,1,0:T(8,128)(2,1)S(1)}, bf16[2,64,512]{2,1,0:T(8,128)(2,1)S(1)}, u32[]{:S(2)}, u32[]{:S(2)}) collective-permute-start(bf16[2,64,512]{2,1,0:T(8,128)(2,1)S(1)} %get-tuple-element.104), channel_id=1, source_target_pairs={{0,5},{1,4},{2,7},{3,6},{4,1},{5,0},{6,3},{7,2},{8,13},{9,12},{10,... | collective-permute-start | bytes 393224 | tf_op jit(solution)/shard_map/ppermute | solution.py:327
  15.5 6.9 %collective-permute-start = (bf16[8,2,64,128]{3,2,1,0:T(8,128)(2,1)S(1)}, bf16[8,2,64,128]{3,2,1,0:T(8,128)(2,1)S(1)}, u32[]{:S(2)}, u32[]{:S(2)}) collective-permute-start(bf16[8,2,64,128]{3,2,1,0:T(8,128)(2,1)S(1)} %get-tuple-element.80), channel_id=1, source_target_pairs={{0,8},{8,16},{16,24},{24,0},{1,9},{9,17},{17,25},{25,1},{2,10},{10... | collective-permute-start | bytes 786440 | tf_op jit(solution)/shard_map/ppermute | solution.py:433
  15.6 2.7 %copy-start.2 = (bf16[1,8,8]{2,1,0:T(8,128)(2,1)S(1)}, bf16[1,8,8]{2,1,0:T(8,128)(2,1)}, u32[]{:S(2)}) copy-start(bf16[1,8,8]{2,1,0:T(8,128)(2,1)} %param.8) | copy-start | bytes 388
  15.6 8.0 %collective-permute-start.1 = (bf16[8,2,64,128]{3,2,1,0:T(8,128)(2,1)S(1)}, bf16[8,2,64,128]{3,2,1,0:T(8,128)(2,1)S(1)}, u32[]{:S(2)}, u32[]{:S(2)}) collective-permute-start(bf16[8,2,64,128]{3,2,1,0:T(8,128)(2,1)S(1)} %get-tuple-element.81), channel_id=1, source_target_pairs={{8,0},{16,8},{24,16},{0,24},{9,1},{17,9},{25,17},{1,25},{10,2},{18... | collective-permute-start | bytes 786440 | tf_op jit(solution)/shard_map/ppermute | solution.py:434
  22.4 9.1 %collective-permute-start.22 = (bf16[2,64,512]{2,1,0:T(8,128)(2,1)S(1)}, bf16[2,64,512]{2,1,0:T(8,128)(2,1)S(1)}, u32[]{:S(2)}, u32[]{:S(2)}) collective-permute-start(bf16[2,64,512]{2,1,0:T(8,128)(2,1)S(1)} %get-tuple-element.106), channel_id=1, source_target_pairs={{0,7},{1,6},{2,5},{3,4},{4,3},{5,2},{6,1},{7,0},{8,15},{9,14},{10,... | collective-permute-start | bytes 393224 | tf_op jit(solution)/shard_map/ppermute | solution.py:327
  23.5 9.9 %copy-start = (s32[1,8]{1,0:T(1,128)S(1)}, s32[1,8]{1,0:T(1,128)}, u32[]{:S(2)}) copy-start(s32[1,8]{1,0:T(1,128)} %param.9) | copy-start | bytes 100
  23.5 12.6 %collective-permute-start.16 = (bf16[2,64,512]{2,1,0:T(8,128)(2,1)S(1)}, bf16[2,64,512]{2,1,0:T(8,128)(2,1)S(1)}, u32[]{:S(2)}, u32[]{:S(2)}) collective-permute-start(bf16[2,64,512]{2,1,0:T(8,128)(2,1)S(1)} %get-tuple-element.100), channel_id=1, source_target_pairs={{0,1},{1,0},{2,3},{3,2},{4,5},{5,4},{6,7},{7,6},{8,9},{9,8},{10,11... | collective-permute-start | bytes 393224 | tf_op jit(solution)/shard_map/ppermute | solution.py:327
  25.2 11.1 %collective-permute-start.17 = (bf16[2,64,512]{2,1,0:T(8,128)(2,1)S(1)}, bf16[2,64,512]{2,1,0:T(8,128)(2,1)S(1)}, u32[]{:S(2)}, u32[]{:S(2)}) collective-permute-start(bf16[2,64,512]{2,1,0:T(8,128)(2,1)S(1)} %get-tuple-element.101), channel_id=1, source_target_pairs={{0,2},{1,3},{2,0},{3,1},{4,6},{5,7},{6,4},{7,5},{8,10},{9,11},{10,... | collective-permute-start | bytes 393224 | tf_op jit(solution)/shard_map/ppermute | solution.py:327
  25.8 14.0 %collective-permute-start.18 = (bf16[2,64,512]{2,1,0:T(8,128)(2,1)S(1)}, bf16[2,64,512]{2,1,0:T(8,128)(2,1)S(1)}, u32[]{:S(2)}, u32[]{:S(2)}) collective-permute-start(bf16[2,64,512]{2,1,0:T(8,128)(2,1)S(1)} %get-tuple-element.102), channel_id=1, source_target_pairs={{0,3},{1,2},{2,1},{3,0},{4,7},{5,6},{6,5},{7,4},{8,11},{9,10},{10,... | collective-permute-start | bytes 393224 | tf_op jit(solution)/shard_map/ppermute | solution.py:327
  27.2 13.7 %collective-permute-start.2 = (bf16[2,64,256]{2,1,0:T(8,128)(2,1)S(1)}, bf16[2,64,256]{2,1,0:T(8,128)(2,1)S(1)}, u32[]{:S(2)}, u32[]{:S(2)}) collective-permute-start(bf16[2,64,256]{2,1,0:T(8,128)(2,1)S(1)} %get-tuple-element.83), channel_id=1, source_target_pairs={{0,1},{1,0},{2,3},{3,2},{4,5},{5,4},{6,7},{7,6},{8,9},{9,8},{10,11... | collective-permute-start | bytes 196616 | tf_op jit(solution)/shard_map/ppermute | solution.py:327
  31.5 11.7 %collective-permute-start.3 = (bf16[2,64,256]{2,1,0:T(8,128)(2,1)S(1)}, bf16[2,64,256]{2,1,0:T(8,128)(2,1)S(1)}, u32[]{:S(2)}, u32[]{:S(2)}) collective-permute-start(bf16[2,64,256]{2,1,0:T(8,128)(2,1)S(1)} %get-tuple-element.84), channel_id=1, source_target_pairs={{0,2},{1,3},{2,0},{3,1},{4,6},{5,7},{6,4},{7,5},{8,10},{9,11},{10,... | collective-permute-start | bytes 196616 | tf_op jit(solution)/shard_map/ppermute | solution.py:327
  36.1 10.7 %collective-permute-start.4 = (bf16[2,64,256]{2,1,0:T(8,128)(2,1)S(1)}, bf16[2,64,256]{2,1,0:T(8,128)(2,1)S(1)}, u32[]{:S(2)}, u32[]{:S(2)}) collective-permute-start(bf16[2,64,256]{2,1,0:T(8,128)(2,1)S(1)} %get-tuple-element.85), channel_id=1, source_target_pairs={{0,3},{1,2},{2,1},{3,0},{4,7},{5,6},{6,5},{7,4},{8,11},{9,10},{10,... | collective-permute-start | bytes 196616 | tf_op jit(solution)/shard_map/ppermute | solution.py:327
  36.2 12.1 %collective-permute-start.5 = (bf16[2,64,256]{2,1,0:T(8,128)(2,1)S(1)}, bf16[2,64,256]{2,1,0:T(8,128)(2,1)S(1)}, u32[]{:S(2)}, u32[]{:S(2)}) collective-permute-start(bf16[2,64,256]{2,1,0:T(8,128)(2,1)S(1)} %get-tuple-element.86), channel_id=1, source_target_pairs={{0,4},{1,5},{2,6},{3,7},{4,0},{5,1},{6,2},{7,3},{8,12},{9,13},{10,... | collective-permute-start | bytes 196616 | tf_op jit(solution)/shard_map/ppermute | solution.py:327
  39.8 9.0 %collective-permute-start.6 = (bf16[2,64,256]{2,1,0:T(8,128)(2,1)S(1)}, bf16[2,64,256]{2,1,0:T(8,128)(2,1)S(1)}, u32[]{:S(2)}, u32[]{:S(2)}) collective-permute-start(bf16[2,64,256]{2,1,0:T(8,128)(2,1)S(1)} %get-tuple-element.87), channel_id=1, source_target_pairs={{0,5},{1,4},{2,7},{3,6},{4,1},{5,0},{6,3},{7,2},{8,13},{9,12},{10,... | collective-permute-start | bytes 196616 | tf_op jit(solution)/shard_map/ppermute | solution.py:327
  40.9 9.5 %collective-permute-start.7 = (bf16[2,64,256]{2,1,0:T(8,128)(2,1)S(1)}, bf16[2,64,256]{2,1,0:T(8,128)(2,1)S(1)}, u32[]{:S(2)}, u32[]{:S(2)}) collective-permute-start(bf16[2,64,256]{2,1,0:T(8,128)(2,1)S(1)} %get-tuple-element.88), channel_id=1, source_target_pairs={{0,6},{1,7},{2,4},{3,5},{4,2},{5,3},{6,0},{7,1},{8,14},{9,15},{10,... | collective-permute-start | bytes 196616 | tf_op jit(solution)/shard_map/ppermute | solution.py:327
  43.2 7.6 %collective-permute-start.8 = (bf16[2,64,256]{2,1,0:T(8,128)(2,1)S(1)}, bf16[2,64,256]{2,1,0:T(8,128)(2,1)S(1)}, u32[]{:S(2)}, u32[]{:S(2)}) collective-permute-start(bf16[2,64,256]{2,1,0:T(8,128)(2,1)S(1)} %get-tuple-element.89), channel_id=1, source_target_pairs={{0,7},{1,6},{2,5},{3,4},{4,3},{5,2},{6,1},{7,0},{8,15},{9,14},{10,... | collective-permute-start | bytes 196616 | tf_op jit(solution)/shard_map/ppermute | solution.py:327
  46.8 8.6 %collective-permute-start.23 = (bf16[2,64,512]{2,1,0:T(8,128)(2,1)S(1)}, bf16[2,64,512]{2,1,0:T(8,128)(2,1)S(1)}, u32[]{:S(2)}, u32[]{:S(2)}) collective-permute-start(bf16[2,64,512]{2,1,0:T(8,128)(2,1)S(1)} %get-tuple-element.108), channel_id=1, source_target_pairs={{0,1},{1,0},{2,3},{3,2},{4,5},{5,4},{6,7},{7,6},{8,9},{9,8},{10,11... | collective-permute-start | bytes 393224 | tf_op jit(solution)/shard_map/ppermute | solution.py:327
  48.3 8.4 %collective-permute-start.24 = (bf16[2,64,512]{2,1,0:T(8,128)(2,1)S(1)}, bf16[2,64,512]{2,1,0:T(8,128)(2,1)S(1)}, u32[]{:S(2)}, u32[]{:S(2)}) collective-permute-start(bf16[2,64,512]{2,1,0:T(8,128)(2,1)S(1)} %get-tuple-element.109), channel_id=1, source_target_pairs={{0,2},{1,3},{2,0},{3,1},{4,6},{5,7},{6,4},{7,5},{8,10},{9,11},{10,... | collective-permute-start | bytes 393224 | tf_op jit(solution)/shard_map/ppermute | solution.py:327
  48.8 10.2 %collective-permute-start.25 = (bf16[2,64,512]{2,1,0:T(8,128)(2,1)S(1)}, bf16[2,64,512]{2,1,0:T(8,128)(2,1)S(1)}, u32[]{:S(2)}, u32[]{:S(2)}) collective-permute-start(bf16[2,64,512]{2,1,0:T(8,128)(2,1)S(1)} %get-tuple-element.110), channel_id=1, source_target_pairs={{0,3},{1,2},{2,1},{3,0},{4,7},{5,6},{6,5},{7,4},{8,11},{9,10},{10,... | collective-permute-start | bytes 393224 | tf_op jit(solution)/shard_map/ppermute | solution.py:327
  52.2 7.5 %collective-permute-start.9 = (bf16[2,64,256]{2,1,0:T(8,128)(2,1)S(1)}, bf16[2,64,256]{2,1,0:T(8,128)(2,1)S(1)}, u32[]{:S(2)}, u32[]{:S(2)}) collective-permute-start(bf16[2,64,256]{2,1,0:T(8,128)(2,1)S(1)} %get-tuple-element.91), channel_id=1, source_target_pairs={{0,1},{1,0},{2,3},{3,2},{4,5},{5,4},{6,7},{7,6},{8,9},{9,8},{10,11... | collective-permute-start | bytes 196616 | tf_op jit(solution)/shard_map/ppermute | solution.py:327
  53.4 9.6 %collective-permute-start.10 = (bf16[2,64,256]{2,1,0:T(8,128)(2,1)S(1)}, bf16[2,64,256]{2,1,0:T(8,128)(2,1)S(1)}, u32[]{:S(2)}, u32[]{:S(2)}) collective-permute-start(bf16[2,64,256]{2,1,0:T(8,128)(2,1)S(1)} %get-tuple-element.92), channel_id=1, source_target_pairs={{0,2},{1,3},{2,0},{3,1},{4,6},{5,7},{6,4},{7,5},{8,10},{9,11},{10,... | collective-permute-start | bytes 196616 | tf_op jit(solution)/shard_map/ppermute | solution.py:327
  55.4 8.2 %collective-permute-start.11 = (bf16[2,64,256]{2,1,0:T(8,128)(2,1)S(1)}, bf16[2,64,256]{2,1,0:T(8,128)(2,1)S(1)}, u32[]{:S(2)}, u32[]{:S(2)}) collective-permute-start(bf16[2,64,256]{2,1,0:T(8,128)(2,1)S(1)} %get-tuple-element.93), channel_id=1, source_target_pairs={{0,3},{1,2},{2,1},{3,0},{4,7},{5,6},{6,5},{7,4},{8,11},{9,10},{10,... | collective-permute-start | bytes 196616 | tf_op jit(solution)/shard_map/ppermute | solution.py:327
  56.8 33.3 %collective-permute-start.26 = (bf16[2,64,512]{2,1,0:T(8,128)(2,1)S(1)}, bf16[2,64,512]{2,1,0:T(8,128)(2,1)S(1)}, u32[]{:S(2)}, u32[]{:S(2)}) collective-permute-start(bf16[2,64,512]{2,1,0:T(8,128)(2,1)S(1)} %get-tuple-element.111), channel_id=1, source_target_pairs={{0,4},{1,5},{2,6},{3,7},{4,0},{5,1},{6,2},{7,3},{8,12},{9,13},{10,... | collective-permute-start | bytes 393224 | tf_op jit(solution)/shard_map/ppermute | solution.py:327
  59.0 18.7 %collective-permute-start.27 = (bf16[2,64,512]{2,1,0:T(8,128)(2,1)S(1)}, bf16[2,64,512]{2,1,0:T(8,128)(2,1)S(1)}, u32[]{:S(2)}, u32[]{:S(2)}) collective-permute-start(bf16[2,64,512]{2,1,0:T(8,128)(2,1)S(1)} %get-tuple-element.112), channel_id=1, source_target_pairs={{0,5},{1,4},{2,7},{3,6},{4,1},{5,0},{6,3},{7,2},{8,13},{9,12},{10,... | collective-permute-start | bytes 393224 | tf_op jit(solution)/shard_map/ppermute | solution.py:327
  59.8 19.4 %collective-permute-start.29 = (bf16[2,64,512]{2,1,0:T(8,128)(2,1)S(1)}, bf16[2,64,512]{2,1,0:T(8,128)(2,1)S(1)}, u32[]{:S(2)}, u32[]{:S(2)}) collective-permute-start(bf16[2,64,512]{2,1,0:T(8,128)(2,1)S(1)} %get-tuple-element.114), channel_id=1, source_target_pairs={{0,7},{1,6},{2,5},{3,4},{4,3},{5,2},{6,1},{7,0},{8,15},{9,14},{10,... | collective-permute-start | bytes 393224 | tf_op jit(solution)/shard_map/ppermute | solution.py:327
  63.0 21.0 %collective-permute-start.13 = (bf16[2,64,256]{2,1,0:T(8,128)(2,1)S(1)}, bf16[2,64,256]{2,1,0:T(8,128)(2,1)S(1)}, u32[]{:S(2)}, u32[]{:S(2)}) collective-permute-start(bf16[2,64,256]{2,1,0:T(8,128)(2,1)S(1)} %get-tuple-element.95), channel_id=1, source_target_pairs={{0,5},{1,4},{2,7},{3,6},{4,1},{5,0},{6,3},{7,2},{8,13},{9,12},{10,... | collective-permute-start | bytes 196616 | tf_op jit(solution)/shard_map/ppermute | solution.py:327
  63.6 24.0 %collective-permute-start.15 = (bf16[2,64,256]{2,1,0:T(8,128)(2,1)S(1)}, bf16[2,64,256]{2,1,0:T(8,128)(2,1)S(1)}, u32[]{:S(2)}, u32[]{:S(2)}) collective-permute-start(bf16[2,64,256]{2,1,0:T(8,128)(2,1)S(1)} %get-tuple-element.97), channel_id=1, source_target_pairs={{0,7},{1,6},{2,5},{3,4},{4,3},{5,2},{6,1},{7,0},{8,15},{9,14},{10,... | collective-permute-start | bytes 196616 | tf_op jit(solution)/shard_map/ppermute | solution.py:327
  77.7 13.0 %collective-permute-start.28 = (bf16[2,64,512]{2,1,0:T(8,128)(2,1)S(1)}, bf16[2,64,512]{2,1,0:T(8,128)(2,1)S(1)}, u32[]{:S(2)}, u32[]{:S(2)}) collective-permute-start(bf16[2,64,512]{2,1,0:T(8,128)(2,1)S(1)} %get-tuple-element.113), channel_id=1, source_target_pairs={{0,6},{1,7},{2,4},{3,5},{4,2},{5,3},{6,0},{7,1},{8,14},{9,15},{10,... | collective-permute-start | bytes 393224 | tf_op jit(solution)/shard_map/ppermute | solution.py:327
  79.2 14.1 %collective-permute-start.12 = (bf16[2,64,256]{2,1,0:T(8,128)(2,1)S(1)}, bf16[2,64,256]{2,1,0:T(8,128)(2,1)S(1)}, u32[]{:S(2)}, u32[]{:S(2)}) collective-permute-start(bf16[2,64,256]{2,1,0:T(8,128)(2,1)S(1)} %get-tuple-element.94), channel_id=1, source_target_pairs={{0,4},{1,5},{2,6},{3,7},{4,0},{5,1},{6,2},{7,3},{8,12},{9,13},{10,... | collective-permute-start | bytes 196616 | tf_op jit(solution)/shard_map/ppermute | solution.py:327
  84.0 10.3 %collective-permute-start.14 = (bf16[2,64,256]{2,1,0:T(8,128)(2,1)S(1)}, bf16[2,64,256]{2,1,0:T(8,128)(2,1)S(1)}, u32[]{:S(2)}, u32[]{:S(2)}) collective-permute-start(bf16[2,64,256]{2,1,0:T(8,128)(2,1)S(1)} %get-tuple-element.96), channel_id=1, source_target_pairs={{0,6},{1,7},{2,4},{3,5},{4,2},{5,3},{6,0},{7,1},{8,14},{9,15},{10,... | collective-permute-start | bytes 196616 | tf_op jit(solution)/shard_map/ppermute | solution.py:327
  87.6 8.7 %collective-permute-start.46 = (bf16[2,64,512]{2,1,0:T(8,128)(2,1)S(1)}, bf16[2,64,512]{2,1,0:T(8,128)(2,1)S(1)}, u32[]{:S(2)}, u32[]{:S(2)}) collective-permute-start(bf16[2,64,512]{2,1,0:T(8,128)(2,1)S(1)} %get-tuple-element.134), channel_id=1, source_target_pairs={{0,1},{1,0},{2,3},{3,2},{4,5},{5,4},{6,7},{7,6},{8,9},{9,8},{10,11... | collective-permute-start | bytes 393224 | tf_op jit(solution)/shard_map/ppermute | solution.py:327
  90.1 7.9 %collective-permute-start.47 = (bf16[2,64,512]{2,1,0:T(8,128)(2,1)S(1)}, bf16[2,64,512]{2,1,0:T(8,128)(2,1)S(1)}, u32[]{:S(2)}, u32[]{:S(2)}) collective-permute-start(bf16[2,64,512]{2,1,0:T(8,128)(2,1)S(1)} %get-tuple-element.135), channel_id=1, source_target_pairs={{0,2},{1,3},{2,0},{3,1},{4,6},{5,7},{6,4},{7,5},{8,10},{9,11},{10,... | collective-permute-start | bytes 393224 | tf_op jit(solution)/shard_map/ppermute | solution.py:327
  90.6 11.2 %collective-permute-start.48 = (bf16[2,64,512]{2,1,0:T(8,128)(2,1)S(1)}, bf16[2,64,512]{2,1,0:T(8,128)(2,1)S(1)}, u32[]{:S(2)}, u32[]{:S(2)}) collective-permute-start(bf16[2,64,512]{2,1,0:T(8,128)(2,1)S(1)} %get-tuple-element.136), channel_id=1, source_target_pairs={{0,3},{1,2},{2,1},{3,0},{4,7},{5,6},{6,5},{7,4},{8,11},{9,10},{10,... | collective-permute-start | bytes 393224 | tf_op jit(solution)/shard_map/ppermute | solution.py:327
  93.3 16.7 %collective-permute-start.50 = (bf16[2,64,512]{2,1,0:T(8,128)(2,1)S(1)}, bf16[2,64,512]{2,1,0:T(8,128)(2,1)S(1)}, u32[]{:S(2)}, u32[]{:S(2)}) collective-permute-start(bf16[2,64,512]{2,1,0:T(8,128)(2,1)S(1)} %get-tuple-element.138), channel_id=1, source_target_pairs={{0,5},{1,4},{2,7},{3,6},{4,1},{5,0},{6,3},{7,2},{8,13},{9,12},{10,... | collective-permute-start | bytes 393224 | tf_op jit(solution)/shard_map/ppermute | solution.py:327
  94.3 15.7 %collective-permute-start.52 = (bf16[2,64,512]{2,1,0:T(8,128)(2,1)S(1)}, bf16[2,64,512]{2,1,0:T(8,128)(2,1)S(1)}, u32[]{:S(2)}, u32[]{:S(2)}) collective-permute-start(bf16[2,64,512]{2,1,0:T(8,128)(2,1)S(1)} %get-tuple-element.140), channel_id=1, source_target_pairs={{0,7},{1,6},{2,5},{3,4},{4,3},{5,2},{6,1},{7,0},{8,15},{9,14},{10,... | collective-permute-start | bytes 393224 | tf_op jit(solution)/shard_map/ppermute | solution.py:327
  96.4 17.8 %collective-permute-start.49 = (bf16[2,64,512]{2,1,0:T(8,128)(2,1)S(1)}, bf16[2,64,512]{2,1,0:T(8,128)(2,1)S(1)}, u32[]{:S(2)}, u32[]{:S(2)}) collective-permute-start(bf16[2,64,512]{2,1,0:T(8,128)(2,1)S(1)} %get-tuple-element.137), channel_id=1, source_target_pairs={{0,4},{1,5},{2,6},{3,7},{4,0},{5,1},{6,2},{7,3},{8,12},{9,13},{10,... | collective-permute-start | bytes 393224 | tf_op jit(solution)/shard_map/ppermute | solution.py:327
  98.0 16.1 %collective-permute-start.51 = (bf16[2,64,512]{2,1,0:T(8,128)(2,1)S(1)}, bf16[2,64,512]{2,1,0:T(8,128)(2,1)S(1)}, u32[]{:S(2)}, u32[]{:S(2)}) collective-permute-start(bf16[2,64,512]{2,1,0:T(8,128)(2,1)S(1)} %get-tuple-element.139), channel_id=1, source_target_pairs={{0,6},{1,7},{2,4},{3,5},{4,2},{5,3},{6,0},{7,1},{8,14},{9,15},{10,... | collective-permute-start | bytes 393224 | tf_op jit(solution)/shard_map/ppermute | solution.py:327
  101.8 17.9 %collective-permute-start.30 = (bf16[8,2,64,128]{3,2,1,0:T(8,128)(2,1)S(1)}, bf16[8,2,64,128]{3,2,1,0:T(8,128)(2,1)S(1)}, u32[]{:S(2)}, u32[]{:S(2)}) collective-permute-start(bf16[8,2,64,128]{3,2,1,0:T(8,128)(2,1)S(1)} %get-tuple-element.115), channel_id=1, source_target_pairs={{0,8},{8,16},{16,24},{24,0},{1,9},{9,17},{17,25},{25,1},{2,10},{10... | collective-permute-start | bytes 786440 | tf_op jit(solution)/shard_map/ppermute | solution.py:433
  110.0 9.7 %collective-permute-start.31 = (bf16[8,2,64,128]{3,2,1,0:T(8,128)(2,1)S(1)}, bf16[8,2,64,128]{3,2,1,0:T(8,128)(2,1)S(1)}, u32[]{:S(2)}, u32[]{:S(2)}) collective-permute-start(bf16[8,2,64,128]{3,2,1,0:T(8,128)(2,1)S(1)} %get-tuple-element.116), channel_id=1, source_target_pairs={{8,0},{16,8},{24,16},{0,24},{9,1},{17,9},{25,17},{1,25},{10,2},{18... | collective-permute-start | bytes 786440 | tf_op jit(solution)/shard_map/ppermute | solution.py:434
  116.2 7.1 %collective-permute-start.53 = (bf16[2,64,512]{2,1,0:T(8,128)(2,1)S(1)}, bf16[2,64,512]{2,1,0:T(8,128)(2,1)S(1)}, u32[]{:S(2)}, u32[]{:S(2)}) collective-permute-start(bf16[2,64,512]{2,1,0:T(8,128)(2,1)S(1)} %get-tuple-element.142), channel_id=1, source_target_pairs={{0,1},{1,0},{2,3},{3,2},{4,5},{5,4},{6,7},{7,6},{8,9},{9,8},{10,11... | collective-permute-start | bytes 393224 | tf_op jit(solution)/shard_map/ppermute | solution.py:327
  117.7 6.4 %collective-permute-start.54 = (bf16[2,64,512]{2,1,0:T(8,128)(2,1)S(1)}, bf16[2,64,512]{2,1,0:T(8,128)(2,1)S(1)}, u32[]{:S(2)}, u32[]{:S(2)}) collective-permute-start(bf16[2,64,512]{2,1,0:T(8,128)(2,1)S(1)} %get-tuple-element.143), channel_id=1, source_target_pairs={{0,2},{1,3},{2,0},{3,1},{4,6},{5,7},{6,4},{7,5},{8,10},{9,11},{10,... | collective-permute-start | bytes 393224 | tf_op jit(solution)/shard_map/ppermute | solution.py:327
  119.8 6.7 %collective-permute-start.32 = (bf16[2,64,256]{2,1,0:T(8,128)(2,1)S(1)}, bf16[2,64,256]{2,1,0:T(8,128)(2,1)S(1)}, u32[]{:S(2)}, u32[]{:S(2)}) collective-permute-start(bf16[2,64,256]{2,1,0:T(8,128)(2,1)S(1)} %get-tuple-element.118), channel_id=1, source_target_pairs={{0,1},{1,0},{2,3},{3,2},{4,5},{5,4},{6,7},{7,6},{8,9},{9,8},{10,11... | collective-permute-start | bytes 196616 | tf_op jit(solution)/shard_map/ppermute | solution.py:327
  120.5 7.7 %collective-permute-start.33 = (bf16[2,64,256]{2,1,0:T(8,128)(2,1)S(1)}, bf16[2,64,256]{2,1,0:T(8,128)(2,1)S(1)}, u32[]{:S(2)}, u32[]{:S(2)}) collective-permute-start(bf16[2,64,256]{2,1,0:T(8,128)(2,1)S(1)} %get-tuple-element.119), channel_id=1, source_target_pairs={{0,2},{1,3},{2,0},{3,1},{4,6},{5,7},{6,4},{7,5},{8,10},{9,11},{10,... | collective-permute-start | bytes 196616 | tf_op jit(solution)/shard_map/ppermute | solution.py:327
  120.5 10.5 %collective-permute-start.34 = (bf16[2,64,256]{2,1,0:T(8,128)(2,1)S(1)}, bf16[2,64,256]{2,1,0:T(8,128)(2,1)S(1)}, u32[]{:S(2)}, u32[]{:S(2)}) collective-permute-start(bf16[2,64,256]{2,1,0:T(8,128)(2,1)S(1)} %get-tuple-element.120), channel_id=1, source_target_pairs={{0,3},{1,2},{2,1},{3,0},{4,7},{5,6},{6,5},{7,4},{8,11},{9,10},{10,... | collective-permute-start | bytes 196616 | tf_op jit(solution)/shard_map/ppermute | solution.py:327
  123.4 8.0 %collective-permute-start.35 = (bf16[2,64,256]{2,1,0:T(8,128)(2,1)S(1)}, bf16[2,64,256]{2,1,0:T(8,128)(2,1)S(1)}, u32[]{:S(2)}, u32[]{:S(2)}) collective-permute-start(bf16[2,64,256]{2,1,0:T(8,128)(2,1)S(1)} %get-tuple-element.121), channel_id=1, source_target_pairs={{0,4},{1,5},{2,6},{3,7},{4,0},{5,1},{6,2},{7,3},{8,12},{9,13},{10,... | collective-permute-start | bytes 196616 | tf_op jit(solution)/shard_map/ppermute | solution.py:327
  124.1 13.4 %collective-permute-start.36 = (bf16[2,64,256]{2,1,0:T(8,128)(2,1)S(1)}, bf16[2,64,256]{2,1,0:T(8,128)(2,1)S(1)}, u32[]{:S(2)}, u32[]{:S(2)}) collective-permute-start(bf16[2,64,256]{2,1,0:T(8,128)(2,1)S(1)} %get-tuple-element.122), channel_id=1, source_target_pairs={{0,5},{1,4},{2,7},{3,6},{4,1},{5,0},{6,3},{7,2},{8,13},{9,12},{10,... | collective-permute-start | bytes 196616 | tf_op jit(solution)/shard_map/ppermute | solution.py:327
  126.5 11.1 %collective-permute-start.37 = (bf16[2,64,256]{2,1,0:T(8,128)(2,1)S(1)}, bf16[2,64,256]{2,1,0:T(8,128)(2,1)S(1)}, u32[]{:S(2)}, u32[]{:S(2)}) collective-permute-start(bf16[2,64,256]{2,1,0:T(8,128)(2,1)S(1)} %get-tuple-element.123), channel_id=1, source_target_pairs={{0,6},{1,7},{2,4},{3,5},{4,2},{5,3},{6,0},{7,1},{8,14},{9,15},{10,... | collective-permute-start | bytes 196616 | tf_op jit(solution)/shard_map/ppermute | solution.py:327
  128.2 11.6 %collective-permute-start.38 = (bf16[2,64,256]{2,1,0:T(8,128)(2,1)S(1)}, bf16[2,64,256]{2,1,0:T(8,128)(2,1)S(1)}, u32[]{:S(2)}, u32[]{:S(2)}) collective-permute-start(bf16[2,64,256]{2,1,0:T(8,128)(2,1)S(1)} %get-tuple-element.124), channel_id=1, source_target_pairs={{0,7},{1,6},{2,5},{3,4},{4,3},{5,2},{6,1},{7,0},{8,15},{9,14},{10,... | collective-permute-start | bytes 196616 | tf_op jit(solution)/shard_map/ppermute | solution.py:327
  131.0 13.6 %collective-permute-start.55 = (bf16[2,64,512]{2,1,0:T(8,128)(2,1)S(1)}, bf16[2,64,512]{2,1,0:T(8,128)(2,1)S(1)}, u32[]{:S(2)}, u32[]{:S(2)}) collective-permute-start(bf16[2,64,512]{2,1,0:T(8,128)(2,1)S(1)} %get-tuple-element.144), channel_id=1, source_target_pairs={{0,3},{1,2},{2,1},{3,0},{4,7},{5,6},{6,5},{7,4},{8,11},{9,10},{10,... | collective-permute-start | bytes 393224 | tf_op jit(solution)/shard_map/ppermute | solution.py:327
  131.4 19.6 %collective-permute-start.56 = (bf16[2,64,512]{2,1,0:T(8,128)(2,1)S(1)}, bf16[2,64,512]{2,1,0:T(8,128)(2,1)S(1)}, u32[]{:S(2)}, u32[]{:S(2)}) collective-permute-start(bf16[2,64,512]{2,1,0:T(8,128)(2,1)S(1)} %get-tuple-element.145), channel_id=1, source_target_pairs={{0,4},{1,5},{2,6},{3,7},{4,0},{5,1},{6,2},{7,3},{8,12},{9,13},{10,... | collective-permute-start | bytes 393224 | tf_op jit(solution)/shard_map/ppermute | solution.py:327
  137.5 16.7 %collective-permute-start.57 = (bf16[2,64,512]{2,1,0:T(8,128)(2,1)S(1)}, bf16[2,64,512]{2,1,0:T(8,128)(2,1)S(1)}, u32[]{:S(2)}, u32[]{:S(2)}) collective-permute-start(bf16[2,64,512]{2,1,0:T(8,128)(2,1)S(1)} %get-tuple-element.146), channel_id=1, source_target_pairs={{0,5},{1,4},{2,7},{3,6},{4,1},{5,0},{6,3},{7,2},{8,13},{9,12},{10,... | collective-permute-start | bytes 393224 | tf_op jit(solution)/shard_map/ppermute | solution.py:327
  137.5 16.7 %collective-permute-start.58 = (bf16[2,64,512]{2,1,0:T(8,128)(2,1)S(1)}, bf16[2,64,512]{2,1,0:T(8,128)(2,1)S(1)}, u32[]{:S(2)}, u32[]{:S(2)}) collective-permute-start(bf16[2,64,512]{2,1,0:T(8,128)(2,1)S(1)} %get-tuple-element.147), channel_id=1, source_target_pairs={{0,6},{1,7},{2,4},{3,5},{4,2},{5,3},{6,0},{7,1},{8,14},{9,15},{10,... | collective-permute-start | bytes 393224 | tf_op jit(solution)/shard_map/ppermute | solution.py:327
  139.8 18.6 %collective-permute-start.59 = (bf16[2,64,512]{2,1,0:T(8,128)(2,1)S(1)}, bf16[2,64,512]{2,1,0:T(8,128)(2,1)S(1)}, u32[]{:S(2)}, u32[]{:S(2)}) collective-permute-start(bf16[2,64,512]{2,1,0:T(8,128)(2,1)S(1)} %get-tuple-element.148), channel_id=1, source_target_pairs={{0,7},{1,6},{2,5},{3,4},{4,3},{5,2},{6,1},{7,0},{8,15},{9,14},{10,... | collective-permute-start | bytes 393224 | tf_op jit(solution)/shard_map/ppermute | solution.py:327
  144.6 18.8 %collective-permute-start.39 = (bf16[2,64,256]{2,1,0:T(8,128)(2,1)S(1)}, bf16[2,64,256]{2,1,0:T(8,128)(2,1)S(1)}, u32[]{:S(2)}, u32[]{:S(2)}) collective-permute-start(bf16[2,64,256]{2,1,0:T(8,128)(2,1)S(1)} %get-tuple-element.126), channel_id=1, source_target_pairs={{0,1},{1,0},{2,3},{3,2},{4,5},{5,4},{6,7},{7,6},{8,9},{9,8},{10,11... | collective-permute-start | bytes 196616 | tf_op jit(solution)/shard_map/ppermute | solution.py:327
  151.0 14.3 %collective-permute-start.40 = (bf16[2,64,256]{2,1,0:T(8,128)(2,1)S(1)}, bf16[2,64,256]{2,1,0:T(8,128)(2,1)S(1)}, u32[]{:S(2)}, u32[]{:S(2)}) collective-permute-start(bf16[2,64,256]{2,1,0:T(8,128)(2,1)S(1)} %get-tuple-element.127), channel_id=1, source_target_pairs={{0,2},{1,3},{2,0},{3,1},{4,6},{5,7},{6,4},{7,5},{8,10},{9,11},{10,... | collective-permute-start | bytes 196616 | tf_op jit(solution)/shard_map/ppermute | solution.py:327
  154.2 14.5 %collective-permute-start.41 = (bf16[2,64,256]{2,1,0:T(8,128)(2,1)S(1)}, bf16[2,64,256]{2,1,0:T(8,128)(2,1)S(1)}, u32[]{:S(2)}, u32[]{:S(2)}) collective-permute-start(bf16[2,64,256]{2,1,0:T(8,128)(2,1)S(1)} %get-tuple-element.128), channel_id=1, source_target_pairs={{0,3},{1,2},{2,1},{3,0},{4,7},{5,6},{6,5},{7,4},{8,11},{9,10},{10,... | collective-permute-start | bytes 196616 | tf_op jit(solution)/shard_map/ppermute | solution.py:327
  154.2 14.5 %collective-permute-start.42 = (bf16[2,64,256]{2,1,0:T(8,128)(2,1)S(1)}, bf16[2,64,256]{2,1,0:T(8,128)(2,1)S(1)}, u32[]{:S(2)}, u32[]{:S(2)}) collective-permute-start(bf16[2,64,256]{2,1,0:T(8,128)(2,1)S(1)} %get-tuple-element.129), channel_id=1, source_target_pairs={{0,4},{1,5},{2,6},{3,7},{4,0},{5,1},{6,2},{7,3},{8,12},{9,13},{10,... | collective-permute-start | bytes 196616 | tf_op jit(solution)/shard_map/ppermute | solution.py:327
  158.3 10.4 %collective-permute-start.43 = (bf16[2,64,256]{2,1,0:T(8,128)(2,1)S(1)}, bf16[2,64,256]{2,1,0:T(8,128)(2,1)S(1)}, u32[]{:S(2)}, u32[]{:S(2)}) collective-permute-start(bf16[2,64,256]{2,1,0:T(8,128)(2,1)S(1)} %get-tuple-element.130), channel_id=1, source_target_pairs={{0,5},{1,4},{2,7},{3,6},{4,1},{5,0},{6,3},{7,2},{8,13},{9,12},{10,... | collective-permute-start | bytes 196616 | tf_op jit(solution)/shard_map/ppermute | solution.py:327
  163.4 6.1 %collective-permute-start.44 = (bf16[2,64,256]{2,1,0:T(8,128)(2,1)S(1)}, bf16[2,64,256]{2,1,0:T(8,128)(2,1)S(1)}, u32[]{:S(2)}, u32[]{:S(2)}) collective-permute-start(bf16[2,64,256]{2,1,0:T(8,128)(2,1)S(1)} %get-tuple-element.131), channel_id=1, source_target_pairs={{0,6},{1,7},{2,4},{3,5},{4,2},{5,3},{6,0},{7,1},{8,14},{9,15},{10,... | collective-permute-start | bytes 196616 | tf_op jit(solution)/shard_map/ppermute | solution.py:327
  165.3 7.0 %collective-permute-start.45 = (bf16[2,64,256]{2,1,0:T(8,128)(2,1)S(1)}, bf16[2,64,256]{2,1,0:T(8,128)(2,1)S(1)}, u32[]{:S(2)}, u32[]{:S(2)}) collective-permute-start(bf16[2,64,256]{2,1,0:T(8,128)(2,1)S(1)} %get-tuple-element.132), channel_id=1, source_target_pairs={{0,7},{1,6},{2,5},{3,4},{4,3},{5,2},{6,1},{7,0},{8,15},{9,14},{10,... | collective-permute-start | bytes 196616 | tf_op jit(solution)/shard_map/ppermute | solution.py:327

commit v4 on v3

--- a/solution.py
+++ b/solution.py
@@ -96,7 +96,6 @@
 KERNEL_BYTES = 24 << 20
 FIRST_BYTES = 53 << 20
 LOAD_BYTES = 50 << 20
-PIECES = 1
 KERNEL_FLOPS = 1 << 31
 
 
@@ -146,29 +145,17 @@
     blocks, operators, (traces, sources, sems) = refs[: len(ks)], refs[len(ks)], refs[-3:]
     wanted = pl.ds(first, columns)
     here = [pl.ds(row_start(k, rows), rows) for k in ks]
-    depth = operators.shape[1] // PIECES
-    depths = [slice(n * depth, (n + 1) * depth) for n in range(PIECES)]
-    pairs = [(traces_ref.at[:, r, :], traces.at[n]) for n, r in enumerate(here)]
-    for d in depths:
-        for part in range(2):
-            pairs.append((operators_ref.at[part, d, wanted], operators.at[part, d]))
+    pairs = [(operators_ref.at[part, :, wanted], operators.at[part]) for part in range(2)]
+    pairs += [(traces_ref.at[:, r, :], traces.at[n]) for n, r in enumerate(here)]
     pairs += [(sources_ref.at[:, r, wanted], sources.at[n]) for n, r in enumerate(here)]
     copies = start_all(pairs, sems)
-    rows_here, pieces, late = copies[: len(ks)], copies[len(ks) : -len(ks)], copies[-len(ks) :]
-    for copy in rows_here:
+    needed, late = copies[: -len(ks)], copies[-len(ks) :]
+    for copy in needed:
         copy.wait()
-    results = [0.0, 0.0]
-    for n, d in enumerate(depths):
-        for copy in pieces[2 * n : 2 * n + 2]:
-            copy.wait()
-        real, imag = (
-            jnp.concatenate([traces[k, part, :, d] for k in range(len(ks))], axis=0)
-            for part in range(2)
-        )
-        for part in range(2):
-            results[part] = results[part] + part_products(
-                part, real, imag, [operators[p, d] for p in range(2)]
-            )
+    real, imag = (
+        jnp.concatenate([traces[n, part] for n in range(len(ks))], axis=0) for part in range(2)
+    )
+    results = [part_products(part, real, imag, operators) for part in range(2)]
     for copy in late:
         copy.wait()
     finish(range(len(ks)), rows, slice(0, columns), pick_block, results, sources, blocks)
@@ -305,7 +292,11 @@
 
 def partners(count_y, count_z):
     across = range(1, count_y * count_z)
-    return sorted(across, key=lambda k: (2 * (k // count_z) < count_y, k % count_z, k))
+    far = [k for k in across if 2 * (k // count_z) >= count_y]
+    near = [k for k in across if k not in far]
+    return sorted(far, key=lambda k: (k % count_z, k)) + sorted(
+        near, key=lambda k: (-(k % count_z), k)
+    )
 
 
 def far_and_near(count_y, count_z):
@@ -366,7 +357,7 @@
                 scratch=[
                     pltpu.VMEM((len(ks), 2, rows, columns_all), dtype),
                     pltpu.VMEM((len(ks), 2, rows, columns), dtype),
-                    pltpu.SemaphoreType.DMA((2 * len(ks) + 2 * PIECES,)),
+                    pltpu.SemaphoreType.DMA((2 * len(ks) + 2,)),
                 ],
                 limit=FIRST_BYTES,
             )(trace_rows, source_rows, operators)

time: 173 us -> 171 us (0.988)
  no operation moved by 1% of the time
where the time goes in v4:
time: 171 us
  starting transfers between devices  99.9 us (58%)
  waiting for transfers between devices  47.7 us (28%)
  Pallas kernels  23.2 us (14%)
    ppermute x56, starting transfers between devices, exchange(): lax.ppermute(blocks[k], ('gy', 'gz'), [(p, p ^ k) for p in range(plane_si...  98.1 us
    ppermute x56, waiting for transfers between devices, exchange(): lax.ppermute(blocks[k], ('gy', 'gz'), [(p, p ^ k) for p in range(plane_si...  43.7 us
    pallas_call x4, Pallas kernels, mix(): call(functools.partial(mix_blocks, plane_size, plans[group]), [VMEM] * pl...  7.15 us
    pallas_call x7, Pallas kernels, solve(): call(functools.partial(solve_blocks, ks, rows, first, columns, pick, 1 if...  5.74 us
    ppermute x2, waiting for transfers between devices, few_subdomains(): from_low = lax.ppermute(high, 'gx', forward)  4.06 us
  transfers between devices with their start and end apart: 60, of which 16 were waited for; matrix products, arithmetic and copies ran while one was open for 0% of the time, Pallas kernels for 11%

profile of v4, /device:TPU:0, one launch (start us, length us, event | category | flops | bytes accessed | tf_op | source)
XLA Modules:
  0.0 171.3 jit_solution(4586458887143442521)
XLA Ops:
  0.0 3.2 %shard_map.60 = (bf16[2,64,512]{2,1,0:T(8,128)(2,1)S(1)}, bf16[2,64,512]{2,1,0:T(8,128)(2,1)S(1)}, bf16[2,768,512]{2,1,0:T(8,128)(2,1)}) custom-call(bf16[2,512,768]{2,1,0:T(8,128)(2,1)} %bitcast.13, bf16[2,512,768]{2,1,0:T(8,128)(2,1)} %bitcast.15, bf16[2,768,768]{2,1,0:T(8,128)(2,1)} %bitcast.11), custom_call_target="tpu_custom_call" | custom-call | flops 2147483648 | bytes 1048576 | tf_op jit(solution)/shard_map/pallas_call | solution.py:353
  3.2 4.1 %collective-permute-start.19 = (bf16[2,64,512]{2,1,0:T(8,128)(2,1)S(1)}, bf16[2,64,512]{2,1,0:T(8,128)(2,1)S(1)}, u32[]{:S(2)}, u32[]{:S(2)}) collective-permute-start(bf16[2,64,512]{2,1,0:T(8,128)(2,1)S(1)} %get-tuple-element.103), channel_id=1, source_target_pairs={{0,4},{1,5},{2,6},{3,7},{4,0},{5,1},{6,2},{7,3},{8,12},{9,13},{10,... | collective-permute-start | bytes 393224 | tf_op jit(solution)/shard_map/ppermute | solution.py:318
  7.4 1.3 collective-permute-start.21
  8.7 2.3 %shard_map.55 = (bf16[8,2,64,768]{3,2,1,0:T(8,128)(2,1)S(1)}, bf16[8,2,64,768]{3,2,1,0:T(8,128)(2,1)S(1)}, bf16[2,768,256]{2,1,0:T(8,128)(2,1)S(1)}) custom-call(bf16[2,512,768]{2,1,0:T(8,128)(2,1)} %bitcast.14, bf16[2,512,768]{2,1,0:T(8,128)(2,1)} %bitcast.16, bf16[2,768,768]{2,1,0:T(8,128)(2,1)} %bitcast.12), custom_call_target="tpu_custom_call" | custom-call | flops 2147483648 | bytes 1048576 | tf_op jit(solution)/shard_map/pallas_call | solution.py:378
  11.7 2.7 %collective-permute-start.20 = (bf16[2,64,512]{2,1,0:T(8,128)(2,1)S(1)}, bf16[2,64,512]{2,1,0:T(8,128)(2,1)S(1)}, u32[]{:S(2)}, u32[]{:S(2)}) collective-permute-start(bf16[2,64,512]{2,1,0:T(8,128)(2,1)S(1)} %get-tuple-element.104), channel_id=1, source_target_pairs={{0,5},{1,4},{2,7},{3,6},{4,1},{5,0},{6,3},{7,2},{8,13},{9,12},{10,... | collective-permute-start | bytes 393224 | tf_op jit(solution)/shard_map/ppermute | solution.py:318
  15.5 1.7 %collective-permute-start.1 = (bf16[8,2,64,128]{3,2,1,0:T(8,128)(2,1)S(1)}, bf16[8,2,64,128]{3,2,1,0:T(8,128)(2,1)S(1)}, u32[]{:S(2)}, u32[]{:S(2)}) collective-permute-start(bf16[8,2,64,128]{3,2,1,0:T(8,128)(2,1)S(1)} %get-tuple-element.81), channel_id=1, source_target_pairs={{8,0},{16,8},{24,16},{0,24},{9,1},{17,9},{25,17},{1,25},{10,2},{18... | collective-permute-start | bytes 786440 | tf_op jit(solution)/shard_map/ppermute | solution.py:425
  18.2 4.1 %collective-permute-done.from_low_ref = bf16[8,2,64,128]{3,2,1,0:T(8,128)(2,1)S(1)} collective-permute-done((bf16[8,2,64,128]{3,2,1,0:T(8,128)(2,1)S(1)}, bf16[8,2,64,128]{3,2,1,0:T(8,128)(2,1)S(1)}, u32[]{:S(2)}, u32[]{:S(2)}) %collective-permute-start) | collective-permute-done | bytes 262176 | tf_op jit(solution)/shard_map/ppermute | solution.py:424
  22.2 1.2 collective-permute-start.22
  23.4 1.5 collective-permute-start.16
  25.7 1.4 collective-permute-start.18
  27.1 1.5 collective-permute-start.2
  28.6 2.7 %collective-permute-done.22.refs_7_ = bf16[2,64,512]{2,1,0:T(8,128)(2,1)S(1)} collective-permute-done((bf16[2,64,512]{2,1,0:T(8,128)(2,1)S(1)}, bf16[2,64,512]{2,1,0:T(8,128)(2,1)S(1)}, u32[]{:S(2)}, u32[]{:S(2)}) %collective-permute-start.22) | collective-permute-done | bytes 131104 | tf_op jit(solution)/shard_map/ppermute | solution.py:318
  31.4 1.9 %collective-permute-start.3 = (bf16[2,64,256]{2,1,0:T(8,128)(2,1)S(1)}, bf16[2,64,256]{2,1,0:T(8,128)(2,1)S(1)}, u32[]{:S(2)}, u32[]{:S(2)}) collective-permute-start(bf16[2,64,256]{2,1,0:T(8,128)(2,1)S(1)} %get-tuple-element.84), channel_id=1, source_target_pairs={{0,2},{1,3},{2,0},{3,1},{4,6},{5,7},{6,4},{7,5},{8,10},{9,11},{10,... | collective-permute-start | bytes 196616 | tf_op jit(solution)/shard_map/ppermute | solution.py:318
  33.3 2.7 %shard_map.58.refs_8_ = f32[5,8,8]{2,1,0:T(8,128)S(1)} custom-call(f32[8,8]{1,0:T(8,128)S(1)} %bitcast_convert_fusion.coupling_ref, s32[8]{0:T(128)S(1)} %bitcast.10), custom_call_target="tpu_custom_call" | custom-call | flops 2147483648 | bytes 1048576 | tf_op jit(solution)/shard_map/pallas_call | solution.py:404
  36.1 3.5 %collective-permute-start.5 = (bf16[2,64,256]{2,1,0:T(8,128)(2,1)S(1)}, bf16[2,64,256]{2,1,0:T(8,128)(2,1)S(1)}, u32[]{:S(2)}, u32[]{:S(2)}) collective-permute-start(bf16[2,64,256]{2,1,0:T(8,128)(2,1)S(1)} %get-tuple-element.86), channel_id=1, source_target_pairs={{0,4},{1,5},{2,6},{3,7},{4,0},{5,1},{6,2},{7,3},{8,12},{9,13},{10,... | collective-permute-start | bytes 196616 | tf_op jit(solution)/shard_map/ppermute | solution.py:318
  39.6 1.1 collective-permute-start.6
  40.7 2.3 %collective-permute-start.7 = (bf16[2,64,256]{2,1,0:T(8,128)(2,1)S(1)}, bf16[2,64,256]{2,1,0:T(8,128)(2,1)S(1)}, u32[]{:S(2)}, u32[]{:S(2)}) collective-permute-start(bf16[2,64,256]{2,1,0:T(8,128)(2,1)S(1)} %get-tuple-element.88), channel_id=1, source_target_pairs={{0,6},{1,7},{2,4},{3,5},{4,2},{5,3},{6,0},{7,1},{8,14},{9,15},{10,... | collective-permute-start | bytes 196616 | tf_op jit(solution)/shard_map/ppermute | solution.py:318
  43.0 1.5 collective-permute-start.8
  44.6 2.1 %shard_map.63 = (bf16[2,64,512]{2,1,0:T(8,128)(2,1)S(1)}, bf16[2,64,512]{2,1,0:T(8,128)(2,1)S(1)}, bf16[2,64,512]{2,1,0:T(8,128)(2,1)S(1)}, bf16[2,64,512]{2,1,0...) custom-call(bf16[2,64,512]{2,1,0:T(8,128)(2,1)S(1)} %get-tuple-eleme, ...), custom_call_target="tpu_custom_call" | custom-call | flops 2147483648 | bytes 1048576 | tf_op jit(solution)/shard_map/pallas_call | solution.py:387
  46.7 1.5 collective-permute-start.23
  48.6 1.6 collective-permute-start.25
  50.6 1.5 shard_map.59
  52.1 1.2 collective-permute-start.9
  53.3 2.0 %collective-permute-start.10 = (bf16[2,64,256]{2,1,0:T(8,128)(2,1)S(1)}, bf16[2,64,256]{2,1,0:T(8,128)(2,1)S(1)}, u32[]{:S(2)}, u32[]{:S(2)}) collective-permute-start(bf16[2,64,256]{2,1,0:T(8,128)(2,1)S(1)} %get-tuple-element.92), channel_id=1, source_target_pairs={{0,2},{1,3},{2,0},{3,1},{4,6},{5,7},{6,4},{7,5},{8,10},{9,11},{10,... | collective-permute-start | bytes 196616 | tf_op jit(solution)/shard_map/ppermute | solution.py:318
  55.2 1.4 collective-permute-start.11
  56.6 2.2 %collective-permute-start.26 = (bf16[2,64,512]{2,1,0:T(8,128)(2,1)S(1)}, bf16[2,64,512]{2,1,0:T(8,128)(2,1)S(1)}, u32[]{:S(2)}, u32[]{:S(2)}) collective-permute-start(bf16[2,64,512]{2,1,0:T(8,128)(2,1)S(1)} %get-tuple-element.111), channel_id=1, source_target_pairs={{0,4},{1,5},{2,6},{3,7},{4,0},{5,1},{6,2},{7,3},{8,12},{9,13},{10,... | collective-permute-start | bytes 393224 | tf_op jit(solution)/shard_map/ppermute | solution.py:318
  59.6 3.3 %collective-permute-start.29 = (bf16[2,64,512]{2,1,0:T(8,128)(2,1)S(1)}, bf16[2,64,512]{2,1,0:T(8,128)(2,1)S(1)}, u32[]{:S(2)}, u32[]{:S(2)}) collective-permute-start(bf16[2,64,512]{2,1,0:T(8,128)(2,1)S(1)} %get-tuple-element.114), channel_id=1, source_target_pairs={{0,7},{1,6},{2,5},{3,4},{4,3},{5,2},{6,1},{7,0},{8,15},{9,14},{10,... | collective-permute-start | bytes 393224 | tf_op jit(solution)/shard_map/ppermute | solution.py:318
  63.5 3.0 %collective-permute-start.15 = (bf16[2,64,256]{2,1,0:T(8,128)(2,1)S(1)}, bf16[2,64,256]{2,1,0:T(8,128)(2,1)S(1)}, u32[]{:S(2)}, u32[]{:S(2)}) collective-permute-start(bf16[2,64,256]{2,1,0:T(8,128)(2,1)S(1)} %get-tuple-element.97), channel_id=1, source_target_pairs={{0,7},{1,6},{2,5},{3,4},{4,3},{5,2},{6,1},{7,0},{8,15},{9,14},{10,... | collective-permute-start | bytes 196616 | tf_op jit(solution)/shard_map/ppermute | solution.py:318
  66.5 1.0 shard_map.67
  67.5 10.0 %collective-permute-done.27.refs_13_.refs_2_ = bf16[2,64,512]{2,1,0:T(8,128)(2,1)S(1)} collective-permute-done((bf16[2,64,512]{2,1,0:T(8,128)(2,1)S(1)}, bf16[2,64,512]{2,1,0:T(8,128)(2,1)S(1)}, u32[]{:S(2)}, u32[]{:S(2)}) %collective-permute-start.27) | collective-permute-done | bytes 131104 | tf_op jit(solution)/shard_map/ppermute | solution.py:318
  77.5 1.5 collective-permute-start.28
  79.1 4.0 %collective-permute-start.12 = (bf16[2,64,256]{2,1,0:T(8,128)(2,1)S(1)}, bf16[2,64,256]{2,1,0:T(8,128)(2,1)S(1)}, u32[]{:S(2)}, u32[]{:S(2)}) collective-permute-start(bf16[2,64,256]{2,1,0:T(8,128)(2,1)S(1)} %get-tuple-element.94), channel_id=1, source_target_pairs={{0,4},{1,5},{2,6},{3,7},{4,0},{5,1},{6,2},{7,3},{8,12},{9,13},{10,... | collective-permute-start | bytes 196616 | tf_op jit(solution)/shard_map/ppermute | solution.py:318
  83.1 2.9 %collective-permute-done.13.refs_5_.refs_0_ = bf16[2,64,256]{2,1,0:T(8,128)(2,1)S(1)} collective-permute-done((bf16[2,64,256]{2,1,0:T(8,128)(2,1)S(1)}, bf16[2,64,256]{2,1,0:T(8,128)(2,1)S(1)}, u32[]{:S(2)}, u32[]{:S(2)}) %collective-permute-start.13) | collective-permute-done | bytes 65568 | tf_op jit(solution)/shard_map/ppermute | solution.py:318
  86.0 1.5 collective-permute-start.14
  87.5 1.8 %collective-permute-start.46 = (bf16[2,64,512]{2,1,0:T(8,128)(2,1)S(1)}, bf16[2,64,512]{2,1,0:T(8,128)(2,1)S(1)}, u32[]{:S(2)}, u32[]{:S(2)}) collective-permute-start(bf16[2,64,512]{2,1,0:T(8,128)(2,1)S(1)} %get-tuple-element.134), channel_id=1, source_target_pairs={{0,1},{1,0},{2,3},{3,2},{4,5},{5,4},{6,7},{7,6},{8,9},{9,8},{10,11... | collective-permute-start | bytes 393224 | tf_op jit(solution)/shard_map/ppermute | solution.py:318
  90.4 1.3 collective-permute-start.48
  91.7 2.5 %collective-permute-start.50 = (bf16[2,64,512]{2,1,0:T(8,128)(2,1)S(1)}, bf16[2,64,512]{2,1,0:T(8,128)(2,1)S(1)}, u32[]{:S(2)}, u32[]{:S(2)}) collective-permute-start(bf16[2,64,512]{2,1,0:T(8,128)(2,1)S(1)} %get-tuple-element.138), channel_id=1, source_target_pairs={{0,5},{1,4},{2,7},{3,6},{4,1},{5,0},{6,3},{7,2},{8,13},{9,12},{10,... | collective-permute-start | bytes 393224 | tf_op jit(solution)/shard_map/ppermute | solution.py:318
  94.1 1.4 collective-permute-start.52
  96.1 1.4 collective-permute-start.49
  97.8 1.9 %collective-permute-start.51 = (bf16[2,64,512]{2,1,0:T(8,128)(2,1)S(1)}, bf16[2,64,512]{2,1,0:T(8,128)(2,1)S(1)}, u32[]{:S(2)}, u32[]{:S(2)}) collective-permute-start(bf16[2,64,512]{2,1,0:T(8,128)(2,1)S(1)} %get-tuple-element.139), channel_id=1, source_target_pairs={{0,6},{1,7},{2,4},{3,5},{4,2},{5,3},{6,0},{7,1},{8,14},{9,15},{10,... | collective-permute-start | bytes 393224 | tf_op jit(solution)/shard_map/ppermute | solution.py:318
  99.7 1.0 shard_map.64
  100.8 7.9 %collective-permute-done.50.refs_5_ = bf16[2,64,512]{2,1,0:T(8,128)(2,1)S(1)} collective-permute-done((bf16[2,64,512]{2,1,0:T(8,128)(2,1)S(1)}, bf16[2,64,512]{2,1,0:T(8,128)(2,1)S(1)}, u32[]{:S(2)}, u32[]{:S(2)}) %collective-permute-start.50) | collective-permute-done | bytes 131104 | tf_op jit(solution)/shard_map/ppermute | solution.py:318
  108.7 5.3 %collective-permute-done.49.refs_4_ = bf16[2,64,512]{2,1,0:T(8,128)(2,1)S(1)} collective-permute-done((bf16[2,64,512]{2,1,0:T(8,128)(2,1)S(1)}, bf16[2,64,512]{2,1,0:T(8,128)(2,1)S(1)}, u32[]{:S(2)}, u32[]{:S(2)}) %collective-permute-start.49) | collective-permute-done | bytes 131104 | tf_op jit(solution)/shard_map/ppermute | solution.py:318
  114.0 2.1 %shard_map.70 = (bf16[2,64,512]{2,1,0:T(8,128)(2,1)S(1)}, bf16[2,64,512]{2,1,0:T(8,128)(2,1)S(1)}, bf16[2,64,512]{2,1,0:T(8,128)(2,1)S(1)}, bf16[2,64,512]{2,1,0...) custom-call(bf16[2,64,512]{2,1,0:T(8,128)(2,1)S(1)} %get-tuple-eleme, ...), custom_call_target="tpu_custom_call" | custom-call | flops 2147483648 | bytes 1048576 | tf_op jit(solution)/shard_map/pallas_call | solution.py:387
  116.8 2.0 %collective-permute-start.54 = (bf16[2,64,512]{2,1,0:T(8,128)(2,1)S(1)}, bf16[2,64,512]{2,1,0:T(8,128)(2,1)S(1)}, u32[]{:S(2)}, u32[]{:S(2)}) collective-permute-start(bf16[2,64,512]{2,1,0:T(8,128)(2,1)S(1)} %get-tuple-element.143), channel_id=1, source_target_pairs={{0,2},{1,3},{2,0},{3,1},{4,6},{5,7},{6,4},{7,5},{8,10},{9,11},{10,... | collective-permute-start | bytes 393224 | tf_op jit(solution)/shard_map/ppermute | solution.py:318
  118.9 1.4 collective-permute-start.32
  120.4 2.1 %collective-permute-start.34 = (bf16[2,64,256]{2,1,0:T(8,128)(2,1)S(1)}, bf16[2,64,256]{2,1,0:T(8,128)(2,1)S(1)}, u32[]{:S(2)}, u32[]{:S(2)}) collective-permute-start(bf16[2,64,256]{2,1,0:T(8,128)(2,1)S(1)} %get-tuple-element.120), channel_id=1, source_target_pairs={{0,3},{1,2},{2,1},{3,0},{4,7},{5,6},{6,5},{7,4},{8,11},{9,10},{10,... | collective-permute-start | bytes 196616 | tf_op jit(solution)/shard_map/ppermute | solution.py:318
  122.4 1.4 collective-permute-start.35
  124.0 2.2 %collective-permute-start.36 = (bf16[2,64,256]{2,1,0:T(8,128)(2,1)S(1)}, bf16[2,64,256]{2,1,0:T(8,128)(2,1)S(1)}, u32[]{:S(2)}, u32[]{:S(2)}) collective-permute-start(bf16[2,64,256]{2,1,0:T(8,128)(2,1)S(1)} %get-tuple-element.122), channel_id=1, source_target_pairs={{0,5},{1,4},{2,7},{3,6},{4,1},{5,0},{6,3},{7,2},{8,13},{9,12},{10,... | collective-permute-start | bytes 196616 | tf_op jit(solution)/shard_map/ppermute | solution.py:318
  126.2 2.1 %collective-permute-start.37 = (bf16[2,64,256]{2,1,0:T(8,128)(2,1)S(1)}, bf16[2,64,256]{2,1,0:T(8,128)(2,1)S(1)}, u32[]{:S(2)}, u32[]{:S(2)}) collective-permute-start(bf16[2,64,256]{2,1,0:T(8,128)(2,1)S(1)} %get-tuple-element.123), channel_id=1, source_target_pairs={{0,6},{1,7},{2,4},{3,5},{4,2},{5,3},{6,0},{7,1},{8,14},{9,15},{10,... | collective-permute-start | bytes 196616 | tf_op jit(solution)/shard_map/ppermute | solution.py:318
  128.3 1.8 %collective-permute-start.38 = (bf16[2,64,256]{2,1,0:T(8,128)(2,1)S(1)}, bf16[2,64,256]{2,1,0:T(8,128)(2,1)S(1)}, u32[]{:S(2)}, u32[]{:S(2)}) collective-permute-start(bf16[2,64,256]{2,1,0:T(8,128)(2,1)S(1)} %get-tuple-element.124), channel_id=1, source_target_pairs={{0,7},{1,6},{2,5},{3,4},{4,3},{5,2},{6,1},{7,0},{8,15},{9,14},{10,... | collective-permute-start | bytes 196616 | tf_op jit(solution)/shard_map/ppermute | solution.py:318
  130.5 3.1 %collective-permute-start.56 = (bf16[2,64,512]{2,1,0:T(8,128)(2,1)S(1)}, bf16[2,64,512]{2,1,0:T(8,128)(2,1)S(1)}, u32[]{:S(2)}, u32[]{:S(2)}) collective-permute-start(bf16[2,64,512]{2,1,0:T(8,128)(2,1)S(1)} %get-tuple-element.145), channel_id=1, source_target_pairs={{0,4},{1,5},{2,6},{3,7},{4,0},{5,1},{6,2},{7,3},{8,12},{9,13},{10,... | collective-permute-start | bytes 393224 | tf_op jit(solution)/shard_map/ppermute | solution.py:318
  133.6 4.7 %collective-permute-done.36.refs_5_ = bf16[2,64,256]{2,1,0:T(8,128)(2,1)S(1)} collective-permute-done((bf16[2,64,256]{2,1,0:T(8,128)(2,1)S(1)}, bf16[2,64,256]{2,1,0:T(8,128)(2,1)S(1)}, u32[]{:S(2)}, u32[]{:S(2)}) %collective-permute-start.36) | collective-permute-done | bytes 65568 | tf_op jit(solution)/shard_map/ppermute | solution.py:318
  138.7 3.2 %collective-permute-start.59 = (bf16[2,64,512]{2,1,0:T(8,128)(2,1)S(1)}, bf16[2,64,512]{2,1,0:T(8,128)(2,1)S(1)}, u32[]{:S(2)}, u32[]{:S(2)}) collective-permute-start(bf16[2,64,512]{2,1,0:T(8,128)(2,1)S(1)} %get-tuple-element.148), channel_id=1, source_target_pairs={{0,7},{1,6},{2,5},{3,4},{4,3},{5,2},{6,1},{7,0},{8,15},{9,14},{10,... | collective-permute-start | bytes 393224 | tf_op jit(solution)/shard_map/ppermute | solution.py:318
  141.9 1.5 shard_map.66
  143.4 1.8 %collective-permute-start.39 = (bf16[2,64,256]{2,1,0:T(8,128)(2,1)S(1)}, bf16[2,64,256]{2,1,0:T(8,128)(2,1)S(1)}, u32[]{:S(2)}, u32[]{:S(2)}) collective-permute-start(bf16[2,64,256]{2,1,0:T(8,128)(2,1)S(1)} %get-tuple-element.126), channel_id=1, source_target_pairs={{0,1},{1,0},{2,3},{3,2},{4,5},{5,4},{6,7},{7,6},{8,9},{9,8},{10,11... | collective-permute-start | bytes 196616 | tf_op jit(solution)/shard_map/ppermute | solution.py:318
  145.2 5.4 %collective-permute-done.56.refs_4_ = bf16[2,64,512]{2,1,0:T(8,128)(2,1)S(1)} collective-permute-done((bf16[2,64,512]{2,1,0:T(8,128)(2,1)S(1)}, bf16[2,64,512]{2,1,0:T(8,128)(2,1)S(1)}, u32[]{:S(2)}, u32[]{:S(2)}) %collective-permute-start.56) | collective-permute-done | bytes 131104 | tf_op jit(solution)/shard_map/ppermute | solution.py:318
  150.6 2.3 %collective-permute-start.40 = (bf16[2,64,256]{2,1,0:T(8,128)(2,1)S(1)}, bf16[2,64,256]{2,1,0:T(8,128)(2,1)S(1)}, u32[]{:S(2)}, u32[]{:S(2)}) collective-permute-start(bf16[2,64,256]{2,1,0:T(8,128)(2,1)S(1)} %get-tuple-element.127), channel_id=1, source_target_pairs={{0,2},{1,3},{2,0},{3,1},{4,6},{5,7},{6,4},{7,5},{8,10},{9,11},{10,... | collective-permute-start | bytes 196616 | tf_op jit(solution)/shard_map/ppermute | solution.py:318
  152.9 1.2 collective-permute-done.57.refs_5_
  154.0 3.6 %collective-permute-start.42 = (bf16[2,64,256]{2,1,0:T(8,128)(2,1)S(1)}, bf16[2,64,256]{2,1,0:T(8,128)(2,1)S(1)}, u32[]{:S(2)}, u32[]{:S(2)}) collective-permute-start(bf16[2,64,256]{2,1,0:T(8,128)(2,1)S(1)} %get-tuple-element.129), channel_id=1, source_target_pairs={{0,4},{1,5},{2,6},{3,7},{4,0},{5,1},{6,2},{7,3},{8,12},{9,13},{10,... | collective-permute-start | bytes 196616 | tf_op jit(solution)/shard_map/ppermute | solution.py:318
  157.7 5.1 %collective-permute-start.43 = (bf16[2,64,256]{2,1,0:T(8,128)(2,1)S(1)}, bf16[2,64,256]{2,1,0:T(8,128)(2,1)S(1)}, u32[]{:S(2)}, u32[]{:S(2)}) collective-permute-start(bf16[2,64,256]{2,1,0:T(8,128)(2,1)S(1)} %get-tuple-element.130), channel_id=1, source_target_pairs={{0,5},{1,4},{2,7},{3,6},{4,1},{5,0},{6,3},{7,2},{8,13},{9,12},{10,... | collective-permute-start | bytes 196616 | tf_op jit(solution)/shard_map/ppermute | solution.py:318
  163.3 4.1 %collective-permute-start.45 = (bf16[2,64,256]{2,1,0:T(8,128)(2,1)S(1)}, bf16[2,64,256]{2,1,0:T(8,128)(2,1)S(1)}, u32[]{:S(2)}, u32[]{:S(2)}) collective-permute-start(bf16[2,64,256]{2,1,0:T(8,128)(2,1)S(1)} %get-tuple-element.132), channel_id=1, source_target_pairs={{0,7},{1,6},{2,5},{3,4},{4,3},{5,2},{6,1},{7,0},{8,15},{9,14},{10,... | collective-permute-start | bytes 196616 | tf_op jit(solution)/shard_map/ppermute | solution.py:318
  167.4 1.0 shard_map.71.refs_8_
  168.8 1.5 collective-permute-done.45.refs_7_
  (81 shorter events, 11.2 us)
Async XLA Ops:
  3.2 21.8 %collective-permute-start.19 = (bf16[2,64,512]{2,1,0:T(8,128)(2,1)S(1)}, bf16[2,64,512]{2,1,0:T(8,128)(2,1)S(1)}, u32[]{:S(2)}, u32[]{:S(2)}) collective-permute-start(bf16[2,64,512]{2,1,0:T(8,128)(2,1)S(1)} %get-tuple-element.103), channel_id=1, source_target_pairs={{0,4},{1,5},{2,6},{3,7},{4,0},{5,1},{6,2},{7,3},{8,12},{9,13},{10,... | collective-permute-start | bytes 393224 | tf_op jit(solution)/shard_map/ppermute | solution.py:318
  7.4 3.7 %copy-start.1 = (bf16[2,768,512]{2,1,0:T(8,128)(2,1)S(1)}, bf16[2,768,512]{2,1,0:T(8,128)(2,1)}, u32[]{:S(2)}) copy-start(bf16[2,768,512]{2,1,0:T(8,128)(2,1)} %get-tuple-element.98.refs_2_.refs_9_.refs_5_) | copy-start | bytes 4718596
  7.4 18.3 %collective-permute-start.21 = (bf16[2,64,512]{2,1,0:T(8,128)(2,1)S(1)}, bf16[2,64,512]{2,1,0:T(8,128)(2,1)S(1)}, u32[]{:S(2)}, u32[]{:S(2)}) collective-permute-start(bf16[2,64,512]{2,1,0:T(8,128)(2,1)S(1)} %get-tuple-element.105), channel_id=1, source_target_pairs={{0,6},{1,7},{2,4},{3,5},{4,2},{5,3},{6,0},{7,1},{8,14},{9,15},{10,... | collective-permute-start | bytes 393224 | tf_op jit(solution)/shard_map/ppermute | solution.py:318
  11.7 15.4 %collective-permute-start.20 = (bf16[2,64,512]{2,1,0:T(8,128)(2,1)S(1)}, bf16[2,64,512]{2,1,0:T(8,128)(2,1)S(1)}, u32[]{:S(2)}, u32[]{:S(2)}) collective-permute-start(bf16[2,64,512]{2,1,0:T(8,128)(2,1)S(1)} %get-tuple-element.104), channel_id=1, source_target_pairs={{0,5},{1,4},{2,7},{3,6},{4,1},{5,0},{6,3},{7,2},{8,13},{9,12},{10,... | collective-permute-start | bytes 393224 | tf_op jit(solution)/shard_map/ppermute | solution.py:318
  15.4 6.9 %collective-permute-start = (bf16[8,2,64,128]{3,2,1,0:T(8,128)(2,1)S(1)}, bf16[8,2,64,128]{3,2,1,0:T(8,128)(2,1)S(1)}, u32[]{:S(2)}, u32[]{:S(2)}) collective-permute-start(bf16[8,2,64,128]{3,2,1,0:T(8,128)(2,1)S(1)} %get-tuple-element.80), channel_id=1, source_target_pairs={{0,8},{8,16},{16,24},{24,0},{1,9},{9,17},{17,25},{25,1},{2,10},{10... | collective-permute-start | bytes 786440 | tf_op jit(solution)/shard_map/ppermute | solution.py:424
  15.4 2.7 %copy-start.2 = (bf16[1,8,8]{2,1,0:T(8,128)(2,1)S(1)}, bf16[1,8,8]{2,1,0:T(8,128)(2,1)}, u32[]{:S(2)}) copy-start(bf16[1,8,8]{2,1,0:T(8,128)(2,1)} %param.8) | copy-start | bytes 388
  15.5 8.0 %collective-permute-start.1 = (bf16[8,2,64,128]{3,2,1,0:T(8,128)(2,1)S(1)}, bf16[8,2,64,128]{3,2,1,0:T(8,128)(2,1)S(1)}, u32[]{:S(2)}, u32[]{:S(2)}) collective-permute-start(bf16[8,2,64,128]{3,2,1,0:T(8,128)(2,1)S(1)} %get-tuple-element.81), channel_id=1, source_target_pairs={{8,0},{16,8},{24,16},{0,24},{9,1},{17,9},{25,17},{1,25},{10,2},{18... | collective-permute-start | bytes 786440 | tf_op jit(solution)/shard_map/ppermute | solution.py:425
  22.2 9.1 %collective-permute-start.22 = (bf16[2,64,512]{2,1,0:T(8,128)(2,1)S(1)}, bf16[2,64,512]{2,1,0:T(8,128)(2,1)S(1)}, u32[]{:S(2)}, u32[]{:S(2)}) collective-permute-start(bf16[2,64,512]{2,1,0:T(8,128)(2,1)S(1)} %get-tuple-element.106), channel_id=1, source_target_pairs={{0,7},{1,6},{2,5},{3,4},{4,3},{5,2},{6,1},{7,0},{8,15},{9,14},{10,... | collective-permute-start | bytes 393224 | tf_op jit(solution)/shard_map/ppermute | solution.py:318
  23.4 9.9 %copy-start = (s32[1,8]{1,0:T(1,128)S(1)}, s32[1,8]{1,0:T(1,128)}, u32[]{:S(2)}) copy-start(s32[1,8]{1,0:T(1,128)} %param.9) | copy-start | bytes 100
  23.4 12.6 %collective-permute-start.16 = (bf16[2,64,512]{2,1,0:T(8,128)(2,1)S(1)}, bf16[2,64,512]{2,1,0:T(8,128)(2,1)S(1)}, u32[]{:S(2)}, u32[]{:S(2)}) collective-permute-start(bf16[2,64,512]{2,1,0:T(8,128)(2,1)S(1)} %get-tuple-element.100), channel_id=1, source_target_pairs={{0,1},{1,0},{2,3},{3,2},{4,5},{5,4},{6,7},{7,6},{8,9},{9,8},{10,11... | collective-permute-start | bytes 393224 | tf_op jit(solution)/shard_map/ppermute | solution.py:318
  25.0 11.1 %collective-permute-start.17 = (bf16[2,64,512]{2,1,0:T(8,128)(2,1)S(1)}, bf16[2,64,512]{2,1,0:T(8,128)(2,1)S(1)}, u32[]{:S(2)}, u32[]{:S(2)}) collective-permute-start(bf16[2,64,512]{2,1,0:T(8,128)(2,1)S(1)} %get-tuple-element.101), channel_id=1, source_target_pairs={{0,2},{1,3},{2,0},{3,1},{4,6},{5,7},{6,4},{7,5},{8,10},{9,11},{10,... | collective-permute-start | bytes 393224 | tf_op jit(solution)/shard_map/ppermute | solution.py:318
  25.7 13.9 %collective-permute-start.18 = (bf16[2,64,512]{2,1,0:T(8,128)(2,1)S(1)}, bf16[2,64,512]{2,1,0:T(8,128)(2,1)S(1)}, u32[]{:S(2)}, u32[]{:S(2)}) collective-permute-start(bf16[2,64,512]{2,1,0:T(8,128)(2,1)S(1)} %get-tuple-element.102), channel_id=1, source_target_pairs={{0,3},{1,2},{2,1},{3,0},{4,7},{5,6},{6,5},{7,4},{8,11},{9,10},{10,... | collective-permute-start | bytes 393224 | tf_op jit(solution)/shard_map/ppermute | solution.py:318
  27.1 13.6 %collective-permute-start.2 = (bf16[2,64,256]{2,1,0:T(8,128)(2,1)S(1)}, bf16[2,64,256]{2,1,0:T(8,128)(2,1)S(1)}, u32[]{:S(2)}, u32[]{:S(2)}) collective-permute-start(bf16[2,64,256]{2,1,0:T(8,128)(2,1)S(1)} %get-tuple-element.83), channel_id=1, source_target_pairs={{0,1},{1,0},{2,3},{3,2},{4,5},{5,4},{6,7},{7,6},{8,9},{9,8},{10,11... | collective-permute-start | bytes 196616 | tf_op jit(solution)/shard_map/ppermute | solution.py:318
  31.4 11.7 %collective-permute-start.3 = (bf16[2,64,256]{2,1,0:T(8,128)(2,1)S(1)}, bf16[2,64,256]{2,1,0:T(8,128)(2,1)S(1)}, u32[]{:S(2)}, u32[]{:S(2)}) collective-permute-start(bf16[2,64,256]{2,1,0:T(8,128)(2,1)S(1)} %get-tuple-element.84), channel_id=1, source_target_pairs={{0,2},{1,3},{2,0},{3,1},{4,6},{5,7},{6,4},{7,5},{8,10},{9,11},{10,... | collective-permute-start | bytes 196616 | tf_op jit(solution)/shard_map/ppermute | solution.py:318
  36.0 10.7 %collective-permute-start.4 = (bf16[2,64,256]{2,1,0:T(8,128)(2,1)S(1)}, bf16[2,64,256]{2,1,0:T(8,128)(2,1)S(1)}, u32[]{:S(2)}, u32[]{:S(2)}) collective-permute-start(bf16[2,64,256]{2,1,0:T(8,128)(2,1)S(1)} %get-tuple-element.85), channel_id=1, source_target_pairs={{0,3},{1,2},{2,1},{3,0},{4,7},{5,6},{6,5},{7,4},{8,11},{9,10},{10,... | collective-permute-start | bytes 196616 | tf_op jit(solution)/shard_map/ppermute | solution.py:318
  36.1 12.1 %collective-permute-start.5 = (bf16[2,64,256]{2,1,0:T(8,128)(2,1)S(1)}, bf16[2,64,256]{2,1,0:T(8,128)(2,1)S(1)}, u32[]{:S(2)}, u32[]{:S(2)}) collective-permute-start(bf16[2,64,256]{2,1,0:T(8,128)(2,1)S(1)} %get-tuple-element.86), channel_id=1, source_target_pairs={{0,4},{1,5},{2,6},{3,7},{4,0},{5,1},{6,2},{7,3},{8,12},{9,13},{10,... | collective-permute-start | bytes 196616 | tf_op jit(solution)/shard_map/ppermute | solution.py:318
  39.6 9.0 %collective-permute-start.6 = (bf16[2,64,256]{2,1,0:T(8,128)(2,1)S(1)}, bf16[2,64,256]{2,1,0:T(8,128)(2,1)S(1)}, u32[]{:S(2)}, u32[]{:S(2)}) collective-permute-start(bf16[2,64,256]{2,1,0:T(8,128)(2,1)S(1)} %get-tuple-element.87), channel_id=1, source_target_pairs={{0,5},{1,4},{2,7},{3,6},{4,1},{5,0},{6,3},{7,2},{8,13},{9,12},{10,... | collective-permute-start | bytes 196616 | tf_op jit(solution)/shard_map/ppermute | solution.py:318
  40.7 9.5 %collective-permute-start.7 = (bf16[2,64,256]{2,1,0:T(8,128)(2,1)S(1)}, bf16[2,64,256]{2,1,0:T(8,128)(2,1)S(1)}, u32[]{:S(2)}, u32[]{:S(2)}) collective-permute-start(bf16[2,64,256]{2,1,0:T(8,128)(2,1)S(1)} %get-tuple-element.88), channel_id=1, source_target_pairs={{0,6},{1,7},{2,4},{3,5},{4,2},{5,3},{6,0},{7,1},{8,14},{9,15},{10,... | collective-permute-start | bytes 196616 | tf_op jit(solution)/shard_map/ppermute | solution.py:318
  43.0 7.6 %collective-permute-start.8 = (bf16[2,64,256]{2,1,0:T(8,128)(2,1)S(1)}, bf16[2,64,256]{2,1,0:T(8,128)(2,1)S(1)}, u32[]{:S(2)}, u32[]{:S(2)}) collective-permute-start(bf16[2,64,256]{2,1,0:T(8,128)(2,1)S(1)} %get-tuple-element.89), channel_id=1, source_target_pairs={{0,7},{1,6},{2,5},{3,4},{4,3},{5,2},{6,1},{7,0},{8,15},{9,14},{10,... | collective-permute-start | bytes 196616 | tf_op jit(solution)/shard_map/ppermute | solution.py:318
  46.7 8.6 %collective-permute-start.23 = (bf16[2,64,512]{2,1,0:T(8,128)(2,1)S(1)}, bf16[2,64,512]{2,1,0:T(8,128)(2,1)S(1)}, u32[]{:S(2)}, u32[]{:S(2)}) collective-permute-start(bf16[2,64,512]{2,1,0:T(8,128)(2,1)S(1)} %get-tuple-element.108), channel_id=1, source_target_pairs={{0,1},{1,0},{2,3},{3,2},{4,5},{5,4},{6,7},{7,6},{8,9},{9,8},{10,11... | collective-permute-start | bytes 393224 | tf_op jit(solution)/shard_map/ppermute | solution.py:318
  48.2 8.4 %collective-permute-start.24 = (bf16[2,64,512]{2,1,0:T(8,128)(2,1)S(1)}, bf16[2,64,512]{2,1,0:T(8,128)(2,1)S(1)}, u32[]{:S(2)}, u32[]{:S(2)}) collective-permute-start(bf16[2,64,512]{2,1,0:T(8,128)(2,1)S(1)} %get-tuple-element.109), channel_id=1, source_target_pairs={{0,2},{1,3},{2,0},{3,1},{4,6},{5,7},{6,4},{7,5},{8,10},{9,11},{10,... | collective-permute-start | bytes 393224 | tf_op jit(solution)/shard_map/ppermute | solution.py:318
  48.6 10.2 %collective-permute-start.25 = (bf16[2,64,512]{2,1,0:T(8,128)(2,1)S(1)}, bf16[2,64,512]{2,1,0:T(8,128)(2,1)S(1)}, u32[]{:S(2)}, u32[]{:S(2)}) collective-permute-start(bf16[2,64,512]{2,1,0:T(8,128)(2,1)S(1)} %get-tuple-element.110), channel_id=1, source_target_pairs={{0,3},{1,2},{2,1},{3,0},{4,7},{5,6},{6,5},{7,4},{8,11},{9,10},{10,... | collective-permute-start | bytes 393224 | tf_op jit(solution)/shard_map/ppermute | solution.py:318
  52.1 7.5 %collective-permute-start.9 = (bf16[2,64,256]{2,1,0:T(8,128)(2,1)S(1)}, bf16[2,64,256]{2,1,0:T(8,128)(2,1)S(1)}, u32[]{:S(2)}, u32[]{:S(2)}) collective-permute-start(bf16[2,64,256]{2,1,0:T(8,128)(2,1)S(1)} %get-tuple-element.91), channel_id=1, source_target_pairs={{0,1},{1,0},{2,3},{3,2},{4,5},{5,4},{6,7},{7,6},{8,9},{9,8},{10,11... | collective-permute-start | bytes 196616 | tf_op jit(solution)/shard_map/ppermute | solution.py:318
  53.3 9.7 %collective-permute-start.10 = (bf16[2,64,256]{2,1,0:T(8,128)(2,1)S(1)}, bf16[2,64,256]{2,1,0:T(8,128)(2,1)S(1)}, u32[]{:S(2)}, u32[]{:S(2)}) collective-permute-start(bf16[2,64,256]{2,1,0:T(8,128)(2,1)S(1)} %get-tuple-element.92), channel_id=1, source_target_pairs={{0,2},{1,3},{2,0},{3,1},{4,6},{5,7},{6,4},{7,5},{8,10},{9,11},{10,... | collective-permute-start | bytes 196616 | tf_op jit(solution)/shard_map/ppermute | solution.py:318
  55.2 8.2 %collective-permute-start.11 = (bf16[2,64,256]{2,1,0:T(8,128)(2,1)S(1)}, bf16[2,64,256]{2,1,0:T(8,128)(2,1)S(1)}, u32[]{:S(2)}, u32[]{:S(2)}) collective-permute-start(bf16[2,64,256]{2,1,0:T(8,128)(2,1)S(1)} %get-tuple-element.93), channel_id=1, source_target_pairs={{0,3},{1,2},{2,1},{3,0},{4,7},{5,6},{6,5},{7,4},{8,11},{9,10},{10,... | collective-permute-start | bytes 196616 | tf_op jit(solution)/shard_map/ppermute | solution.py:318
  56.6 33.3 %collective-permute-start.26 = (bf16[2,64,512]{2,1,0:T(8,128)(2,1)S(1)}, bf16[2,64,512]{2,1,0:T(8,128)(2,1)S(1)}, u32[]{:S(2)}, u32[]{:S(2)}) collective-permute-start(bf16[2,64,512]{2,1,0:T(8,128)(2,1)S(1)} %get-tuple-element.111), channel_id=1, source_target_pairs={{0,4},{1,5},{2,6},{3,7},{4,0},{5,1},{6,2},{7,3},{8,12},{9,13},{10,... | collective-permute-start | bytes 393224 | tf_op jit(solution)/shard_map/ppermute | solution.py:318
  58.9 18.7 %collective-permute-start.27 = (bf16[2,64,512]{2,1,0:T(8,128)(2,1)S(1)}, bf16[2,64,512]{2,1,0:T(8,128)(2,1)S(1)}, u32[]{:S(2)}, u32[]{:S(2)}) collective-permute-start(bf16[2,64,512]{2,1,0:T(8,128)(2,1)S(1)} %get-tuple-element.112), channel_id=1, source_target_pairs={{0,5},{1,4},{2,7},{3,6},{4,1},{5,0},{6,3},{7,2},{8,13},{9,12},{10,... | collective-permute-start | bytes 393224 | tf_op jit(solution)/shard_map/ppermute | solution.py:318
  59.6 19.4 %collective-permute-start.29 = (bf16[2,64,512]{2,1,0:T(8,128)(2,1)S(1)}, bf16[2,64,512]{2,1,0:T(8,128)(2,1)S(1)}, u32[]{:S(2)}, u32[]{:S(2)}) collective-permute-start(bf16[2,64,512]{2,1,0:T(8,128)(2,1)S(1)} %get-tuple-element.114), channel_id=1, source_target_pairs={{0,7},{1,6},{2,5},{3,4},{4,3},{5,2},{6,1},{7,0},{8,15},{9,14},{10,... | collective-permute-start | bytes 393224 | tf_op jit(solution)/shard_map/ppermute | solution.py:318
  62.9 23.0 %collective-permute-start.13 = (bf16[2,64,256]{2,1,0:T(8,128)(2,1)S(1)}, bf16[2,64,256]{2,1,0:T(8,128)(2,1)S(1)}, u32[]{:S(2)}, u32[]{:S(2)}) collective-permute-start(bf16[2,64,256]{2,1,0:T(8,128)(2,1)S(1)} %get-tuple-element.95), channel_id=1, source_target_pairs={{0,5},{1,4},{2,7},{3,6},{4,1},{5,0},{6,3},{7,2},{8,13},{9,12},{10,... | collective-permute-start | bytes 196616 | tf_op jit(solution)/shard_map/ppermute | solution.py:318
  63.5 24.0 %collective-permute-start.15 = (bf16[2,64,256]{2,1,0:T(8,128)(2,1)S(1)}, bf16[2,64,256]{2,1,0:T(8,128)(2,1)S(1)}, u32[]{:S(2)}, u32[]{:S(2)}) collective-permute-start(bf16[2,64,256]{2,1,0:T(8,128)(2,1)S(1)} %get-tuple-element.97), channel_id=1, source_target_pairs={{0,7},{1,6},{2,5},{3,4},{4,3},{5,2},{6,1},{7,0},{8,15},{9,14},{10,... | collective-permute-start | bytes 196616 | tf_op jit(solution)/shard_map/ppermute | solution.py:318
  77.5 12.9 %collective-permute-start.28 = (bf16[2,64,512]{2,1,0:T(8,128)(2,1)S(1)}, bf16[2,64,512]{2,1,0:T(8,128)(2,1)S(1)}, u32[]{:S(2)}, u32[]{:S(2)}) collective-permute-start(bf16[2,64,512]{2,1,0:T(8,128)(2,1)S(1)} %get-tuple-element.113), channel_id=1, source_target_pairs={{0,6},{1,7},{2,4},{3,5},{4,2},{5,3},{6,0},{7,1},{8,14},{9,15},{10,... | collective-permute-start | bytes 393224 | tf_op jit(solution)/shard_map/ppermute | solution.py:318
  79.1 12.6 %collective-permute-start.12 = (bf16[2,64,256]{2,1,0:T(8,128)(2,1)S(1)}, bf16[2,64,256]{2,1,0:T(8,128)(2,1)S(1)}, u32[]{:S(2)}, u32[]{:S(2)}) collective-permute-start(bf16[2,64,256]{2,1,0:T(8,128)(2,1)S(1)} %get-tuple-element.94), channel_id=1, source_target_pairs={{0,4},{1,5},{2,6},{3,7},{4,0},{5,1},{6,2},{7,3},{8,12},{9,13},{10,... | collective-permute-start | bytes 196616 | tf_op jit(solution)/shard_map/ppermute | solution.py:318
  86.0 8.2 %collective-permute-start.14 = (bf16[2,64,256]{2,1,0:T(8,128)(2,1)S(1)}, bf16[2,64,256]{2,1,0:T(8,128)(2,1)S(1)}, u32[]{:S(2)}, u32[]{:S(2)}) collective-permute-start(bf16[2,64,256]{2,1,0:T(8,128)(2,1)S(1)} %get-tuple-element.96), channel_id=1, source_target_pairs={{0,6},{1,7},{2,4},{3,5},{4,2},{5,3},{6,0},{7,1},{8,14},{9,15},{10,... | collective-permute-start | bytes 196616 | tf_op jit(solution)/shard_map/ppermute | solution.py:318
  87.5 8.6 %collective-permute-start.46 = (bf16[2,64,512]{2,1,0:T(8,128)(2,1)S(1)}, bf16[2,64,512]{2,1,0:T(8,128)(2,1)S(1)}, u32[]{:S(2)}, u32[]{:S(2)}) collective-permute-start(bf16[2,64,512]{2,1,0:T(8,128)(2,1)S(1)} %get-tuple-element.134), channel_id=1, source_target_pairs={{0,1},{1,0},{2,3},{3,2},{4,5},{5,4},{6,7},{7,6},{8,9},{9,8},{10,11... | collective-permute-start | bytes 393224 | tf_op jit(solution)/shard_map/ppermute | solution.py:318
  89.9 7.9 %collective-permute-start.47 = (bf16[2,64,512]{2,1,0:T(8,128)(2,1)S(1)}, bf16[2,64,512]{2,1,0:T(8,128)(2,1)S(1)}, u32[]{:S(2)}, u32[]{:S(2)}) collective-permute-start(bf16[2,64,512]{2,1,0:T(8,128)(2,1)S(1)} %get-tuple-element.135), channel_id=1, source_target_pairs={{0,2},{1,3},{2,0},{3,1},{4,6},{5,7},{6,4},{7,5},{8,10},{9,11},{10,... | collective-permute-start | bytes 393224 | tf_op jit(solution)/shard_map/ppermute | solution.py:318
  90.4 10.3 %collective-permute-start.48 = (bf16[2,64,512]{2,1,0:T(8,128)(2,1)S(1)}, bf16[2,64,512]{2,1,0:T(8,128)(2,1)S(1)}, u32[]{:S(2)}, u32[]{:S(2)}) collective-permute-start(bf16[2,64,512]{2,1,0:T(8,128)(2,1)S(1)} %get-tuple-element.136), channel_id=1, source_target_pairs={{0,3},{1,2},{2,1},{3,0},{4,7},{5,6},{6,5},{7,4},{8,11},{9,10},{10,... | collective-permute-start | bytes 393224 | tf_op jit(solution)/shard_map/ppermute | solution.py:318
  91.7 17.0 %collective-permute-start.50 = (bf16[2,64,512]{2,1,0:T(8,128)(2,1)S(1)}, bf16[2,64,512]{2,1,0:T(8,128)(2,1)S(1)}, u32[]{:S(2)}, u32[]{:S(2)}) collective-permute-start(bf16[2,64,512]{2,1,0:T(8,128)(2,1)S(1)} %get-tuple-element.138), channel_id=1, source_target_pairs={{0,5},{1,4},{2,7},{3,6},{4,1},{5,0},{6,3},{7,2},{8,13},{9,12},{10,... | collective-permute-start | bytes 393224 | tf_op jit(solution)/shard_map/ppermute | solution.py:318
  94.1 14.5 %collective-permute-start.52 = (bf16[2,64,512]{2,1,0:T(8,128)(2,1)S(1)}, bf16[2,64,512]{2,1,0:T(8,128)(2,1)S(1)}, u32[]{:S(2)}, u32[]{:S(2)}) collective-permute-start(bf16[2,64,512]{2,1,0:T(8,128)(2,1)S(1)} %get-tuple-element.140), channel_id=1, source_target_pairs={{0,7},{1,6},{2,5},{3,4},{4,3},{5,2},{6,1},{7,0},{8,15},{9,14},{10,... | collective-permute-start | bytes 393224 | tf_op jit(solution)/shard_map/ppermute | solution.py:318
  96.1 17.8 %collective-permute-start.49 = (bf16[2,64,512]{2,1,0:T(8,128)(2,1)S(1)}, bf16[2,64,512]{2,1,0:T(8,128)(2,1)S(1)}, u32[]{:S(2)}, u32[]{:S(2)}) collective-permute-start(bf16[2,64,512]{2,1,0:T(8,128)(2,1)S(1)} %get-tuple-element.137), channel_id=1, source_target_pairs={{0,4},{1,5},{2,6},{3,7},{4,0},{5,1},{6,2},{7,3},{8,12},{9,13},{10,... | collective-permute-start | bytes 393224 | tf_op jit(solution)/shard_map/ppermute | solution.py:318
  97.8 16.1 %collective-permute-start.51 = (bf16[2,64,512]{2,1,0:T(8,128)(2,1)S(1)}, bf16[2,64,512]{2,1,0:T(8,128)(2,1)S(1)}, u32[]{:S(2)}, u32[]{:S(2)}) collective-permute-start(bf16[2,64,512]{2,1,0:T(8,128)(2,1)S(1)} %get-tuple-element.139), channel_id=1, source_target_pairs={{0,6},{1,7},{2,4},{3,5},{4,2},{5,3},{6,0},{7,1},{8,14},{9,15},{10,... | collective-permute-start | bytes 393224 | tf_op jit(solution)/shard_map/ppermute | solution.py:318
  100.7 18.1 %collective-permute-start.30 = (bf16[8,2,64,128]{3,2,1,0:T(8,128)(2,1)S(1)}, bf16[8,2,64,128]{3,2,1,0:T(8,128)(2,1)S(1)}, u32[]{:S(2)}, u32[]{:S(2)}) collective-permute-start(bf16[8,2,64,128]{3,2,1,0:T(8,128)(2,1)S(1)} %get-tuple-element.115), channel_id=1, source_target_pairs={{0,8},{8,16},{16,24},{24,0},{1,9},{9,17},{17,25},{25,1},{2,10},{10... | collective-permute-start | bytes 786440 | tf_op jit(solution)/shard_map/ppermute | solution.py:424
  108.6 10.1 %collective-permute-start.31 = (bf16[8,2,64,128]{3,2,1,0:T(8,128)(2,1)S(1)}, bf16[8,2,64,128]{3,2,1,0:T(8,128)(2,1)S(1)}, u32[]{:S(2)}, u32[]{:S(2)}) collective-permute-start(bf16[8,2,64,128]{3,2,1,0:T(8,128)(2,1)S(1)} %get-tuple-element.116), channel_id=1, source_target_pairs={{8,0},{16,8},{24,16},{0,24},{9,1},{17,9},{25,17},{1,25},{10,2},{18... | collective-permute-start | bytes 786440 | tf_op jit(solution)/shard_map/ppermute | solution.py:425
  116.1 6.4 %collective-permute-start.53 = (bf16[2,64,512]{2,1,0:T(8,128)(2,1)S(1)}, bf16[2,64,512]{2,1,0:T(8,128)(2,1)S(1)}, u32[]{:S(2)}, u32[]{:S(2)}) collective-permute-start(bf16[2,64,512]{2,1,0:T(8,128)(2,1)S(1)} %get-tuple-element.142), channel_id=1, source_target_pairs={{0,1},{1,0},{2,3},{3,2},{4,5},{5,4},{6,7},{7,6},{8,9},{9,8},{10,11... | collective-permute-start | bytes 393224 | tf_op jit(solution)/shard_map/ppermute | solution.py:318
  116.8 7.2 %collective-permute-start.54 = (bf16[2,64,512]{2,1,0:T(8,128)(2,1)S(1)}, bf16[2,64,512]{2,1,0:T(8,128)(2,1)S(1)}, u32[]{:S(2)}, u32[]{:S(2)}) collective-permute-start(bf16[2,64,512]{2,1,0:T(8,128)(2,1)S(1)} %get-tuple-element.143), channel_id=1, source_target_pairs={{0,2},{1,3},{2,0},{3,1},{4,6},{5,7},{6,4},{7,5},{8,10},{9,11},{10,... | collective-permute-start | bytes 393224 | tf_op jit(solution)/shard_map/ppermute | solution.py:318
  118.9 7.3 %collective-permute-start.32 = (bf16[2,64,256]{2,1,0:T(8,128)(2,1)S(1)}, bf16[2,64,256]{2,1,0:T(8,128)(2,1)S(1)}, u32[]{:S(2)}, u32[]{:S(2)}) collective-permute-start(bf16[2,64,256]{2,1,0:T(8,128)(2,1)S(1)} %get-tuple-element.118), channel_id=1, source_target_pairs={{0,1},{1,0},{2,3},{3,2},{4,5},{5,4},{6,7},{7,6},{8,9},{9,8},{10,11... | collective-permute-start | bytes 196616 | tf_op jit(solution)/shard_map/ppermute | solution.py:318
  120.3 8.0 %collective-permute-start.33 = (bf16[2,64,256]{2,1,0:T(8,128)(2,1)S(1)}, bf16[2,64,256]{2,1,0:T(8,128)(2,1)S(1)}, u32[]{:S(2)}, u32[]{:S(2)}) collective-permute-start(bf16[2,64,256]{2,1,0:T(8,128)(2,1)S(1)} %get-tuple-element.119), channel_id=1, source_target_pairs={{0,2},{1,3},{2,0},{3,1},{4,6},{5,7},{6,4},{7,5},{8,10},{9,11},{10,... | collective-permute-start | bytes 196616 | tf_op jit(solution)/shard_map/ppermute | solution.py:318
  120.4 9.7 %collective-permute-start.34 = (bf16[2,64,256]{2,1,0:T(8,128)(2,1)S(1)}, bf16[2,64,256]{2,1,0:T(8,128)(2,1)S(1)}, u32[]{:S(2)}, u32[]{:S(2)}) collective-permute-start(bf16[2,64,256]{2,1,0:T(8,128)(2,1)S(1)} %get-tuple-element.120), channel_id=1, source_target_pairs={{0,3},{1,2},{2,1},{3,0},{4,7},{5,6},{6,5},{7,4},{8,11},{9,10},{10,... | collective-permute-start | bytes 196616 | tf_op jit(solution)/shard_map/ppermute | solution.py:318
  122.4 8.1 %collective-permute-start.35 = (bf16[2,64,256]{2,1,0:T(8,128)(2,1)S(1)}, bf16[2,64,256]{2,1,0:T(8,128)(2,1)S(1)}, u32[]{:S(2)}, u32[]{:S(2)}) collective-permute-start(bf16[2,64,256]{2,1,0:T(8,128)(2,1)S(1)} %get-tuple-element.121), channel_id=1, source_target_pairs={{0,4},{1,5},{2,6},{3,7},{4,0},{5,1},{6,2},{7,3},{8,12},{9,13},{10,... | collective-permute-start | bytes 196616 | tf_op jit(solution)/shard_map/ppermute | solution.py:318
  124.0 14.4 %collective-permute-start.36 = (bf16[2,64,256]{2,1,0:T(8,128)(2,1)S(1)}, bf16[2,64,256]{2,1,0:T(8,128)(2,1)S(1)}, u32[]{:S(2)}, u32[]{:S(2)}) collective-permute-start(bf16[2,64,256]{2,1,0:T(8,128)(2,1)S(1)} %get-tuple-element.122), channel_id=1, source_target_pairs={{0,5},{1,4},{2,7},{3,6},{4,1},{5,0},{6,3},{7,2},{8,13},{9,12},{10,... | collective-permute-start | bytes 196616 | tf_op jit(solution)/shard_map/ppermute | solution.py:318
  126.2 12.2 %collective-permute-start.37 = (bf16[2,64,256]{2,1,0:T(8,128)(2,1)S(1)}, bf16[2,64,256]{2,1,0:T(8,128)(2,1)S(1)}, u32[]{:S(2)}, u32[]{:S(2)}) collective-permute-start(bf16[2,64,256]{2,1,0:T(8,128)(2,1)S(1)} %get-tuple-element.123), channel_id=1, source_target_pairs={{0,6},{1,7},{2,4},{3,5},{4,2},{5,3},{6,0},{7,1},{8,14},{9,15},{10,... | collective-permute-start | bytes 196616 | tf_op jit(solution)/shard_map/ppermute | solution.py:318
  128.3 10.4 %collective-permute-start.38 = (bf16[2,64,256]{2,1,0:T(8,128)(2,1)S(1)}, bf16[2,64,256]{2,1,0:T(8,128)(2,1)S(1)}, u32[]{:S(2)}, u32[]{:S(2)}) collective-permute-start(bf16[2,64,256]{2,1,0:T(8,128)(2,1)S(1)} %get-tuple-element.124), channel_id=1, source_target_pairs={{0,7},{1,6},{2,5},{3,4},{4,3},{5,2},{6,1},{7,0},{8,15},{9,14},{10,... | collective-permute-start | bytes 196616 | tf_op jit(solution)/shard_map/ppermute | solution.py:318
  130.1 13.3 %collective-permute-start.55 = (bf16[2,64,512]{2,1,0:T(8,128)(2,1)S(1)}, bf16[2,64,512]{2,1,0:T(8,128)(2,1)S(1)}, u32[]{:S(2)}, u32[]{:S(2)}) collective-permute-start(bf16[2,64,512]{2,1,0:T(8,128)(2,1)S(1)} %get-tuple-element.144), channel_id=1, source_target_pairs={{0,3},{1,2},{2,1},{3,0},{4,7},{5,6},{6,5},{7,4},{8,11},{9,10},{10,... | collective-permute-start | bytes 393224 | tf_op jit(solution)/shard_map/ppermute | solution.py:318
  130.5 20.1 %collective-permute-start.56 = (bf16[2,64,512]{2,1,0:T(8,128)(2,1)S(1)}, bf16[2,64,512]{2,1,0:T(8,128)(2,1)S(1)}, u32[]{:S(2)}, u32[]{:S(2)}) collective-permute-start(bf16[2,64,512]{2,1,0:T(8,128)(2,1)S(1)} %get-tuple-element.145), channel_id=1, source_target_pairs={{0,4},{1,5},{2,6},{3,7},{4,0},{5,1},{6,2},{7,3},{8,12},{9,13},{10,... | collective-permute-start | bytes 393224 | tf_op jit(solution)/shard_map/ppermute | solution.py:318
  138.3 15.7 %collective-permute-start.57 = (bf16[2,64,512]{2,1,0:T(8,128)(2,1)S(1)}, bf16[2,64,512]{2,1,0:T(8,128)(2,1)S(1)}, u32[]{:S(2)}, u32[]{:S(2)}) collective-permute-start(bf16[2,64,512]{2,1,0:T(8,128)(2,1)S(1)} %get-tuple-element.146), channel_id=1, source_target_pairs={{0,5},{1,4},{2,7},{3,6},{4,1},{5,0},{6,3},{7,2},{8,13},{9,12},{10,... | collective-permute-start | bytes 393224 | tf_op jit(solution)/shard_map/ppermute | solution.py:318
  138.3 15.7 %collective-permute-start.58 = (bf16[2,64,512]{2,1,0:T(8,128)(2,1)S(1)}, bf16[2,64,512]{2,1,0:T(8,128)(2,1)S(1)}, u32[]{:S(2)}, u32[]{:S(2)}) collective-permute-start(bf16[2,64,512]{2,1,0:T(8,128)(2,1)S(1)} %get-tuple-element.147), channel_id=1, source_target_pairs={{0,6},{1,7},{2,4},{3,5},{4,2},{5,3},{6,0},{7,1},{8,14},{9,15},{10,... | collective-permute-start | bytes 393224 | tf_op jit(solution)/shard_map/ppermute | solution.py:318
  138.7 18.9 %collective-permute-start.59 = (bf16[2,64,512]{2,1,0:T(8,128)(2,1)S(1)}, bf16[2,64,512]{2,1,0:T(8,128)(2,1)S(1)}, u32[]{:S(2)}, u32[]{:S(2)}) collective-permute-start(bf16[2,64,512]{2,1,0:T(8,128)(2,1)S(1)} %get-tuple-element.148), channel_id=1, source_target_pairs={{0,7},{1,6},{2,5},{3,4},{4,3},{5,2},{6,1},{7,0},{8,15},{9,14},{10,... | collective-permute-start | bytes 393224 | tf_op jit(solution)/shard_map/ppermute | solution.py:318
  143.4 19.3 %collective-permute-start.39 = (bf16[2,64,256]{2,1,0:T(8,128)(2,1)S(1)}, bf16[2,64,256]{2,1,0:T(8,128)(2,1)S(1)}, u32[]{:S(2)}, u32[]{:S(2)}) collective-permute-start(bf16[2,64,256]{2,1,0:T(8,128)(2,1)S(1)} %get-tuple-element.126), channel_id=1, source_target_pairs={{0,1},{1,0},{2,3},{3,2},{4,5},{5,4},{6,7},{7,6},{8,9},{9,8},{10,11... | collective-permute-start | bytes 196616 | tf_op jit(solution)/shard_map/ppermute | solution.py:318
  150.6 12.7 %collective-permute-start.40 = (bf16[2,64,256]{2,1,0:T(8,128)(2,1)S(1)}, bf16[2,64,256]{2,1,0:T(8,128)(2,1)S(1)}, u32[]{:S(2)}, u32[]{:S(2)}) collective-permute-start(bf16[2,64,256]{2,1,0:T(8,128)(2,1)S(1)} %get-tuple-element.127), channel_id=1, source_target_pairs={{0,2},{1,3},{2,0},{3,1},{4,6},{5,7},{6,4},{7,5},{8,10},{9,11},{10,... | collective-permute-start | bytes 196616 | tf_op jit(solution)/shard_map/ppermute | solution.py:318
  154.0 14.4 %collective-permute-start.41 = (bf16[2,64,256]{2,1,0:T(8,128)(2,1)S(1)}, bf16[2,64,256]{2,1,0:T(8,128)(2,1)S(1)}, u32[]{:S(2)}, u32[]{:S(2)}) collective-permute-start(bf16[2,64,256]{2,1,0:T(8,128)(2,1)S(1)} %get-tuple-element.128), channel_id=1, source_target_pairs={{0,3},{1,2},{2,1},{3,0},{4,7},{5,6},{6,5},{7,4},{8,11},{9,10},{10,... | collective-permute-start | bytes 196616 | tf_op jit(solution)/shard_map/ppermute | solution.py:318
  154.0 14.4 %collective-permute-start.42 = (bf16[2,64,256]{2,1,0:T(8,128)(2,1)S(1)}, bf16[2,64,256]{2,1,0:T(8,128)(2,1)S(1)}, u32[]{:S(2)}, u32[]{:S(2)}) collective-permute-start(bf16[2,64,256]{2,1,0:T(8,128)(2,1)S(1)} %get-tuple-element.129), channel_id=1, source_target_pairs={{0,4},{1,5},{2,6},{3,7},{4,0},{5,1},{6,2},{7,3},{8,12},{9,13},{10,... | collective-permute-start | bytes 196616 | tf_op jit(solution)/shard_map/ppermute | solution.py:318
  157.7 10.8 %collective-permute-start.43 = (bf16[2,64,256]{2,1,0:T(8,128)(2,1)S(1)}, bf16[2,64,256]{2,1,0:T(8,128)(2,1)S(1)}, u32[]{:S(2)}, u32[]{:S(2)}) collective-permute-start(bf16[2,64,256]{2,1,0:T(8,128)(2,1)S(1)} %get-tuple-element.130), channel_id=1, source_target_pairs={{0,5},{1,4},{2,7},{3,6},{4,1},{5,0},{6,3},{7,2},{8,13},{9,12},{10,... | collective-permute-start | bytes 196616 | tf_op jit(solution)/shard_map/ppermute | solution.py:318
  162.7 6.1 %collective-permute-start.44 = (bf16[2,64,256]{2,1,0:T(8,128)(2,1)S(1)}, bf16[2,64,256]{2,1,0:T(8,128)(2,1)S(1)}, u32[]{:S(2)}, u32[]{:S(2)}) collective-permute-start(bf16[2,64,256]{2,1,0:T(8,128)(2,1)S(1)} %get-tuple-element.131), channel_id=1, source_target_pairs={{0,6},{1,7},{2,4},{3,5},{4,2},{5,3},{6,0},{7,1},{8,14},{9,15},{10,... | collective-permute-start | bytes 196616 | tf_op jit(solution)/shard_map/ppermute | solution.py:318
  163.3 7.1 %collective-permute-start.45 = (bf16[2,64,256]{2,1,0:T(8,128)(2,1)S(1)}, bf16[2,64,256]{2,1,0:T(8,128)(2,1)S(1)}, u32[]{:S(2)}, u32[]{:S(2)}) collective-permute-start(bf16[2,64,256]{2,1,0:T(8,128)(2,1)S(1)} %get-tuple-element.132), channel_id=1, source_target_pairs={{0,7},{1,6},{2,5},{3,4},{4,3},{5,2},{6,1},{7,0},{8,15},{9,14},{10,... | collective-permute-start | bytes 196616 | tf_op jit(solution)/shard_map/ppermute | solution.py:318
